TPU v7x, 256 devices: a 2x2x32 block of a 4x8x32 slice. The times are simulated.
256 devices in a mesh: groups: 4 (over y, x), tm: 32 (over z), space: 2 (over core).
Axes of the slice: x: 2, y: 2, z: 32, core: 2. Of those that a mesh axis runs over, the one named last changes fastest.
The devices are a block of a 4x8x32 slice.
Arguments:
- query_pre: bfloat16 [128, 8, 32, 2240], P(('groups', 'tm'), 'space'), parts along dimension 0, may hold values from -6 to 6
- key_pre: bfloat16 [128, 8, 32, 2240], P(('groups', 'tm'), 'space'), parts along dimension 0, may hold values from -6 to 6
- value_pre: bfloat16 [128, 8, 32, 2240], P(('groups', 'tm'), 'space'), parts along dimension 0, may hold values from -8 to 8
- grad_out: bfloat16 [128, 8, 32, 2240], P(('groups', 'tm'), 'space'), parts along dimension 0, may hold values from -96 to 96
- conv_taps: float32 [3, 3, 2240], replicated, may hold values from -4 to 4
Outputs:
- attended: bfloat16 [128, 8, 32, 2240], P(('groups', 'tm'), 'space'), parts along dimension 0
- query_grad: bfloat16 [128, 8, 32, 2240], P(('groups', 'tm'), 'space'), parts along dimension 0
- key_grad: bfloat16 [128, 8, 32, 2240], P(('groups', 'tm'), 'space'), parts along dimension 0
- value_grad: bfloat16 [128, 8, 32, 2240], P(('groups', 'tm'), 'space'), parts along dimension 0
- taps_grad: float32 [12, 3, 2240], P('groups'), parts along dimension 0
There are 4 independent parts, one for each index of `groups`. A program takes and returns all parts, laid end to end along the dimension named above; an argument that names none is the same for every part. Nothing has to cross between parts.
All inputs are finite; a program needn't handle non-finite values.
Results may differ from a plain program's by a relative error of at most 0.013.
Values may be sent and summed in bfloat16 or wider, within the bound.
No kernel may reach another device: no remote copies, remote signals or barrier semaphores. Data moves between devices by JAX's collectives and lax.ppermute only.
A program may use at most 128 MiB of HBM per device.

v0:
```python
import jax
import jax.numpy as jnp
from jax import lax
from jax.sharding import PartitionSpec as P

HEADS = 20
HEAD_DIM = 112


def extended(block, sides, width):
    for axis, dim in sides:
        count = lax.axis_size(axis)
        forward = [(i, i + 1) for i in range(count - 1)]
        backward = [(target, source) for source, target in forward]
        low = lax.ppermute(
            lax.slice_in_dim(block, block.shape[dim] - width, None, axis=dim), axis, forward
        )
        high = lax.ppermute(lax.slice_in_dim(block, 0, width, axis=dim), axis, backward)
        block = jnp.concatenate([low, block, high], axis=dim)
    return block


def split_up(x, dim, size):
    before, after = (x.shape[:dim], x.shape[dim + 1 :])
    return jnp.moveaxis(x.reshape(*before, size, -1, *after), dim, 0)


def summed_on_arrival(x, axis, dim):
    blocks = split_up(x, dim, lax.axis_size(axis))
    arrived = lax.all_to_all(blocks, axis, split_axis=0, concat_axis=0, tiled=True)
    return arrived.sum(axis=0)


def sent_together(arrays, axis, dim, along):
    columns = [a.reshape(*a.shape[:along], -1) for a in arrays]
    both = jnp.concatenate(columns, axis=along)
    result, at, outs = (summed_on_arrival(both, axis, dim), 0, [])
    for a, column in zip(arrays, columns):
        piece = result[..., at : at + column.shape[along]]
        outs.append(piece.reshape(*piece.shape[:along], *a.shape[along:]))
        at += column.shape[along]
    return tuple(outs)


def carried_in(part, axis, combine, identity):
    place = lax.axis_index(axis)
    gathered = jax.tree.map(lambda a: lax.all_gather(a, axis), part)
    state = jax.tree.map(lambda a, e: jnp.zeros_like(a) + jnp.asarray(e, a.dtype), part, identity)

    def one(turn, state):
        return combine(
            state, jax.tree.map(lambda a: lax.dynamic_index_in_dim(a, turn, 0, False), gathered)
        )

    return lax.fori_loop(0, place, one, state)


def carried_in_2(x, axis, join, neutral):
    count = lax.axis_size(axis)
    place = lax.axis_index(axis)
    ahead = count - 1 - place
    gathered = jax.tree.map(
        lambda a, kind: lax.all_gather(a.astype(kind), axis), x, (jnp.bfloat16, jnp.bfloat16)
    )
    state = jax.tree.map(lambda a, e: jnp.zeros_like(a) + jnp.asarray(e, a.dtype), x, neutral)

    def one(turn, state):
        source = count - 1 - turn
        return join(
            state,
            jax.tree.map(
                lambda a, own: lax.dynamic_index_in_dim(a, source, 0, False).astype(own.dtype),
                gathered,
                x,
            ),
        )

    return lax.fori_loop(0, ahead, one, state)


def gather_turned(arrays, axis, dims):
    turned = [jnp.moveaxis(a, dim, 0) for a, dim in zip(arrays, dims)]
    widths = [t[0].size for t in turned]
    both = jnp.concatenate([t.reshape(-1, w) for t, w in zip(turned, widths)], axis=1)
    result = lax.all_gather(both, axis, axis=0, tiled=True)
    blocks = jnp.split(result, [sum(widths[:k]) for k in range(1, len(widths))], axis=1)
    return tuple(
        (
            jnp.moveaxis(b.reshape(-1, *t.shape[1:]), 0, dim)
            for b, t, dim in zip(blocks, turned, dims)
        )
    )


def total_of_pieces(x, axis):
    return lax.all_gather(x, axis).sum(0)


def mix_rows(padded, conv_taps, row_count, col_count, flipped):
    summed = jnp.zeros(padded.shape[:1] + (row_count, col_count, padded.shape[3]), jnp.float32)
    for row_off in range(3):
        for col_off in range(3):
            if flipped:
                window = padded[
                    :, 2 - row_off : 2 - row_off + row_count, 2 - col_off : 2 - col_off + col_count
                ]
            else:
                window = padded[:, row_off : row_off + row_count, col_off : col_off + col_count]
            summed = summed + conv_taps[row_off, col_off] * window
    return summed


def add_pair(earlier, later):
    return (earlier[0] + later[0], earlier[1] + later[1])


def shards(query_pre, key_pre, value_pre, grad_out, conv_taps):
    frame_count, row_count, col_count, model_width = value_pre.shape
    head_count = HEADS
    head_size = HEAD_DIM
    token_count = frame_count * row_count * col_count
    split = (token_count, head_count, head_size)
    highest = lax.Precision.HIGHEST
    value_rows, grad_band = (
        extended(value_pre, (("space", 1),), 1),
        extended(grad_out, (("space", 1),), 1),
    )
    value_pad = jnp.pad(value_rows, ((0, 0), (0, 0), (1, 1), (0, 0)))
    local = mix_rows(value_pad, conv_taps, row_count, col_count, False)
    queries = jnp.maximum(query_pre, 0).reshape(split)
    keys = jnp.maximum(key_pre, 0).reshape(split)
    values = value_pre.reshape(split)
    partial_value = jnp.einsum("the,thd->hed", keys, values, preferred_element_type=jnp.float32)
    key_sum = jnp.sum(keys, axis=0, dtype=jnp.float32)
    half_state, half_sum = sent_together((partial_value, key_sum), "space", 0, 2)
    before = carried_in(
        (half_state, half_sum),
        "tm",
        add_pair,
        (jnp.zeros_like(half_state), jnp.zeros_like(half_sum)),
    )
    kv_state, key_total = (
        lax.all_gather(before[0] + half_state, "space", axis=0, tiled=True),
        lax.all_gather(before[1] + half_sum, "space", axis=0, tiled=True),
    )
    query_f32 = queries.astype(jnp.float32)
    numerator = jnp.einsum("the,hed->thd", query_f32, kv_state, precision=highest)
    denominator = jnp.einsum("the,he->th", query_f32, key_total, precision=highest) + 1.0
    output_f32 = numerator / denominator[..., None]
    attended = (output_f32.reshape(value_pre.shape) + local).astype(jnp.bfloat16)
    cotangent = grad_out.astype(jnp.float32).reshape(split)
    grad_num = cotangent / denominator[..., None]
    grad_den = -jnp.sum(cotangent * output_f32, axis=-1) / denominator
    grad_query = (
        jnp.einsum("thd,hed->the", grad_num, kv_state, precision=highest)
        + grad_den[..., None] * key_total[None]
    )
    grad_partial = jnp.einsum("the,thd->hed", query_f32, grad_num, precision=highest)
    grad_keysum = jnp.einsum("th,the->he", grad_den, query_f32, precision=highest)
    half_grad, half_keysum = (
        summed_on_arrival(grad_partial, "space", 0),
        summed_on_arrival(grad_keysum, "space", 0),
    )
    after = carried_in_2(
        (half_grad, half_keysum),
        "tm",
        add_pair,
        (jnp.zeros_like(half_grad), jnp.zeros_like(half_keysum)),
    )
    grad_state, grad_total = tuple(
        (
            part.astype(jnp.float32)
            for part in gather_turned(
                (
                    (after[0] + half_grad).astype(jnp.bfloat16),
                    (after[1] + half_keysum).astype(jnp.bfloat16),
                ),
                "space",
                (0, 0),
            )
        )
    )
    grad_key = (
        jnp.einsum("thd,hed->the", values.astype(jnp.float32), grad_state, precision=highest)
        + grad_total[None]
    )
    grad_mixed = jnp.einsum(
        "the,hed->thd", keys.astype(jnp.float32), grad_state, precision=highest
    ).reshape(value_pre.shape)
    query_grad = jnp.where(query_pre > 0, grad_query.reshape(value_pre.shape), 0.0).astype(
        jnp.bfloat16
    )
    key_grad = jnp.where(key_pre > 0, grad_key.reshape(value_pre.shape), 0.0).astype(jnp.bfloat16)
    grad_pad = jnp.pad(grad_band, ((0, 0), (0, 0), (1, 1), (0, 0)))
    value_grad = (grad_mixed + mix_rows(grad_pad, conv_taps, row_count, col_count, True)).astype(
        jnp.bfloat16
    )
    cotangent_full = grad_out.astype(jnp.float32)
    tap_rows = []
    for row_off in range(3):
        tap_cols = []
        for col_off in range(3):
            window = value_pad[:, row_off : row_off + row_count, col_off : col_off + col_count]
            tap_cols.append(jnp.sum(cotangent_full * window, axis=(0, 1, 2)))
        tap_rows.append(jnp.stack(tap_cols))
    taps_grad = total_of_pieces(jnp.stack(tap_rows), ("tm", "space"))
    return (attended, query_grad, key_grad, value_grad, taps_grad)


def solution(mesh):
    return jax.shard_map(
        shards,
        mesh=mesh,
        in_specs=(
            P(("groups", "tm"), "space", None, None),
            P(("groups", "tm"), "space", None, None),
            P(("groups", "tm"), "space", None, None),
            P(("groups", "tm"), "space", None, None),
            P(),
        ),
        out_specs=(
            P(("groups", "tm"), "space", None, None),
            P(("groups", "tm"), "space", None, None),
            P(("groups", "tm"), "space", None, None),
            P(("groups", "tm"), "space", None, None),
            P("groups", None, None),
        ),
        check_vma=False,
    )
```

profile of v0, /device:TPU:37, one launch (start us, length us, event | category | flops | bytes accessed | tf_op | source)
XLA Modules:
  0.0 602.0 jit_solution(15287799481472229838)
XLA Ops:
  18.8 24.0 %all-to-all-start = ((f32[2,10,112,113]{3,2,1,0:T(8,128)}), f32[2,10,112,113]{3,2,1,0:T(8,128)S(1)}, u32[]{:S(2)}, u32[]{:S(2)}) async-start(f32[2,10,112,113]{3,2,1,0:T(8,128)} %pad_maximum_fusion), calls=%async_computation | async-start | bytes 2293760 | tf_op jit(solution)/shard_map/all_to_all | solution.py:30
  45.8 2.4 collective-permute-start.1
  49.6 2.0 collective-permute-done
  54.1 2.0 reshape.112
  56.1 2.9 copy.65
  61.2 50.2 %all-gather.1 = f32[320,112,1]{1,2,0:T(1,128)S(1)} all-gather(f32[10,112,1]{1,2,0:T(1,128)S(1)} %copy.61), channel_id=3, replica_groups=mesh['groups'=4,'tm'=32,'space'=2] {'tm'}, dimensions={0}, use_global_device_ids=true | all-gather | bytes 147840 | tf_op jit(solution)/shard_map/all_gather | solution.py:47
  114.6 2.0 reshape.109
  117.9 141.0 %all-gather.12.cloned.1.call-done = f32[320,112,112]{2,1,0:T(8,128)} async-done(((f32[10,112,112]{2,1,0:T(8,128)}), f32[320,112,112]{2,1,0:T(8,128)}) %all-gather.12.cloned.1.call-update) | async-done | bytes 16056336 | tf_op jit(solution)/shard_map/all_gather | solution.py:47
  258.9 2.5 all-gather.5
  263.1 2.8 fusion.31
  265.9 5.5 all_to_all.15
  271.4 2.2 reduce_sum.138
  273.6 1.9 convert_element_type.154
  275.6 2.3 collective-permute-start.3
  282.8 114.3 %all-gather.16.cloned.1.call-done = f32[192,3,2240]{2,1,0:T(4,128)} async-done(((f32[3,3,2240]{2,1,0:T(4,128)}), f32[192,3,2240]{2,1,0:T(4,128)}) %all-gather.16.cloned.1.call-update) | async-done | bytes 5160976 | tf_op jit(solution)/shard_map/all_gather | solution.py:96
  397.1 4.7 reduce_sum.149
  403.5 2.8 all_gather.35
  406.3 2.7 multiply_reduce_fusion
  409.0 2.9 copy.64
  412.0 2.7 reshape.111
  417.0 3.5 all-to-all-start.2
  420.5 3.9 fusion.3
  424.5 2.5 copy.67
  427.0 2.4 reshape.113
  429.4 43.8 %all-gather.6 = bf16[32,10,112]{2,1,0:T(8,128)(2,1)S(1)} all-gather(bf16[1,10,112]{2,1,0:T(8,128)(2,1)S(1)} %convert_bitcast_fusion), channel_id=5, replica_groups=mesh['groups'=4,'tm'=32,'space'=2] {'tm'}, dimensions={0}, use_global_device_ids=true | all-gather | bytes 73920 | tf_op jit(solution)/shard_map/all_gather | solution.py:63
  473.3 3.1 fusion.13
  476.4 45.7 %all-gather.14.cloned.1.call-done = bf16[320,112,112]{2,1,0:T(8,128)(2,1)} async-done(((bf16[10,112,112]{2,1,0:T(8,128)(2,1)}), bf16[320,112,112]{2,1,0:T(8,128)(2,1)}) %all-gather.14.cloned.1.call-update) | async-done | bytes 8028176 | tf_op jit(solution)/shard_map/all_gather | solution.py:63
  522.1 34.3 %while.27 = (s32[]{:T(128)}, f32[10,112,112]{2,1,0:T(8,128)S(1)}, f32[10,112]{1,0:T(8,128)S(1)}, s32[]{:T(128)}, bf16[32,10,112,112]{3,2,1,0:T(8,128)(2,1)}, /*i...) while((s32[]{:T(128)}, f32[10,112,112]{2,1,0:T(8,128)S(1)}, ...), condition=%wide.region_8.9_spmd, body=%wide.region_7.8_spmd.sunk | while | flops 253126 | bytes 1265763 | solution.py:78
  557.0 20.6 %all-gather.7 = bf16[2,10,12656]{2,1,0:T(8,128)(2,1)S(1)} all-gather(bf16[1,10,12656]{2,1,0:T(8,128)(2,1)S(1)} %maximum_bitcast_fusion), channel_id=1, replica_groups=mesh['groups'=4,'tm'=32,'space'=2] {'space'}, dimensions={0}, use_global_device_ids=true | all-gather | bytes 759360 | tf_op jit(solution)/shard_map/all_gather | solution.py:85
  578.8 2.2 reshape.117
  589.8 2.9 select_convert_fusion
  592.8 2.7 fusion.20
  (222 shorter events, 79.6 us)
Async XLA Ops:
  10.5 3.2 copy-start
  13.7 3.2 copy-start.6
  18.8 25.8 %all-to-all-start = ((f32[2,10,112,113]{3,2,1,0:T(8,128)}), f32[2,10,112,113]{3,2,1,0:T(8,128)S(1)}, u32[]{:S(2)}, u32[]{:S(2)}) async-start(f32[2,10,112,113]{3,2,1,0:T(8,128)} %pad_maximum_fusion), calls=%async_computation | async-start | bytes 2293760 | tf_op jit(solution)/shard_map/all_to_all | solution.py:30
  42.8 216.0 %all-gather.12.cloned.1.call-start = ((), (), s32[]{:S(2)}) async-start(), calls=%async_computation.3 | async-start | bytes 18923520 | tf_op jit(solution)/shard_map/all_gather | solution.py:47
  45.7 6.2 %copy-start.1 = (bf16[1,4,32,2240]{3,2,1,0:T(8,128)(2,1)S(1)}, bf16[1,4,32,2240]{3,2,1,0:T(8,128)(2,1)}, u32[]{:S(2)}) copy-start(bf16[1,4,32,2240]{3,2,1,0:T(8,128)(2,1)} %param.12) | copy-start | bytes 1720324
  45.7 351.4 %all-gather.16.cloned.1.call-start = ((), (), s32[]{:S(2)}) async-start(), calls=%async_computation.5 | async-start | bytes 7188480 | tf_op jit(solution)/shard_map/all_gather | solution.py:96
  45.8 3.8 collective-permute-start.1
  48.3 3.3 collective-permute-start
  49.6 3.4 copy-start.13
  54.0 468.0 %all-gather.14.cloned.1.call-start = ((), (), s32[]{:S(2)}) async-start(), calls=%async_computation.4 | async-start | bytes 9461760 | tf_op jit(solution)/shard_map/all_gather | solution.py:63
  59.0 54.8 %copy-start.12 = (bf16[1,4,32,2240]{3,2,1,0:T(8,128)(2,1)S(1)}, bf16[1,4,32,2240]{3,2,1,0:T(8,128)(2,1)}, u32[]{:S(2)}) copy-start(bf16[1,4,32,2240]{3,2,1,0:T(8,128)(2,1)} %param.9) | copy-start | bytes 1720324
  273.6 5.6 copy-start.37
  275.6 4.5 collective-permute-start.3
  277.9 3.4 collective-permute-start.2
  402.3 4.0 copy-start.40
  417.0 12.4 %all-to-all-start.2 = ((f32[2,10,112]{2,1,0:T(8,128)}), f32[2,10,112]{2,1,0:T(8,128)S(1)}, u32[]{:S(2)}, u32[]{:S(2)}) async-start(f32[2,10,112]{2,1,0:T(8,128)} %reshape.115), calls=%async_computation.2 | async-start | bytes 32768 | tf_op jit(solution)/shard_map/all_to_all | solution.py:30
  424.4 48.9 %copy-start.14 = (bf16[1,1,32,2240]{3,2,1,0:T(8,128)(2,1)S(1)}, bf16[1,1,32,2240]{3,2,1,0:T(8,128)(2,1)}, u32[]{:S(2)}) copy-start(bf16[1,1,32,2240]{3,2,1,0:T(8,128)(2,1)} %copy-done.13) | copy-start | bytes 430084
  424.4 48.9 %copy-start.16 = (bf16[1,1,32,2240]{3,2,1,0:T(8,128)(2,1)S(1)}, bf16[1,1,32,2240]{3,2,1,0:T(8,128)(2,1)}, u32[]{:S(2)}) copy-start(bf16[1,1,32,2240]{3,2,1,0:T(8,128)(2,1)} %copy-done.15) | copy-start | bytes 430084
  424.4 48.9 %copy-start.19 = (f32[2240]{0:T(1024)S(1)}, f32[2240]{0:T(1024)}, u32[]{:S(2)}) copy-start(f32[2240]{0:T(1024)} %get-tuple-element.149) | copy-start | bytes 26884
  424.4 48.9 %copy-start.21 = (f32[2240]{0:T(1024)S(1)}, f32[2240]{0:T(1024)}, u32[]{:S(2)}) copy-start(f32[2240]{0:T(1024)} %get-tuple-element.150) | copy-start | bytes 26884
  424.4 48.9 %copy-start.23 = (f32[2240]{0:T(1024)S(1)}, f32[2240]{0:T(1024)}, u32[]{:S(2)}) copy-start(f32[2240]{0:T(1024)} %get-tuple-element.151) | copy-start | bytes 26884
  424.4 48.9 %copy-start.25 = (f32[2240]{0:T(1024)S(1)}, f32[2240]{0:T(1024)}, u32[]{:S(2)}) copy-start(f32[2240]{0:T(1024)} %get-tuple-element.152) | copy-start | bytes 26884
  424.4 48.9 %copy-start.27 = (f32[2240]{0:T(1024)S(1)}, f32[2240]{0:T(1024)}, u32[]{:S(2)}) copy-start(f32[2240]{0:T(1024)} %get-tuple-element.153) | copy-start | bytes 26884
  424.4 48.9 %copy-start.29 = (f32[2240]{0:T(1024)S(1)}, f32[2240]{0:T(1024)}, u32[]{:S(2)}) copy-start(f32[2240]{0:T(1024)} %get-tuple-element.154) | copy-start | bytes 26884
  424.4 48.9 %copy-start.31 = (f32[2240]{0:T(1024)S(1)}, f32[2240]{0:T(1024)}, u32[]{:S(2)}) copy-start(f32[2240]{0:T(1024)} %get-tuple-element.155) | copy-start | bytes 26884
  424.5 48.9 %copy-start.33 = (f32[2240]{0:T(1024)S(1)}, f32[2240]{0:T(1024)}, u32[]{:S(2)}) copy-start(f32[2240]{0:T(1024)} %get-tuple-element.156) | copy-start | bytes 26884
  522.1 34.4 %copy-start.5 = (f32[10,112,112]{2,1,0:T(8,128)S(1)}, f32[10,112,112]{2,1,0:T(8,128)}, u32[]{:S(2)}) copy-start(f32[10,112,112]{2,1,0:T(8,128)} %reduce_sum.138) | copy-start | bytes 1505284
  577.9 3.0 copy-start.7
  589.7 3.0 copy-start.22
  589.8 3.0 copy-start.24
  589.8 3.0 copy-start.26
  589.8 3.0 copy-start.28
  (18 other events, 44.6 us)
Sparse Core Ops, SparseCore 0:
  46.0 212.7 all-gather.11
  261.3 135.7 all-gather.15
  398.9 123.1 all-gather.13
where the time goes:
time: 606 us; the launch traced here: 602 us
  waiting for transfers between devices  306 us (50%)
  blocking collectives  125 us (21%)
  other arithmetic  63 us (10%)
  local copies, waits for them, and re-layouts  41.8 us (7%)
  starting transfers between devices  35.1 us (6%)
  matrix products  15.1 us (2%)
  between operations  14.5 us (2%)
    all_gather x1, waiting for transfers between devices, carried_in(): gathered = jax.tree.map(lambda a: lax.all_gather(a, axis), part)  141 us
    all_gather x1, waiting for transfers between devices, total_of_pieces(): return lax.all_gather(x, axis).sum(0)  114 us
    all_gather x1, blocking collectives, carried_in(): gathered = jax.tree.map(lambda a: lax.all_gather(a, axis), part)  50.2 us
    all_gather x1, waiting for transfers between devices, carried_in_2(): lax.all_gather(a.astype(kind), axis)  45.7 us
    all_gather x1, blocking collectives, carried_in_2(): lax.all_gather(a.astype(kind), axis)  43.8 us
    add x62, other arithmetic, add_pair(): return (earlier[0] + later[0], earlier[1] + later[1])  33.4 us
    all_to_all x2, starting transfers between devices, summed_on_arrival(): lax.all_to_all(blocks, axis, split_axis=0, concat_axis=0, tiled=True)  27.5 us
    all_gather x1, blocking collectives, gather_turned(): result = lax.all_gather(both, axis, axis=0, tiled=True)  20.6 us
  transfers between devices with their start and end apart: 9, of which 6 were waited for; matrix products, arithmetic and copies ran while one was open for 9% of the time, Pallas kernels for 0%

commit v1 on v0

v1 whole, which is shorter than its diff:
```python
import functools

import jax
import jax.numpy as jnp
from jax import lax
from jax.experimental import pallas as pl
from jax.experimental.pallas import tpu as pltpu
from jax.sharding import PartitionSpec as P

HEADS = 20
HD = 112
LN = 128
HC = 10
WC = HC * LN
NEAR = 4
ROWS = 1024
F32 = jnp.float32
BF = jnp.bfloat16
INTERPRET = False


def call(kernel, outs, *args):
    specs = [pl.BlockSpec(memory_space=pltpu.SMEM)]
    specs += [pl.BlockSpec(memory_space=pltpu.VMEM)] * (len(args) - 1)
    return pl.pallas_call(
        kernel,
        out_shape=[jax.ShapeDtypeStruct(s, d) for s, d in outs],
        in_specs=specs,
        out_specs=[pl.BlockSpec(memory_space=pltpu.VMEM)] * len(outs),
        interpret=INTERPRET,
    )(*args)


def lane(shape):
    return lax.broadcasted_iota(jnp.int32, shape, len(shape) - 1)


def halves(x):
    hi = x.astype(BF)
    return hi, (x - hi.astype(F32)).astype(BF)


def joined(hi, lo):
    return hi.astype(F32) + lo.astype(F32)


def mm(a, b, dims):
    return lax.dot_general(a, b, (dims, ((), ())), preferred_element_type=F32)


NN = ((1,), (0,))
NT = ((1,), (1,))
TN = ((0,), (0,))


def flag(cond):
    return jnp.where(cond, 1.0, 0.0).astype(F32)


def pack(ref, mats):
    last = mats[7]
    lanes = lane((HD, LN))
    for i in range(7):
        piece = pltpu.roll(last, HD - 16 * i, 1) if i < 7 else last
        ref[HD * i : HD * (i + 1), :] = jnp.where(lanes < HD, mats[i], piece)
    ref[HD * 7 : HD * 8, :] = mats[8]
    ref[HD * 8 : HD * 9, :] = mats[9]
    ref[HD * 9 : ROWS, :] = jnp.zeros((ROWS - HD * 9, LN), F32)


def unpack(ref):
    lanes = lane((HD, LN))
    mats, last = [], jnp.zeros((HD, LN), F32)
    for i in range(7):
        x = ref[HD * i : HD * (i + 1), :]
        mats.append(jnp.where(lanes < HD, x, 0.0))
        inside = (lanes >= 16 * i) & (lanes < 16 * i + 16)
        last = jnp.where(inside, pltpu.roll(x, 16 + 16 * i, 1), last)
    return mats + [last, ref[HD * 7 : HD * 8, :], ref[HD * 8 : HD * 9, :]]


def pad_rows(x):
    return jnp.concatenate([x, jnp.zeros((LN - HD, LN), x.dtype)], axis=0)


def heads_of(tile, width):
    out = []
    for h in range(HEADS):
        t, off = divmod(HD * h, LN)
        x = tile(t)
        if off:
            x = pltpu.roll(x, LN - off, 1)
        if off + HD > LN:
            y = pltpu.roll(tile(t + 1), LN - off, 1)
            x = jnp.where(lane(x.shape) < LN - off, x, y)
        out.append(jnp.where(lane(x.shape) < HD, x, 0.0))
    return out


def tiles_of(heads):
    out = []
    for t in range(-(-HEADS * HD // LN)):
        first, off = divmod(LN * t, HD)
        x = heads[first]
        if off:
            x = pltpu.roll(x, LN - off, 1)
        left = HD - off
        while left < LN and first + 1 < HEADS:
            first += 1
            y = pltpu.roll(heads[first], left, 1)
            x = jnp.where(lane(x.shape) < left, x, y)
            left += HD
        out.append(x)
    return out


def loader(ref, rows, width):
    cache = {}

    def tile(t):
        if t not in cache:
            n = min(LN, width - LN * t)
            x = ref[0:rows, LN * t : LN * t + n].astype(F32)
            if n < LN:
                x = jnp.concatenate([x, jnp.zeros((rows, LN - n), F32)], axis=1)
            cache[t] = x
        return cache[t]

    return tile


def spread_kernel(idx, q, k, v, g, taps, keep, send, taps_out):
    first = idx[0] == 0
    width = q.shape[1]
    rows = q.shape[0]
    for j, ref in enumerate((q, k, v, g)):
        heads = heads_of(loader(ref, rows, width), width)
        for i in range(HC):
            a, b = heads[i], heads[i + HC]
            if j < 2:
                a, b = jnp.maximum(a, 0.0), jnp.maximum(b, 0.0)
            keep[j, :, LN * i : LN * (i + 1)] = lax.select(first, a, b).astype(BF)
            send[j, :, LN * i : LN * (i + 1)] = lax.select(first, b, a).astype(BF)
    heads = heads_of(loader(taps, 9, width), width)
    for i in range(HC):
        taps_out[0:9, LN * i : LN * (i + 1)] = lax.select(first, heads[i], heads[i + HC])


def col(i):
    return slice(LN * i, LN * (i + 1))


def both(keep, recv, j, i):
    return jnp.concatenate([keep[j, :, col(i)], recv[j, :, col(i)]], axis=0)


def conv_kernel(idx, keep, recv, taps, local, gconv, taps_out):
    first = idx[0] == 0
    half = keep.shape[1]
    n = 2 * half
    cols = 32
    taps_out[...] = jnp.zeros_like(taps_out)
    pos = lax.broadcasted_iota(jnp.int32, (n, LN), 0) % cols
    zero_row = jnp.zeros((cols, LN), F32)

    def shifts(j, i):
        a, b = keep[j, :, col(i)].astype(F32), recv[j, :, col(i)].astype(F32)
        x = jnp.concatenate([lax.select(first, a, b), lax.select(first, b, a)], axis=0)
        before = jnp.where(pos == 0, 0.0, pltpu.roll(x, 1, 0))
        after = jnp.where(pos == cols - 1, 0.0, pltpu.roll(x, n - 1, 0))
        return before, x, after

    def up(u):
        return jnp.concatenate([zero_row, u[: n - cols]], axis=0)

    def down(u):
        return jnp.concatenate([u[cols:], zero_row], axis=0)

    def put(ref, x, i):
        ref[0:half, col(i)] = lax.select(first, x[:half], x[half:])
        ref[half:n, col(i)] = lax.select(first, x[half:], x[:half])

    for i in range(HC):
        w = taps[0:9, col(i)]
        vs, gs = shifts(2, i), shifts(3, i)
        u = [sum(w[3 * a + b : 3 * a + b + 1] * vs[b] for b in range(3)) for a in range(3)]
        put(local, up(u[0]) + u[1] + down(u[2]), i)
        u = [sum(w[3 * a + b : 3 * a + b + 1] * gs[2 - b] for b in range(3)) for a in range(3)]
        put(gconv, down(u[0]) + u[1] + up(u[2]), i)
        g = gs[1]
        for b in range(3):
            s = vs[b]
            for a, prod in enumerate((g[cols:] * s[: n - cols], g * s, g[: n - cols] * s[cols:])):
                r = 9 * i + 3 * a + b
                taps_out[r : r + 1, :] = jnp.sum(prod, axis=0, keepdims=True)


def rows_at(p, k, n):
    return pl.ds(pl.multiple_of((p ^ k) * n, n), n)


def partial_kernel(idx, keep, recv, own, ksum, a1, a2, a3, state):
    p = idx[1]
    ksum[...] = jnp.zeros_like(ksum)
    mats = []
    for i in range(HC):
        keys = both(keep, recv, 1, i)
        mats.append(mm(keys, both(keep, recv, 2, i), TN)[:HD])
        ksum[i : i + 1, :] = jnp.sum(keys.astype(F32), axis=0, keepdims=True)
    pack(state, mats)
    n = ROWS // NEAR
    own[...] = state[rows_at(p, 0, n), :]
    khi, klo = halves(ksum[...])
    for k, ref in enumerate((a1, a2, a3), 1):
        hi, lo = halves(state[rows_at(p, k, n), :])
        ref[0:n, :] = hi
        ref[n : 2 * n, :] = lo
        ref[2 * n : 2 * n + 16, :] = khi
        ref[2 * n + 16 : 2 * n + 32, :] = klo


def block_kernel(idx, own, ksum, a1, a2, a3, pay, kpre):
    p = idx[1]
    n = ROWS // NEAR
    total, ktot, kp = own[...], ksum[...], ksum[...]
    for k, ref in enumerate((a1, a2, a3), 1):
        total = total + joined(ref[0:n, :], ref[n : 2 * n, :])
        ks = joined(ref[2 * n : 2 * n + 16, :], ref[2 * n + 16 : 2 * n + 32, :])
        ktot = ktot + ks
        kp = kp + flag((p ^ k) <= p) * ks
    kpre[...] = kp
    khi, klo = halves(ktot)
    m = n // pay.shape[0]
    for b in range(pay.shape[0]):
        hi, lo = halves(total[m * b : m * (b + 1)])
        pay[b, 0:m, :] = hi
        pay[b, m : 2 * m, :] = lo
        pay[b, 2 * m : 2 * m + 16, :] = khi
        pay[b, 2 * m + 16 : 2 * m + 32, :] = klo


def reciprocal_of(q, kt, i):
    row = jnp.broadcast_to(kt[i : i + 1, :], (LN, LN))
    hi, lo = halves(row)
    den = mm(jnp.concatenate([q, q], axis=1), jnp.concatenate([hi, lo], axis=1), NT)
    return 1.0 / (den + 1.0)


def turn_kernel(idx, got, kpre, keep, recv, down, kt, own, c1, c2, c3, state):
    p, mine = idx[1], idx[2]
    nb = got.shape[0]
    n = ROWS // NEAR
    m = n // nb
    run, key_total = jnp.zeros((m, LN), F32), kpre[...]
    for b in range(nb):
        hi, lo = halves(run)
        down[b, 0:m, :] = hi
        down[b, m : 2 * m, :] = lo
        run = run + joined(got[b, 0:m, :], got[b, m : 2 * m, :])
        ks = joined(got[b, 2 * m : 2 * m + 16, :], got[b, 2 * m + 16 : 2 * m + 32, :])
        key_total = key_total + flag(b < mine) * ks
    kt[...] = key_total
    mats = []
    for i in range(HC):
        q = both(keep, recv, 0, i)
        scaled = both(keep, recv, 3, i).astype(F32) * reciprocal_of(q, key_total, i)
        hi, lo = halves(scaled)
        x = mm(q, jnp.concatenate([hi, lo], axis=1), TN)[:HD]
        mats.append(x[:, :LN] + x[:, LN:])
    pack(state, mats)
    own[...] = state[rows_at(p, 0, n), :]
    for k, ref in enumerate((c1, c2, c3), 1):
        ref[...] = state[rows_at(p, k, n), :].astype(BF)


def back_block_kernel(idx, own, c1, c2, c3, down, taps, pay):
    nb = pay.shape[0]
    m = ROWS // NEAR // nb
    total = own[...]
    for ref in (c1, c2, c3):
        total = total + ref[...].astype(F32)
    for b in range(nb):
        pay[b, 0 : 2 * m, :] = down[b]
        pay[b, 2 * m : 3 * m, :] = total[m * b : m * (b + 1)].astype(BF)
        hi, lo = halves(taps[16 * b : 16 * (b + 1), :])
        pay[b, 3 * m : 3 * m + 16, :] = hi
        pay[b, 3 * m + 16 : 3 * m + 32, :] = lo


def four_rows(x):
    hi = x.astype(BF).astype(F32)
    return jnp.concatenate([hi, x - hi, jnp.zeros((8, LN), F32)], axis=0).astype(BF)


def of_four(x):
    x = x.astype(F32)
    return x[0:4] + x[4:8]


def prefix_kernel(idx, got, own, a1, a2, a3, s_own, e1, e2, e3, taps_own, back, taps):
    p = idx[1]
    nb = got.shape[0]
    n = ROWS // NEAR
    m = n // nb
    base = jnp.concatenate([joined(got[b, 0:m, :], got[b, m : 2 * m, :]) for b in range(nb)], axis=0)
    run = jnp.zeros((m, LN), F32)
    t = jnp.zeros((16, LN), F32)
    for b in reversed(range(nb)):
        back[b] = run.astype(BF)
        run = run + got[b, 2 * m : 3 * m, :].astype(F32)
        t = t + joined(got[b, 3 * m : 3 * m + 16, :], got[b, 3 * m + 16 : 3 * m + 32, :])
    for j in range(NEAR):
        taps[j] = t[4 * j : 4 * (j + 1)]
    parts = [own[...]] + [joined(r[0:n, :], r[n : 2 * n, :]) for r in (a1, a2, a3)]
    for k, ref in enumerate((s_own, e1, e2, e3)):
        x = base
        for j in range(NEAR):
            x = x + flag((p ^ j) <= (p ^ k)) * parts[j]
        if k == 0:
            ref[...] = x
        else:
            hi, lo = halves(x)
            ref[0:n, :] = hi
            ref[n : 2 * n, :] = lo
            ref[2 * n : 2 * n + 16, :] = four_rows(taps[p ^ k])
    taps_own[...] = taps[p]


def attend_kernel(
    idx, e1, e2, e3, s_own, kt, keep, recv, local, taps_own, back, att, query, pay, gks_out, state, gks
):
    p = idx[1]
    nb = pay.shape[0]
    n = ROWS // NEAR
    m = n // nb
    half = keep.shape[1]
    state[rows_at(p, 0, n), :] = s_own[...]
    taps = taps_own[...]
    for k, ref in enumerate((e1, e2, e3), 1):
        state[rows_at(p, k, n), :] = joined(ref[0:n, :], ref[n : 2 * n, :])
        taps = taps + of_four(ref[2 * n : 2 * n + 16, :])
    mats = unpack(state)
    key_total = kt[...]
    gks[...] = jnp.zeros_like(gks)
    ones = jnp.ones((2 * LN, LN), BF)
    for i in range(HC):
        q, g = both(keep, recv, 0, i), both(keep, recv, 3, i)
        hi, lo = halves(pad_rows(mats[i]))
        recip = reciprocal_of(q, key_total, i)
        out = mm(jnp.concatenate([q, q], axis=1), jnp.concatenate([hi, lo], axis=0), NN) * recip
        x = (out + local[:, col(i)]).astype(BF)
        att[0, :, col(i)] = x[:half]
        att[1, :, col(i)] = x[half:]
        ghi, glo = halves(g.astype(F32) * out)
        gden = -mm(jnp.concatenate([ghi, glo], axis=1), ones, NN) * recip
        gs = mm(jnp.concatenate([g, g], axis=1), jnp.concatenate([hi, lo], axis=1), NT)
        qf = q.astype(F32)
        x = jnp.where(qf > 0.0, gs * recip + gden * key_total[i : i + 1, :], 0.0).astype(BF)
        query[0, :, col(i)] = x[:half]
        query[1, :, col(i)] = x[half:]
        gks[i : i + 1, :] = jnp.sum(gden * qf, axis=0, keepdims=True)
    gks_out[...] = gks[...]
    khi, klo = halves(gks[...])
    four = four_rows(taps)
    for b in range(nb):
        pay[b, 0:m, :] = back[b]
        pay[b, m : m + 16, :] = khi
        pay[b, m + 16 : m + 32, :] = klo
        pay[b, m + 32 : m + 48, :] = four


def suffix_kernel(idx, got, own, c1, c2, c3, gks, g_own, gt_own, taps_own, g1, g2, g3):
    p, mine = idx[1], idx[2]
    nb = got.shape[0]
    n = ROWS // NEAR
    m = n // nb
    base = jnp.concatenate([got[b, 0:m, :].astype(F32) for b in range(nb)], axis=0)
    later = jnp.zeros((16, LN), F32)
    for b in range(nb):
        ks = joined(got[b, m : m + 16, :], got[b, m + 16 : m + 32, :])
        later = later + flag(b > mine) * ks
    taps = jnp.concatenate([of_four(got[b, m + 32 : m + 48, :]) for b in range(nb)], axis=0)
    taps_own[...] = taps
    thi, tlo = halves(taps)
    parts = [own[...]] + [r[...].astype(F32) for r in (c1, c2, c3)]
    nt = taps.shape[0]
    for k, ref in enumerate((g_own, g1, g2, g3)):
        x = base
        for j in range(NEAR):
            x = x + flag((p ^ j) >= (p ^ k)) * parts[j]
        if k == 0:
            ref[...] = x
            gt_own[...] = later + gks[...]
        else:
            ref[0:n, :] = x.astype(BF)
            hi, lo = halves(later + flag(p >= (p ^ k)) * gks[...])
            ref[n : n + 16, :] = hi
            ref[n + 16 : n + 32, :] = lo
            ref[n + 32 : n + 32 + nt, :] = thi
            ref[n + 32 + nt : n + 32 + 2 * nt, :] = tlo


def finish_kernel(
    idx, g1, g2, g3, g_own, gt_own, taps_own, keep, recv, gconv, key, value, taps, state
):
    p = idx[1]
    n = ROWS // NEAR
    half = keep.shape[1]
    nt = taps_own.shape[0]
    state[rows_at(p, 0, n), :] = g_own[...]
    taps[p] = joined(*halves(taps_own[...]))
    total = gt_own[...]
    for k, ref in enumerate((g1, g2, g3), 1):
        state[rows_at(p, k, n), :] = ref[0:n, :].astype(F32)
        total = total + joined(ref[n : n + 16, :], ref[n + 16 : n + 32, :])
        taps[p ^ k] = joined(ref[n + 32 : n + 32 + nt, :], ref[n + 32 + nt : n + 32 + 2 * nt, :])
    mats = unpack(state)
    for i in range(HC):
        keys, v = both(keep, recv, 1, i), both(keep, recv, 2, i)
        hi, lo = halves(pad_rows(mats[i]))
        gk = mm(jnp.concatenate([v, v], axis=1), jnp.concatenate([hi, lo], axis=1), NT)
        x = jnp.where(keys.astype(F32) > 0.0, gk + total[i : i + 1, :], 0.0).astype(BF)
        key[0, :, col(i)] = x[:half]
        key[1, :, col(i)] = x[half:]
        gm = mm(jnp.concatenate([keys, keys], axis=1), jnp.concatenate([hi, lo], axis=0), NN)
        x = (gm + gconv[:, col(i)]).astype(BF)
        value[0, :, col(i)] = x[:half]
        value[1, :, col(i)] = x[half:]


def gather_heads(first, mine, other, ref):
    heads = [lax.select(first, mine(i), other(i)) for i in range(HC)]
    heads += [lax.select(first, other(i), mine(i)) for i in range(HC)]
    width = ref.shape[1]
    rows = ref.shape[0]
    for t, x in enumerate(tiles_of(heads)):
        n = min(LN, width - LN * t)
        ref[:, LN * t : LN * t + n] = x[:rows, :n].astype(ref.dtype)


def merge_kernel(idx, mine_a, mine_b, other_a, other_b, out_a, out_b):
    first = idx[0] == 0
    for mine, other, ref in ((mine_a, other_a, out_a), (mine_b, other_b, out_b)):
        gather_heads(
            first,
            lambda i: mine[0, :, col(i)].astype(F32),
            lambda i: other[:, col(i)].astype(F32),
            ref,
        )


def merge_taps_kernel(
    idx, mine_a, mine_b, other_a, other_b, mine_t, other_t, out_a, out_b, out_t, mine_s, other_s
):
    merge_kernel(idx, mine_a, mine_b, other_a, other_b, out_a, out_b)
    for src, dst in ((mine_t, mine_s), (other_t, other_s)):
        for u in range(-(-9 * HC // 4)):
            j, b = u % NEAR, u // NEAR
            dst[4 * u : 4 * (u + 1), :] = src[j, 4 * b : 4 * (b + 1), :]
    gather_heads(
        idx[0] == 0, lambda i: mine_s[9 * i : 9 * (i + 1), :], lambda i: other_s[9 * i : 9 * (i + 1), :], out_t
    )


def with_scratch(kernel, outs, scratch, *args):
    specs = [pl.BlockSpec(memory_space=pltpu.SMEM)]
    specs += [pl.BlockSpec(memory_space=pltpu.VMEM)] * (len(args) - 1)
    return pl.pallas_call(
        kernel,
        out_shape=[jax.ShapeDtypeStruct(s, d) for s, d in outs],
        in_specs=specs,
        out_specs=[pl.BlockSpec(memory_space=pltpu.VMEM)] * len(outs),
        scratch_shapes=[pltpu.VMEM(s, d) for s, d in scratch],
        interpret=INTERPRET,
    )(*args)


def shards(query_pre, key_pre, value_pre, grad_out, conv_taps):
    shape = value_pre.shape
    width = shape[-1]
    t = shape[0] * shape[1] * shape[2]
    frames = lax.axis_size("tm")
    nb = frames // NEAR
    place = lax.axis_index("tm")
    core = lax.axis_index("space")
    idx = jnp.stack([core, place % NEAR, place // NEAR]).astype(jnp.int32)
    swap = [(0, 1), (1, 0)]
    across = [[j + NEAR * b for b in range(nb)] for j in range(NEAR)]

    def over(x):
        return lax.ppermute(x, "space", swap)

    def near(arrays):
        return [
            lax.ppermute(a, "tm", [(i, i ^ k) for i in range(frames)])
            for k, a in enumerate(arrays, 1)
        ]

    def far(x):
        return lax.all_to_all(x, "tm", 0, 0, axis_index_groups=across, tiled=True)

    n = ROWS // NEAR
    m = n // nb
    flat = [x.reshape(t, width) for x in (query_pre, key_pre, value_pre, grad_out)]
    half = ((4, t, WC), BF)
    keep, send, taps = call(
        spread_kernel, [half, half, ((16, WC), F32)], idx, *flat, conv_taps.reshape(9, width)
    )
    recv = over(send)

    share = ((n, LN), F32)
    small = ((16, LN), F32)
    state = ((ROWS, LN), F32)
    own_b, ksum, *out = with_scratch(
        partial_kernel, [share, small] + [((2 * n + 32, LN), BF)] * 3, [state], idx, keep, recv
    )
    got_a = near(out)
    local, gconv, taps_part = call(
        conv_kernel, [((2 * t, WC), F32)] * 2 + [((LN, LN), F32)], idx, keep, recv, taps
    )
    pay, kpre = call(
        block_kernel, [((nb, 2 * m + 32, LN), BF), small], idx, own_b, ksum, *got_a
    )
    got = far(pay)
    down, kt, own_d, *out = with_scratch(
        turn_kernel,
        [((nb, 2 * m, LN), BF), small, share] + [((n, LN), BF)] * 3,
        [state],
        idx, got, kpre, keep, recv,
    )
    got_c = near(out)
    (pay,) = call(
        back_block_kernel, [((nb, 3 * m + 32, LN), BF)], idx, own_d, *got_c, down, taps_part
    )
    got = far(pay)
    s_own, e1, e2, e3, taps_own, back = with_scratch(
        prefix_kernel,
        [share] + [((2 * n + 16, LN), BF)] * 3 + [((4, LN), F32), ((nb, m, LN), BF)],
        [((NEAR, 4, LN), F32)],
        idx, got, own_b, *got_a,
    )
    got_e = near((e1, e2, e3))
    pair = ((2, t, WC), BF)
    att, query, pay, gks = with_scratch(
        attend_kernel,
        [pair, pair, ((nb, m + 48, LN), BF), small],
        [state, small],
        idx, *got_e, s_own, kt, keep, recv, local, taps_own, back,
    )
    got = far(pay)
    g_own, gt_own, taps_own, *out = call(
        suffix_kernel,
        [share, small, ((4 * nb, LN), F32)] + [((n + 32 + 8 * nb, LN), BF)] * 3,
        idx, got, own_d, *got_c, gks,
    )
    got_g = near(out)
    whole = ((t, width), BF)
    attended, query_grad = call(
        merge_kernel, [whole, whole], idx, att, query, over(att[1]), over(query[1])
    )
    key, value, taps_all = with_scratch(
        finish_kernel,
        [pair, pair, ((NEAR, 4 * nb, LN), F32)],
        [state],
        idx, *got_g, g_own, gt_own, taps_own, keep, recv, gconv,
    )
    key_grad, value_grad, taps_grad = with_scratch(
        merge_taps_kernel,
        [whole, whole, ((9, width), F32)],
        [((LN, LN), F32)] * 2,
        idx, key, value, over(key[1]), over(value[1]), taps_all, over(taps_all),
    )
    return (
        attended.reshape(shape),
        query_grad.reshape(shape),
        key_grad.reshape(shape),
        value_grad.reshape(shape),
        taps_grad.reshape(conv_taps.shape),
    )


def solution(mesh):
    frame = P(("groups", "tm"), "space", None, None)
    return jax.shard_map(
        shards,
        mesh=mesh,
        in_specs=(frame, frame, frame, frame, P()),
        out_specs=(frame, frame, frame, frame, P("groups", None, None)),
        check_vma=False,
    )
```

time: 606 us -> 250 us (0.41)
  waiting for transfers between devices: 306 us -> 46.7 us
  other arithmetic: 63 us -> 0.65 us
  blocking collectives: 125 us -> 69.9 us
  Pallas kernels: 0 us -> 41.7 us
  starting transfers between devices: 35.1 us -> 75.9 us
  local copies, waits for them, and re-layouts: 41.8 us -> 13.5 us
  matrix products: 15.1 us -> 0 us
  between operations: 14.5 us -> 0.78 us
    all_gather x3 -> x0, waiting for transfers between devices: 301 us -> none  [the longest x1 141 us: carried_in(): gathered = jax.tree.map(lambda a: lax.all_gather(a, axis), part)]
    all_gather x5 -> x0, blocking collectives: 120 us -> none  [the longest x1 50.2 us: carried_in(): gathered = jax.tree.map(lambda a: lax.all_gather(a, axis), part)]
    all_to_all x1 -> x2, blocking collectives: 5.49 us -> 69.9 us  [far(): return lax.all_to_all(x, 'tm', 0, 0, axis_index_groups=across, tiled=True)]
    ppermute x4 -> x18, starting transfers between devices: 7.38 us -> 64.3 us  [the longest x12 37 us: near(): lax.ppermute(a, 'tm', [(i, i ^ k) for i in range(frames)])]
    pallas_call x0 -> x12, Pallas kernels: none -> 41.7 us  [the longest x6 22.9 us: with_scratch(): pl.pallas_call(kernel, out_shape=[jax.ShapeDtypeStruct(s, d) for s, d in...]
    add x64 -> x0, other arithmetic: 34.5 us -> none  [the longest x62 33.4 us: add_pair(): return (earlier[0] + later[0], earlier[1] + later[1])]
    all_to_all x2 -> x1, waiting for transfers between devices: 1.82 us -> 27.1 us  [far(): return lax.all_to_all(x, 'tm', 0, 0, axis_index_groups=across, tiled=True)]
    reshape x15 -> x2, local copies, waits for them, and re-layouts: 25.7 us -> 3.19 us  [the longest x1 1.6 us: shards(): conv_taps.reshape(9, width)]
  transfers between devices with their start and end apart: 9 -> 19, of which waited for: 6 -> 7; matrix products, arithmetic and copies ran while one was open for 9% -> 1% of each run, Pallas kernels for 0% -> 5%
where the time goes in v1:
time: 250 us; the launch traced here: 249 us
  starting transfers between devices  75.9 us (30%)
  blocking collectives  69.9 us (28%)
  waiting for transfers between devices  46.7 us (19%)
  Pallas kernels  41.7 us (17%)
  local copies, waits for them, and re-layouts  13.5 us (5%)
    all_to_all x2, blocking collectives, far(): return lax.all_to_all(x, 'tm', 0, 0, axis_index_groups=across, tiled=True)  69.9 us
    ppermute x12, starting transfers between devices, near(): lax.ppermute(a, 'tm', [(i, i ^ k) for i in range(frames)])  37 us
    ppermute x6, starting transfers between devices, over(): return lax.ppermute(x, 'space', swap)  27.3 us
    all_to_all x1, waiting for transfers between devices, far(): return lax.all_to_all(x, 'tm', 0, 0, axis_index_groups=across, tiled=True)  27.1 us
    pallas_call x6, Pallas kernels, with_scratch(): pl.pallas_call(kernel, out_shape=[jax.ShapeDtypeStruct(s, d) for s, d in...  22.9 us
    pallas_call x6, Pallas kernels, call(): pl.pallas_call(kernel, out_shape=[jax.ShapeDtypeStruct(s, d) for s, d in...  18.8 us
    ppermute x12, waiting for transfers between devices, near(): lax.ppermute(a, 'tm', [(i, i ^ k) for i in range(frames)])  16.7 us
    all_to_all x1, starting transfers between devices, far(): return lax.all_to_all(x, 'tm', 0, 0, axis_index_groups=across, tiled=True)  11.6 us
  transfers between devices with their start and end apart: 19, of which 7 were waited for; matrix products, arithmetic and copies ran while one was open for 1% of the time, Pallas kernels for 5%

profile of v1, /device:TPU:37, one launch (start us, length us, event | category | flops | bytes accessed | tf_op | source)
XLA Modules:
  0.0 249.1 jit_solution(18238163554577142768)
XLA Ops:
  0.6 1.6 reshape.44.taps
  2.9 4.6 %shard_map.92 = (bf16[4,128,1280]{2,1,0:T(8,128)(2,1)}, bf16[4,128,1280]{2,1,0:T(8,128)(2,1)}, f32[16,1280]{1,0:T(8,128)}) custom-call(s32[3]{0:T(128)} %pad_add_fusion.idx, bf16[128,2240]{1,0:T(8,128)(2,1)} %bitcast.19, bf16[128,2240]{1,0:T(8,128)(2,1)} %bitcast.20, bf16[128,2240]{1,0:T(8,128)(2,1)} %bitcast.21, bf16[128,2240]{1,0:T(8,128)(2,1)} %bitcast.22, ...), custom_call_target="tpu_custom_call" | custom-call | tf_op jit(solution)/shard_map/pallas_call | solution.py:25
  7.5 20.4 %collective-permute-start = (bf16[4,128,1280]{2,1,0:T(8,128)(2,1)}, bf16[4,128,1280]{2,1,0:T(8,128)(2,1)S(1)}, u32[]{:S(2)}, u32[]{:S(2)}) collective-permute-start(bf16[4,128,1280]{2,1,0:T(8,128)(2,1)} %get-tuple-element.49), channel_id=1, source_target_pairs={{0,1},{1,0},{2,3},{3,2},{4,5},{5,4},{6,7},{7,6},{8,9},{9,8},{10,11... | collective-permute-start | bytes 3932168 | tf_op jit(solution)/shard_map/ppermute | solution.py:491
  27.9 2.9 %collective-permute-done.recv = bf16[4,128,1280]{2,1,0:T(8,128)(2,1)S(1)} collective-permute-done((bf16[4,128,1280]{2,1,0:T(8,128)(2,1)}, bf16[4,128,1280]{2,1,0:T(8,128)(2,1)S(1)}, u32[]{:S(2)}, u32[]{:S(2)}) %collective-permute-start) | collective-permute-done | bytes 1310752 | tf_op jit(solution)/shard_map/ppermute | solution.py:491
  31.8 3.0 %shard_map.93 = (f32[256,128]{1,0:T(8,128)}, f32[16,128]{1,0:T(8,128)}, bf16[544,128]{1,0:T(8,128)(2,1)}, bf16[544,128]{1,0:T(8,128)(2,1)}, bf16[544,128]{1,0:T(8,128)(2,1)}) custom-call(s32[3]{0:T(128)} %pad_add_fusion.idx, bf16[4,128,1280]{2,1,0:T(8,128)(2,1)} %get-tuple-element.48.keep, bf16[4,128,1280]{2,1,0:T(8,128)(2,1)} %copy-done), custom_call_target="tpu_custom_call" | custom-call | tf_op jit(solution)/shard_map/pallas_call | solution.py:468
  34.9 3.5 %collective-permute-start.3 = (bf16[544,128]{1,0:T(8,128)(2,1)}, bf16[544,128]{1,0:T(8,128)(2,1)S(1)}, u32[]{:S(2)}, u32[]{:S(2)}) collective-permute-start(bf16[544,128]{1,0:T(8,128)(2,1)} %get-tuple-element.54), channel_id=1, source_target_pairs={{0,6},{2,4},{4,2},{6,0},{8,14},{10,12},{12,10},{14,8},{16,22},{18,... | collective-permute-start | bytes 417800 | tf_op jit(solution)/shard_map/ppermute | solution.py:495
  38.4 2.7 %collective-permute-done.1.a1 = bf16[544,128]{1,0:T(8,128)(2,1)S(1)} collective-permute-done((bf16[544,128]{1,0:T(8,128)(2,1)}, bf16[544,128]{1,0:T(8,128)(2,1)S(1)}, u32[]{:S(2)}, u32[]{:S(2)}) %collective-permute-start.1) | collective-permute-done | bytes 139296 | tf_op jit(solution)/shard_map/ppermute | solution.py:495
  41.1 5.7 %collective-permute-done.2.a2 = bf16[544,128]{1,0:T(8,128)(2,1)S(1)} collective-permute-done((bf16[544,128]{1,0:T(8,128)(2,1)}, bf16[544,128]{1,0:T(8,128)(2,1)S(1)}, u32[]{:S(2)}, u32[]{:S(2)}) %collective-permute-start.2) | collective-permute-done | bytes 139296 | tf_op jit(solution)/shard_map/ppermute | solution.py:495
  47.5 1.9 shard_map.94
  49.4 36.2 %all_to_all.15.got = bf16[8,96,128]{2,1,0:T(8,128)(2,1)} all-to-all(bf16[8,96,128]{2,1,0:T(8,128)(2,1)} %get-tuple-element.55), channel_id=1, replica_groups={{0,8,16,24,32,40,48,56},{2,10,18,26,34,42,50,58},{4,12,20,28,36,44,52,6..., dimensions={0} | all-to-all | bytes 393216 | tf_op jit(solution)/shard_map/all_to_all | solution.py:500
  85.6 5.0 %shard_map.95 = (bf16[8,64,128]{2,1,0:T(8,128)(2,1)}, f32[16,128]{1,0:T(8,128)}, f32[256,128]{1,0:T(8,128)}, bf16[256,128]{1,0:T(8,128)(2,1)}, bf16[256,128]{1,0:T(8,128)(2,1)}, /*index=5*/bf16[256,128]{1,0:T(8,128)(2,1)}) custom-call(s32[3]{0:T(128)} %pad_add_fusion.idx, bf16[8,96,128]{2,1,0:T(8,128)(2,1)} %all_to_all.15.got, ...), custom_call_target="tpu_custom_call" | custom-call | tf_op jit(solution)/shard_map/pallas_call | solution.py:468
  90.7 12.2 %collective-permute-start.4 = (bf16[256,128]{1,0:T(8,128)(2,1)}, bf16[256,128]{1,0:T(8,128)(2,1)S(1)}, u32[]{:S(2)}, u32[]{:S(2)}) collective-permute-start(bf16[256,128]{1,0:T(8,128)(2,1)} %get-tuple-element.58), channel_id=1, source_target_pairs={{0,2},{2,0},{4,6},{6,4},{8,10},{10,8},{12,14},{14,12},{16,18},{18,... | collective-permute-start | bytes 196616 | tf_op jit(solution)/shard_map/ppermute | solution.py:495
  105.3 5.8 %shard_map.96 = (f32[256,1280]{1,0:T(8,128)}, f32[256,1280]{1,0:T(8,128)}, f32[128,128]{1,0:T(8,128)}) custom-call(s32[3]{0:T(128)} %pad_add_fusion.idx, bf16[4,128,1280]{2,1,0:T(8,128)(2,1)} %get-tuple-element.48.keep, bf16[4,128,1280]{2,1,0:T(8,128)(2,1)} %copy-done, f32[16,1280]{1,0:T(8,128)} %get-tuple-element.62.taps), custom_call_target="tpu_custom_call" | custom-call | tf_op jit(solution)/shard_map/pallas_call | solution.py:25
  111.7 1.8 shard_map.97
  113.6 33.7 %all_to_all.16.got = bf16[8,128,128]{2,1,0:T(8,128)(2,1)} all-to-all(bf16[8,128,128]{2,1,0:T(8,128)(2,1)} %shard_map.97), channel_id=1, replica_groups={{0,8,16,24,32,40,48,56},{2,10,18,26,34,42,50,58},{4,12,20,28,36,44,52,6..., dimensions={0} | all-to-all | bytes 524288 | tf_op jit(solution)/shard_map/all_to_all | solution.py:500
  147.2 2.1 shard_map.98
  149.3 2.5 collective-permute-start.7
  151.8 6.1 %collective-permute-start.8 = (bf16[528,128]{1,0:T(8,128)(2,1)}, bf16[528,128]{1,0:T(8,128)(2,1)S(1)}, u32[]{:S(2)}, u32[]{:S(2)}) collective-permute-start(bf16[528,128]{1,0:T(8,128)(2,1)} %get-tuple-element.65), channel_id=1, source_target_pairs={{0,4},{2,6},{4,0},{6,2},{8,12},{10,14},{12,8},{14,10},{16,20},{18,... | collective-permute-start | bytes 405512 | tf_op jit(solution)/shard_map/ppermute | solution.py:495
  160.6 4.4 %collective-permute-done.9.e3 = bf16[528,128]{1,0:T(8,128)(2,1)S(1)} collective-permute-done((bf16[528,128]{1,0:T(8,128)(2,1)}, bf16[528,128]{1,0:T(8,128)(2,1)S(1)}, u32[]{:S(2)}, u32[]{:S(2)}) %collective-permute-start.9) | collective-permute-done | bytes 135200 | tf_op jit(solution)/shard_map/ppermute | solution.py:495
  165.7 5.5 %shard_map.99 = (bf16[2,128,1280]{2,1,0:T(8,128)(2,1)}, bf16[2,128,1280]{2,1,0:T(8,128)(2,1)}, bf16[8,80,128]{2,1,0:T(8,128)(2,1)}, f32[16,128]{1,0:T(8,128)}) custom-call(s32[3]{0:T(128)} %pad_add_fusion.idx, bf16[528,128]{1,0:T(8,128)(2,1)} %copy-done.13, bf16[528,128]{1,0:T(8,128)(2,1)} %copy-done.14, bf16[528,128]{1,0:T(8,128)(2,1)} %copy-done.15, ...), custom_call_target="tpu_custom_call" | custom-call | tf_op jit(solution)/shard_map/pallas_call | solution.py:468
  171.2 11.6 %all-to-all-start.2 = ((bf16[8,80,128]{2,1,0:T(8,128)(2,1)}), bf16[8,80,128]{2,1,0:T(8,128)(2,1)S(1)}, u32[]{:S(2)}, u32[]{:S(2)}) async-start(bf16[8,80,128]{2,1,0:T(8,128)(2,1)} %get-tuple-element.76), calls=%async_computation.2 | async-start | bytes 327680 | tf_op jit(solution)/shard_map/all_to_all | solution.py:500
  183.8 27.1 %all-to-all-done.2.got = bf16[8,80,128]{2,1,0:T(8,128)(2,1)S(1)} async-done(((bf16[8,80,128]{2,1,0:T(8,128)(2,1)}), bf16[8,80,128]{2,1,0:T(8,128)(2,1)S(1)}, u32[]{:S(2)}, u32[]{:S(2)}) %all-to-all-start.2) | async-done | bytes 163872 | tf_op jit(solution)/shard_map/all_to_all | solution.py:500
  211.5 1.9 shard_map.101
  213.4 7.0 %collective-permute-start.12 = (bf16[352,128]{1,0:T(8,128)(2,1)}, bf16[352,128]{1,0:T(8,128)(2,1)S(1)}, u32[]{:S(2)}, u32[]{:S(2)}) collective-permute-start(bf16[352,128]{1,0:T(8,128)(2,1)} %get-tuple-element.78), channel_id=1, source_target_pairs={{0,2},{2,0},{4,6},{6,4},{8,10},{10,8},{12,14},{14,12},{16,18},{18,... | collective-permute-start | bytes 270344 | tf_op jit(solution)/shard_map/ppermute | solution.py:495
  220.9 1.7 collective-permute-start.14
  222.6 2.3 collective-permute-start.11
  225.0 2.3 collective-permute-done.13.g2
  228.0 4.4 %shard_map.102 = (bf16[2,128,1280]{2,1,0:T(8,128)(2,1)}, bf16[2,128,1280]{2,1,0:T(8,128)(2,1)}, f32[4,32,128]{2,1,0:T(8,128)}) custom-call(s32[3]{0:T(128)} %pad_add_fusion.idx, bf16[352,128]{1,0:T(8,128)(2,1)} %copy-done.16, bf16[352,128]{1,0:T(8,128)(2,1)} %copy-done.17, bf16[352,128]{1,0:T(8,128)(2,1)} %copy-done.18, f32[256,128]{1,0:T(8,128)} %get-tuple-element.81.g_own, ...), custom_call_target="tpu_custom_call" | custom-call | tf_op jit(solution)/shard_map/pallas_call | solution.py:468
  234.4 3.9 %collective-permute-start.16 = (bf16[128,1280]{1,0:T(8,128)(2,1)S(1)}, bf16[128,1280]{1,0:T(8,128)(2,1)S(1)}, u32[]{:S(2)}, u32[]{:S(2)}) collective-permute-start(bf16[128,1280]{1,0:T(8,128)(2,1)S(1)} %slice_bitcast_fusion), channel_id=1, source_target_pairs={{0,1},{1,0},{2,3},{3,2},{4,5},{5,4},{6,7},{7,6},{8,9},{9,8},{10,11... | collective-permute-start | bytes 983048 | tf_op jit(solution)/shard_map/ppermute | solution.py:491
  240.2 2.9 %shard_map.100 = (bf16[128,2240]{1,0:T(8,128)(2,1)}, bf16[128,2240]{1,0:T(8,128)(2,1)}) custom-call(s32[3]{0:T(128)} %pad_add_fusion.idx, bf16[2,128,1280]{2,1,0:T(8,128)(2,1)} %get-tuple-element.72.mine_a, bf16[2,128,1280]{2,1,0:T(8,128)(2,1)} %get-tuple-element.73.mine_b, bf16[128,1280]{1,0:T(8,128)(2,1)} %copy-done.9, bf16[128,1280]{1,0:T(8,128)(2,1)} %copy-done.8), custom_call_target="tpu_custom_call" | custom-call | tf_op jit(solution)/shard_map/pallas_call | solution.py:25
  244.6 2.9 %shard_map.103 = (bf16[128,2240]{1,0:T(8,128)(2,1)}, bf16[128,2240]{1,0:T(8,128)(2,1)}, f32[9,2240]{1,0:T(8,128)}) custom-call(s32[3]{0:T(128)} %pad_add_fusion.idx, bf16[2,128,1280]{2,1,0:T(8,128)(2,1)} %get-tuple-element.85.mine_a, bf16[2,128,1280]{2,1,0:T(8,128)(2,1)} %get-tuple-element.86.mine_b, bf16[128,1280]{1,0:T(8,128)(2,1)} %copy-done.7, ...), custom_call_target="tpu_custom_call" | custom-call | tf_op jit(solution)/shard_map/pallas_call | solution.py:468
  247.5 1.6 reshape.49
  (69 shorter events, 17.3 us)
Async XLA Ops:
  7.5 23.3 %collective-permute-start = (bf16[4,128,1280]{2,1,0:T(8,128)(2,1)}, bf16[4,128,1280]{2,1,0:T(8,128)(2,1)S(1)}, u32[]{:S(2)}, u32[]{:S(2)}) collective-permute-start(bf16[4,128,1280]{2,1,0:T(8,128)(2,1)} %get-tuple-element.49), channel_id=1, source_target_pairs={{0,1},{1,0},{2,3},{3,2},{4,5},{5,4},{6,7},{7,6},{8,9},{9,8},{10,11... | collective-permute-start | bytes 3932168 | tf_op jit(solution)/shard_map/ppermute | solution.py:491
  30.8 1.1 copy-start
  34.8 6.3 %collective-permute-start.1 = (bf16[544,128]{1,0:T(8,128)(2,1)}, bf16[544,128]{1,0:T(8,128)(2,1)S(1)}, u32[]{:S(2)}, u32[]{:S(2)}) collective-permute-start(bf16[544,128]{1,0:T(8,128)(2,1)} %get-tuple-element.52), channel_id=1, source_target_pairs={{0,2},{2,0},{4,6},{6,4},{8,10},{10,8},{12,14},{14,12},{16,18},{18,... | collective-permute-start | bytes 417800 | tf_op jit(solution)/shard_map/ppermute | solution.py:495
  34.8 12.0 %collective-permute-start.2 = (bf16[544,128]{1,0:T(8,128)(2,1)}, bf16[544,128]{1,0:T(8,128)(2,1)S(1)}, u32[]{:S(2)}, u32[]{:S(2)}) collective-permute-start(bf16[544,128]{1,0:T(8,128)(2,1)} %get-tuple-element.53), channel_id=1, source_target_pairs={{0,4},{2,6},{4,0},{6,2},{8,12},{10,14},{12,8},{14,10},{16,20},{18,... | collective-permute-start | bytes 417800 | tf_op jit(solution)/shard_map/ppermute | solution.py:495
  34.9 12.0 %collective-permute-start.3 = (bf16[544,128]{1,0:T(8,128)(2,1)}, bf16[544,128]{1,0:T(8,128)(2,1)S(1)}, u32[]{:S(2)}, u32[]{:S(2)}) collective-permute-start(bf16[544,128]{1,0:T(8,128)(2,1)} %get-tuple-element.54), channel_id=1, source_target_pairs={{0,6},{2,4},{4,2},{6,0},{8,14},{10,12},{12,10},{14,8},{16,22},{18,... | collective-permute-start | bytes 417800 | tf_op jit(solution)/shard_map/ppermute | solution.py:495
  41.1 5.7 %copy-start.3 = (bf16[544,128]{1,0:T(8,128)(2,1)}, bf16[544,128]{1,0:T(8,128)(2,1)S(1)}, u32[]{:S(2)}) copy-start(bf16[544,128]{1,0:T(8,128)(2,1)S(1)} %collective-permute-done.1.a1) | copy-start | bytes 417796
  46.8 0.7 copy-start.5
  90.7 20.4 %collective-permute-start.4 = (bf16[256,128]{1,0:T(8,128)(2,1)}, bf16[256,128]{1,0:T(8,128)(2,1)S(1)}, u32[]{:S(2)}, u32[]{:S(2)}) collective-permute-start(bf16[256,128]{1,0:T(8,128)(2,1)} %get-tuple-element.58), channel_id=1, source_target_pairs={{0,2},{2,0},{4,6},{6,4},{8,10},{10,8},{12,14},{14,12},{16,18},{18,... | collective-permute-start | bytes 196616 | tf_op jit(solution)/shard_map/ppermute | solution.py:495
  102.9 8.2 %collective-permute-start.5 = (bf16[256,128]{1,0:T(8,128)(2,1)}, bf16[256,128]{1,0:T(8,128)(2,1)S(1)}, u32[]{:S(2)}, u32[]{:S(2)}) collective-permute-start(bf16[256,128]{1,0:T(8,128)(2,1)} %get-tuple-element.59), channel_id=1, source_target_pairs={{0,4},{2,6},{4,0},{6,2},{8,12},{10,14},{12,8},{14,10},{16,20},{18,... | collective-permute-start | bytes 196616 | tf_op jit(solution)/shard_map/ppermute | solution.py:495
  104.2 6.9 %collective-permute-start.6 = (bf16[256,128]{1,0:T(8,128)(2,1)}, bf16[256,128]{1,0:T(8,128)(2,1)S(1)}, u32[]{:S(2)}, u32[]{:S(2)}) collective-permute-start(bf16[256,128]{1,0:T(8,128)(2,1)} %get-tuple-element.60), channel_id=1, source_target_pairs={{0,6},{2,4},{4,2},{6,0},{8,14},{10,12},{12,10},{14,8},{16,22},{18,... | collective-permute-start | bytes 196616 | tf_op jit(solution)/shard_map/ppermute | solution.py:495
  149.3 9.7 %collective-permute-start.7 = (bf16[528,128]{1,0:T(8,128)(2,1)}, bf16[528,128]{1,0:T(8,128)(2,1)S(1)}, u32[]{:S(2)}, u32[]{:S(2)}) collective-permute-start(bf16[528,128]{1,0:T(8,128)(2,1)} %get-tuple-element.64), channel_id=1, source_target_pairs={{0,2},{2,0},{4,6},{6,4},{8,10},{10,8},{12,14},{14,12},{16,18},{18,... | collective-permute-start | bytes 405512 | tf_op jit(solution)/shard_map/ppermute | solution.py:495
  151.8 8.8 %collective-permute-start.8 = (bf16[528,128]{1,0:T(8,128)(2,1)}, bf16[528,128]{1,0:T(8,128)(2,1)S(1)}, u32[]{:S(2)}, u32[]{:S(2)}) collective-permute-start(bf16[528,128]{1,0:T(8,128)(2,1)} %get-tuple-element.65), channel_id=1, source_target_pairs={{0,4},{2,6},{4,0},{6,2},{8,12},{10,14},{12,8},{14,10},{16,20},{18,... | collective-permute-start | bytes 405512 | tf_op jit(solution)/shard_map/ppermute | solution.py:495
  157.9 7.1 %collective-permute-start.9 = (bf16[528,128]{1,0:T(8,128)(2,1)}, bf16[528,128]{1,0:T(8,128)(2,1)S(1)}, u32[]{:S(2)}, u32[]{:S(2)}) collective-permute-start(bf16[528,128]{1,0:T(8,128)(2,1)} %get-tuple-element.66), channel_id=1, source_target_pairs={{0,6},{2,4},{4,2},{6,0},{8,14},{10,12},{12,10},{14,8},{16,22},{18,... | collective-permute-start | bytes 405512 | tf_op jit(solution)/shard_map/ppermute | solution.py:495
  159.0 6.0 %copy-start.13 = (bf16[528,128]{1,0:T(8,128)(2,1)}, bf16[528,128]{1,0:T(8,128)(2,1)S(1)}, u32[]{:S(2)}) copy-start(bf16[528,128]{1,0:T(8,128)(2,1)S(1)} %collective-permute-done.7.e1) | copy-start | bytes 405508
  160.6 4.4 %copy-start.14 = (bf16[528,128]{1,0:T(8,128)(2,1)}, bf16[528,128]{1,0:T(8,128)(2,1)S(1)}, u32[]{:S(2)}) copy-start(bf16[528,128]{1,0:T(8,128)(2,1)S(1)} %collective-permute-done.8.e2) | copy-start | bytes 405508
  171.2 51.3 %copy-start.1 = (bf16[2,128,1280]{2,1,0:T(8,128)(2,1)S(1)}, bf16[2,128,1280]{2,1,0:T(8,128)(2,1)}, u32[]{:S(2)}) copy-start(bf16[2,128,1280]{2,1,0:T(8,128)(2,1)} %get-tuple-element.73.mine_b) | copy-start | bytes 1966084
  171.2 39.6 %all-to-all-start.2 = ((bf16[8,80,128]{2,1,0:T(8,128)(2,1)}), bf16[8,80,128]{2,1,0:T(8,128)(2,1)S(1)}, u32[]{:S(2)}, u32[]{:S(2)}) async-start(bf16[8,80,128]{2,1,0:T(8,128)(2,1)} %get-tuple-element.76), calls=%async_computation.2 | async-start | bytes 327680 | tf_op jit(solution)/shard_map/all_to_all | solution.py:500
  210.8 0.7 copy-start.2
  213.4 11.7 %collective-permute-start.12 = (bf16[352,128]{1,0:T(8,128)(2,1)}, bf16[352,128]{1,0:T(8,128)(2,1)S(1)}, u32[]{:S(2)}, u32[]{:S(2)}) collective-permute-start(bf16[352,128]{1,0:T(8,128)(2,1)} %get-tuple-element.78), channel_id=1, source_target_pairs={{0,2},{2,0},{4,6},{6,4},{8,10},{10,8},{12,14},{14,12},{16,18},{18,... | collective-permute-start | bytes 270344 | tf_op jit(solution)/shard_map/ppermute | solution.py:495
  220.3 7.0 %collective-permute-start.13 = (bf16[352,128]{1,0:T(8,128)(2,1)}, bf16[352,128]{1,0:T(8,128)(2,1)S(1)}, u32[]{:S(2)}, u32[]{:S(2)}) collective-permute-start(bf16[352,128]{1,0:T(8,128)(2,1)} %get-tuple-element.79), channel_id=1, source_target_pairs={{0,4},{2,6},{4,0},{6,2},{8,12},{10,14},{12,8},{14,10},{16,20},{18,... | collective-permute-start | bytes 270344 | tf_op jit(solution)/shard_map/ppermute | solution.py:495
  220.9 6.4 %collective-permute-start.14 = (bf16[352,128]{1,0:T(8,128)(2,1)}, bf16[352,128]{1,0:T(8,128)(2,1)S(1)}, u32[]{:S(2)}, u32[]{:S(2)}) collective-permute-start(bf16[352,128]{1,0:T(8,128)(2,1)} %get-tuple-element.80), channel_id=1, source_target_pairs={{0,6},{2,4},{4,2},{6,0},{8,14},{10,12},{12,10},{14,8},{16,22},{18,... | collective-permute-start | bytes 270344 | tf_op jit(solution)/shard_map/ppermute | solution.py:495
  222.6 16.2 %collective-permute-start.11 = (bf16[128,1280]{1,0:T(8,128)(2,1)S(1)}, bf16[128,1280]{1,0:T(8,128)(2,1)S(1)}, u32[]{:S(2)}, u32[]{:S(2)}) collective-permute-start(bf16[128,1280]{1,0:T(8,128)(2,1)S(1)} %slice_bitcast_fusion.2), channel_id=1, source_target_pairs={{0,1},{1,0},{2,3},{3,2},{4,5},{5,4},{6,7},{7,6},{8,9},{9,8},{10,11... | collective-permute-start | bytes 983048 | tf_op jit(solution)/shard_map/ppermute | solution.py:491
  224.9 13.9 %collective-permute-start.10 = (bf16[128,1280]{1,0:T(8,128)(2,1)S(1)}, bf16[128,1280]{1,0:T(8,128)(2,1)S(1)}, u32[]{:S(2)}, u32[]{:S(2)}) collective-permute-start(bf16[128,1280]{1,0:T(8,128)(2,1)S(1)} %slice_bitcast_fusion.3), channel_id=1, source_target_pairs={{0,1},{1,0},{2,3},{3,2},{4,5},{5,4},{6,7},{7,6},{8,9},{9,8},{10,11... | collective-permute-start | bytes 983048 | tf_op jit(solution)/shard_map/ppermute | solution.py:491
  225.0 2.3 copy-start.16
  232.3 6.1 %copy-start.19 = (f32[4,32,128]{2,1,0:T(8,128)S(1)}, f32[4,32,128]{2,1,0:T(8,128)}, u32[]{:S(2)}) copy-start(f32[4,32,128]{2,1,0:T(8,128)} %get-tuple-element.87.mine_t) | copy-start | bytes 196612
  234.4 8.7 %collective-permute-start.16 = (bf16[128,1280]{1,0:T(8,128)(2,1)S(1)}, bf16[128,1280]{1,0:T(8,128)(2,1)S(1)}, u32[]{:S(2)}, u32[]{:S(2)}) collective-permute-start(bf16[128,1280]{1,0:T(8,128)(2,1)S(1)} %slice_bitcast_fusion), channel_id=1, source_target_pairs={{0,1},{1,0},{2,3},{3,2},{4,5},{5,4},{6,7},{7,6},{8,9},{9,8},{10,11... | collective-permute-start | bytes 983048 | tf_op jit(solution)/shard_map/ppermute | solution.py:491
  238.3 4.9 %collective-permute-start.15 = (bf16[128,1280]{1,0:T(8,128)(2,1)S(1)}, bf16[128,1280]{1,0:T(8,128)(2,1)S(1)}, u32[]{:S(2)}, u32[]{:S(2)}) collective-permute-start(bf16[128,1280]{1,0:T(8,128)(2,1)S(1)} %slice_bitcast_fusion.1), channel_id=1, source_target_pairs={{0,1},{1,0},{2,3},{3,2},{4,5},{5,4},{6,7},{7,6},{8,9},{9,8},{10,11... | collective-permute-start | bytes 983048 | tf_op jit(solution)/shard_map/ppermute | solution.py:491
  238.4 4.7 %collective-permute-start.17 = (f32[4,32,128]{2,1,0:T(8,128)S(1)}, f32[4,32,128]{2,1,0:T(8,128)S(1)}, u32[]{:S(2)}, u32[]{:S(2)}) collective-permute-start(f32[4,32,128]{2,1,0:T(8,128)S(1)} %copy-done.19), channel_id=1, source_target_pairs={{0,1},{1,0},{2,3},{3,2},{4,5},{5,4},{6,7},{7,6},{8,9},{9,8},{10,11... | collective-permute-start | bytes 196616 | tf_op jit(solution)/shard_map/ppermute | solution.py:491
  238.8 0.7 copy-start.8
  239.5 0.7 copy-start.9
  243.1 0.8 copy-start.6
  243.8 0.7 copy-start.7
  (8 other events, 5.1 us)

commit v2 on v1

v2 whole, which is shorter than its diff:
```python
import functools

import jax
import jax.numpy as jnp
from jax import lax
from jax.experimental import pallas as pl
from jax.experimental.pallas import tpu as pltpu
from jax.sharding import PartitionSpec as P

HEADS = 20
HD = 112
LN = 128
HC = 10
WC = HC * LN
NEAR = 4
ROWS = 1024
F32 = jnp.float32
BF = jnp.bfloat16
INTERPRET = False
VMEM_LIMIT = 16 << 20


def call(kernel, outs, *args, scratch=(), us=1):
    return pl.pallas_call(
        kernel,
        out_shape=[jax.ShapeDtypeStruct(s, d) for s, d in outs],
        in_specs=[pl.BlockSpec(memory_space=pltpu.VMEM)] * len(args),
        out_specs=[pl.BlockSpec(memory_space=pltpu.VMEM)] * len(outs),
        scratch_shapes=[pltpu.VMEM(s, d) for s, d in scratch],
        interpret=INTERPRET,
        cost_estimate=pl.CostEstimate(flops=us * 10**9, bytes_accessed=10**6, transcendentals=0),
        compiler_params=pltpu.CompilerParams(vmem_limit_bytes=VMEM_LIMIT),
    )(*args)


def place():
    frame = lax.axis_index("tm")
    return lax.axis_index("space"), lax.rem(frame, NEAR), lax.div(frame, NEAR)


def lane(shape):
    return lax.broadcasted_iota(jnp.int32, shape, len(shape) - 1)


def halves(x):
    hi = x.astype(BF)
    return hi, (x - hi.astype(F32)).astype(BF)


def joined(hi, lo):
    return hi.astype(F32) + lo.astype(F32)


def mm(a, b, dims):
    return lax.dot_general(a, b, (dims, ((), ())), preferred_element_type=F32)


NN = ((1,), (0,))
NT = ((1,), (1,))
TN = ((0,), (0,))


def flag(cond):
    return jnp.where(cond, 1.0, 0.0).astype(F32)


def pack(ref, mats):
    last = mats[7]
    lanes = lane((HD, LN))
    for i in range(7):
        piece = pltpu.roll(last, HD - 16 * i, 1) if i < 7 else last
        ref[HD * i : HD * (i + 1), :] = jnp.where(lanes < HD, mats[i], piece)
    ref[HD * 7 : HD * 8, :] = mats[8]
    ref[HD * 8 : HD * 9, :] = mats[9]
    ref[HD * 9 : ROWS, :] = jnp.zeros((ROWS - HD * 9, LN), F32)


def unpack(ref):
    lanes = lane((HD, LN))
    mats, last = [], jnp.zeros((HD, LN), F32)
    for i in range(7):
        x = ref[HD * i : HD * (i + 1), :]
        mats.append(jnp.where(lanes < HD, x, 0.0))
        inside = (lanes >= 16 * i) & (lanes < 16 * i + 16)
        last = jnp.where(inside, pltpu.roll(x, 16 + 16 * i, 1), last)
    return mats + [last, ref[HD * 7 : HD * 8, :], ref[HD * 8 : HD * 9, :]]


def pad_rows(x):
    return jnp.concatenate([x, jnp.zeros((LN - HD, LN), x.dtype)], axis=0)


def heads_of(tile):
    out = []
    for h in range(HEADS):
        t, off = divmod(HD * h, LN)
        x = tile(t)
        if off:
            x = pltpu.roll(x, LN - off, 1)
        if off + HD > LN:
            y = pltpu.roll(tile(t + 1), LN - off, 1)
            x = jnp.where(lane(x.shape) < LN - off, x, y)
        out.append(jnp.where(lane(x.shape) < HD, x, 0.0))
    return out


def tiles_of(heads):
    out = []
    for t in range(-(-HEADS * HD // LN)):
        first, off = divmod(LN * t, HD)
        x = heads[first]
        if off:
            x = pltpu.roll(x, LN - off, 1)
        left = HD - off
        while left < LN and first + 1 < HEADS:
            first += 1
            y = pltpu.roll(heads[first], left, 1)
            x = jnp.where(lane(x.shape) < left, x, y)
            left += HD
        out.append(x)
    return out


def loader(ref, rows, width):
    cache = {}

    def tile(t):
        if t not in cache:
            n = min(LN, width - LN * t)
            x = ref[0:rows, LN * t : LN * t + n].astype(F32)
            if n < LN:
                x = jnp.concatenate([x, jnp.zeros((rows, LN - n), F32)], axis=1)
            cache[t] = x
        return cache[t]

    return tile


def spread(refs, relu, keep, send):
    first = place()[0] == 0
    for j, ref in enumerate(refs):
        rows, width = ref.shape
        heads = heads_of(loader(ref, rows, width))
        for i in range(HC):
            a, b = heads[i], heads[i + HC]
            if relu[j]:
                a, b = jnp.maximum(a, 0.0), jnp.maximum(b, 0.0)
            keep[j, :, col(i)] = lax.select(first, a, b).astype(BF)
            send[j, :, col(i)] = lax.select(first, b, a).astype(BF)


def spread_kv_kernel(k, v, keep, send):
    spread((k, v), (True, False), keep, send)


def spread_qg_kernel(q, g, taps, after, keep, send, taps_out):
    first = place()[0] == 0
    spread((q, g), (True, False), keep, send)
    for a in range(3):
        heads = heads_of(loader(taps.at[a], 3, taps.shape[2]))
        for i in range(HC):
            taps_out[a, :, col(i)] = lax.select(first, heads[i], heads[i + HC])


def col(i):
    return slice(LN * i, LN * (i + 1))


def both(keep, recv, j, i):
    return jnp.concatenate([keep[j, :, col(i)], recv[j, :, col(i)]], axis=0)


def conv_kernel(keep_v, recv_v, keep_g, recv_g, taps, local, gc_mine, gc_other, taps_out):
    first = place()[0] == 0
    half = keep_v.shape[1]
    n = 2 * half
    cols = 32
    taps_out[...] = jnp.zeros_like(taps_out)
    pos = lax.broadcasted_iota(jnp.int32, (n, LN), 0) % cols
    zero_row = jnp.zeros((cols, LN), F32)

    def shifts(keep, recv, i):
        a, b = keep[1, :, col(i)].astype(F32), recv[1, :, col(i)].astype(F32)
        x = jnp.concatenate([lax.select(first, a, b), lax.select(first, b, a)], axis=0)
        before = jnp.where(pos == 0, 0.0, pltpu.roll(x, 1, 0))
        after = jnp.where(pos == cols - 1, 0.0, pltpu.roll(x, n - 1, 0))
        return before, x, after

    def up(u):
        return jnp.concatenate([zero_row, u[: n - cols]], axis=0)

    def down(u):
        return jnp.concatenate([u[cols:], zero_row], axis=0)

    def put(mine, other, x, i):
        mine[:, col(i)] = lax.select(first, x[:half], x[half:])
        other[:, col(i)] = lax.select(first, x[half:], x[:half])

    for i in range(HC):
        w = [taps[a, :, col(i)] for a in range(3)]
        vs, gs = shifts(keep_v, recv_v, i), shifts(keep_g, recv_g, i)
        u = [sum(w[a][b : b + 1] * vs[b] for b in range(3)) for a in range(3)]
        put(local.at[0:half], local.at[half:n], up(u[0]) + u[1] + down(u[2]), i)
        u = [sum(w[a][b : b + 1] * gs[2 - b] for b in range(3)) for a in range(3)]
        put(gc_mine, gc_other, down(u[0]) + u[1] + up(u[2]), i)
        g = gs[1]
        for b in range(3):
            s = vs[b]
            for a, prod in enumerate((g[cols:] * s[: n - cols], g * s, g[: n - cols] * s[cols:])):
                r = 9 * i + 3 * a + b
                taps_out[r : r + 1, :] = jnp.sum(prod, axis=0, keepdims=True)


def rows_at(p, k, n):
    return pl.ds(pl.multiple_of((p ^ k) * n, n), n)


def partial_kernel(keep, recv, own, ksum, a1, a2, a3, state):
    p = place()[1]
    ksum[...] = jnp.zeros_like(ksum)
    mats = []
    for i in range(HC):
        keys = both(keep, recv, 0, i)
        mats.append(mm(keys, both(keep, recv, 1, i), TN)[:HD])
        ksum[i : i + 1, :] = jnp.sum(keys.astype(F32), axis=0, keepdims=True)
    pack(state, mats)
    n = ROWS // NEAR
    own[...] = state[rows_at(p, 0, n), :]
    khi, klo = halves(ksum[...])
    for k, ref in enumerate((a1, a2, a3), 1):
        hi, lo = halves(state[rows_at(p, k, n), :])
        ref[0:n, :] = hi
        ref[n : 2 * n, :] = lo
        ref[2 * n : 2 * n + 16, :] = khi
        ref[2 * n + 16 : 2 * n + 32, :] = klo


def block_kernel(own, ksum, a1, a2, a3, pay, kpre):
    p = place()[1]
    n = ROWS // NEAR
    total, ktot, kp = own[...], ksum[...], ksum[...]
    for k, ref in enumerate((a1, a2, a3), 1):
        total = total + joined(ref[0:n, :], ref[n : 2 * n, :])
        ks = joined(ref[2 * n : 2 * n + 16, :], ref[2 * n + 16 : 2 * n + 32, :])
        ktot = ktot + ks
        kp = kp + flag((p ^ k) <= p) * ks
    kpre[...] = kp
    khi, klo = halves(ktot)
    m = n // pay.shape[0]
    for b in range(pay.shape[0]):
        hi, lo = halves(total[m * b : m * (b + 1)])
        pay[b, 0:m, :] = hi
        pay[b, m : 2 * m, :] = lo
        pay[b, 2 * m : 2 * m + 16, :] = khi
        pay[b, 2 * m + 16 : 2 * m + 32, :] = klo


def reciprocal_of(q, kt, i):
    row = jnp.broadcast_to(kt[i : i + 1, :], (LN, LN))
    hi, lo = halves(row)
    den = mm(jnp.concatenate([q, q], axis=1), jnp.concatenate([hi, lo], axis=1), NT)
    return 1.0 / (den + 1.0)


def turn_kernel(got, kpre, keep, recv, down, kt, own, c1, c2, c3, state):
    _, p, mine = place()
    nb = got.shape[0]
    n = ROWS // NEAR
    m = n // nb
    run, key_total = jnp.zeros((m, LN), F32), kpre[...]
    for b in range(nb):
        hi, lo = halves(run)
        down[b, 0:m, :] = hi
        down[b, m : 2 * m, :] = lo
        run = run + joined(got[b, 0:m, :], got[b, m : 2 * m, :])
        ks = joined(got[b, 2 * m : 2 * m + 16, :], got[b, 2 * m + 16 : 2 * m + 32, :])
        key_total = key_total + flag(b < mine) * ks
    kt[...] = key_total
    mats = []
    for i in range(HC):
        q = both(keep, recv, 0, i)
        scaled = both(keep, recv, 1, i).astype(F32) * reciprocal_of(q, key_total, i)
        hi, lo = halves(scaled)
        x = mm(q, jnp.concatenate([hi, lo], axis=1), TN)[:HD]
        mats.append(x[:, :LN] + x[:, LN:])
    pack(state, mats)
    own[...] = state[rows_at(p, 0, n), :]
    for k, ref in enumerate((c1, c2, c3), 1):
        ref[...] = state[rows_at(p, k, n), :].astype(BF)


def back_block_kernel(own, c1, c2, c3, down, taps, pay):
    nb = pay.shape[0]
    m = ROWS // NEAR // nb
    total = own[...]
    for ref in (c1, c2, c3):
        total = total + ref[...].astype(F32)
    for b in range(nb):
        pay[b, 0 : 2 * m, :] = down[b]
        pay[b, 2 * m : 3 * m, :] = total[m * b : m * (b + 1)].astype(BF)
        hi, lo = halves(taps[16 * b : 16 * (b + 1), :])
        pay[b, 3 * m : 3 * m + 16, :] = hi
        pay[b, 3 * m + 16 : 3 * m + 32, :] = lo


def four_rows(x):
    hi = x.astype(BF).astype(F32)
    return jnp.concatenate([hi, x - hi, jnp.zeros((8, LN), F32)], axis=0).astype(BF)


def of_four(x):
    x = x.astype(F32)
    return x[0:4] + x[4:8]


def prefix_kernel(got, own, a1, a2, a3, s_own, e1, e2, e3, taps_own, back, taps):
    p = place()[1]
    nb = got.shape[0]
    n = ROWS // NEAR
    m = n // nb
    base = jnp.concatenate([joined(got[b, 0:m, :], got[b, m : 2 * m, :]) for b in range(nb)], axis=0)
    run = jnp.zeros((m, LN), F32)
    t = jnp.zeros((16, LN), F32)
    for b in reversed(range(nb)):
        back[b] = run.astype(BF)
        run = run + got[b, 2 * m : 3 * m, :].astype(F32)
        t = t + joined(got[b, 3 * m : 3 * m + 16, :], got[b, 3 * m + 16 : 3 * m + 32, :])
    for j in range(NEAR):
        taps[j] = t[4 * j : 4 * (j + 1)]
    parts = [own[...]] + [joined(r[0:n, :], r[n : 2 * n, :]) for r in (a1, a2, a3)]
    for k, ref in enumerate((s_own, e1, e2, e3)):
        x = base
        for j in range(NEAR):
            x = x + flag((p ^ j) <= (p ^ k)) * parts[j]
        if k == 0:
            ref[...] = x
        else:
            hi, lo = halves(x)
            ref[0:n, :] = hi
            ref[n : 2 * n, :] = lo
            ref[2 * n : 2 * n + 16, :] = four_rows(taps[p ^ k])
    taps_own[...] = taps[p]


def attend_kernel(
    e1, e2, e3, s_own, kt, keep, recv, local, taps_own, back, mine, other, pay, gks_out, state, gks
):
    p = place()[1]
    nb = pay.shape[0]
    n = ROWS // NEAR
    m = n // nb
    half = keep.shape[1]
    state[rows_at(p, 0, n), :] = s_own[...]
    taps = taps_own[...]
    for k, ref in enumerate((e1, e2, e3), 1):
        state[rows_at(p, k, n), :] = joined(ref[0:n, :], ref[n : 2 * n, :])
        taps = taps + of_four(ref[2 * n : 2 * n + 16, :])
    mats = unpack(state)
    key_total = kt[...]
    gks[...] = jnp.zeros_like(gks)
    ones = jnp.ones((2 * LN, LN), BF)
    for i in range(HC):
        q, g = both(keep, recv, 0, i), both(keep, recv, 1, i)
        hi, lo = halves(pad_rows(mats[i]))
        recip = reciprocal_of(q, key_total, i)
        out = mm(jnp.concatenate([q, q], axis=1), jnp.concatenate([hi, lo], axis=0), NN) * recip
        x = (out + local[:, col(i)]).astype(BF)
        mine[0, :, col(i)] = x[:half]
        other[0, :, col(i)] = x[half:]
        ghi, glo = halves(g.astype(F32) * out)
        gden = -mm(jnp.concatenate([ghi, glo], axis=1), ones, NN) * recip
        gs = mm(jnp.concatenate([g, g], axis=1), jnp.concatenate([hi, lo], axis=1), NT)
        qf = q.astype(F32)
        x = jnp.where(qf > 0.0, gs * recip + gden * key_total[i : i + 1, :], 0.0).astype(BF)
        mine[1, :, col(i)] = x[:half]
        other[1, :, col(i)] = x[half:]
        gks[i : i + 1, :] = jnp.sum(gden * qf, axis=0, keepdims=True)
    gks_out[...] = gks[...]
    khi, klo = halves(gks[...])
    four = four_rows(taps)
    for b in range(nb):
        pay[b, 0:m, :] = back[b]
        pay[b, m : m + 16, :] = khi
        pay[b, m + 16 : m + 32, :] = klo
        pay[b, m + 32 : m + 48, :] = four


def suffix_kernel(got, own, c1, c2, c3, gks, g0, g1, g2, g3):
    _, p, mine = place()
    nb = got.shape[0]
    n = ROWS // NEAR
    m = n // nb
    base = jnp.concatenate([got[b, 0:m, :].astype(F32) for b in range(nb)], axis=0)
    later = jnp.zeros((16, LN), F32)
    for b in range(nb):
        ks = joined(got[b, m : m + 16, :], got[b, m + 16 : m + 32, :])
        later = later + flag(b > mine) * ks
    taps = jnp.concatenate([of_four(got[b, m + 32 : m + 48, :]) for b in range(nb)], axis=0)
    thi, tlo = halves(taps)
    parts = [own[...]] + [r[...].astype(F32) for r in (c1, c2, c3)]
    nt = taps.shape[0]
    for k, ref in enumerate((g0, g1, g2, g3)):
        x = base
        for j in range(NEAR):
            x = x + flag((p ^ j) >= (p ^ k)) * parts[j]
        ref[0:n, :] = x.astype(BF)
        hi, lo = halves(later + flag(p >= (p ^ k)) * gks[...])
        ref[n : n + 16, :] = hi
        ref[n + 16 : n + 32, :] = lo
        ref[n + 32 : n + 32 + nt, :] = thi
        ref[n + 32 + nt : n + 32 + 2 * nt, :] = tlo


def assembled(refs, state, taps):
    p = place()[1]
    n = ROWS // NEAR
    nt = (refs[0].shape[0] - n - 32) // 2
    total = jnp.zeros((16, LN), F32)
    for k, ref in enumerate(refs):
        state[rows_at(p, k, n), :] = ref[0:n, :].astype(F32)
        total = total + joined(ref[n : n + 16, :], ref[n + 16 : n + 32, :])
        part = joined(ref[n + 32 : n + 32 + nt, :], ref[n + 32 + nt : n + 32 + 2 * nt, :])
        for b in range(nt // 4):
            taps[b, p ^ k] = part[4 * b : 4 * (b + 1)]
    return unpack(state), total


def finish_kernel(
    g0, g1, g2, g3, o0, o1, o2, o3, keep, send, gc_mine, gc_other, key, value, taps, state, taps_a, taps_b
):
    first = place()[0] == 0
    sides = []
    for refs, tokens, conv, scratch in (
        ((g0, g1, g2, g3), keep, gc_mine, taps_a),
        ((o0, o1, o2, o3), send, gc_other, taps_b),
    ):
        mats, total = assembled(refs, state, scratch)
        keys_out, values_out, taps_out = [], [], []
        for i in range(HC):
            keys, v = tokens[0, :, col(i)], tokens[1, :, col(i)]
            hi, lo = halves(pad_rows(mats[i]))
            gk = mm(jnp.concatenate([v, v], axis=1), jnp.concatenate([hi, lo], axis=1), NT)
            keys_out.append(jnp.where(keys.astype(F32) > 0.0, gk + total[i : i + 1, :], 0.0))
            gm = mm(jnp.concatenate([keys, keys], axis=1), jnp.concatenate([hi, lo], axis=0), NN)
            values_out.append(gm + conv[:, col(i)])
        sides.append((keys_out, values_out))
    for j, ref in enumerate((key, value)):
        gather_heads(first, sides[0][j], sides[1][j], ref)
    for a in range(3):
        rows = []
        for scratch in (taps_a, taps_b):
            heads = []
            for i in range(HC):
                lines = []
                for b in range(3):
                    r = 9 * i + 3 * a + b
                    lines.append(scratch[r // 16, (r % 16) // 4, r % 4 : r % 4 + 1, :])
                heads.append(jnp.concatenate(lines, axis=0))
            rows.append(heads)
        gather_heads(first, rows[0], rows[1], taps.at[a])


def gather_heads(first, mine, other, ref):
    heads = [lax.select(first, mine[i], other[i]) for i in range(HC)]
    heads += [lax.select(first, other[i], mine[i]) for i in range(HC)]
    width = ref.shape[1]
    for t, x in enumerate(tiles_of(heads)):
        n = min(LN, width - LN * t)
        ref[:, LN * t : LN * t + n] = x[:, :n].astype(ref.dtype)


def merge_kernel(mine, other, out_a, out_b):
    first = place()[0] == 0
    for j, ref in enumerate((out_a, out_b)):
        heads = [[x[j, :, col(i)].astype(F32) for i in range(HC)] for x in (mine, other)]
        gather_heads(first, heads[0], heads[1], ref)


def shards(query_pre, key_pre, value_pre, grad_out, conv_taps):
    shape = value_pre.shape
    width = shape[-1]
    t = shape[0] * shape[1] * shape[2]
    frames = lax.axis_size("tm")
    nb = frames // NEAR
    across = [[j + NEAR * b for b in range(nb)] for j in range(NEAR)]

    def over(x):
        return lax.ppermute(x, "space", [(0, 1), (1, 0)])

    def near(arrays):
        return [
            lax.ppermute(a, "tm", [(i, i ^ k) for i in range(frames)])
            for k, a in enumerate(arrays, 1)
        ]

    def far(x):
        return lax.all_to_all(x, "tm", 0, 0, axis_index_groups=across, tiled=True)

    n = ROWS // NEAR
    m = n // nb
    q, k, v, g = (x.reshape(t, width) for x in (query_pre, key_pre, value_pre, grad_out))
    pair = ((2, t, WC), BF)
    share = ((n, LN), F32)
    small = ((16, LN), F32)
    state = ((ROWS, LN), F32)

    keep_kv, send_kv = call(spread_kv_kernel, [pair, pair], k, v, us=3)
    recv_kv = over(send_kv)
    own_b, ksum, *out = call(
        partial_kernel, [share, small] + [((2 * n + 32, LN), BF)] * 3, keep_kv, recv_kv, scratch=[state], us=3
    )
    got_a = near(out)
    keep_qg, send_qg, taps = call(
        spread_qg_kernel, [pair, pair, ((3, 3, WC), F32)], q, g, conv_taps, ksum, us=3
    )
    recv_qg = over(send_qg)
    local, gc_mine, gc_other, taps_part = call(
        conv_kernel,
        [((2 * t, WC), F32), ((t, WC), F32), ((t, WC), F32), ((LN, LN), F32)],
        keep_kv, recv_kv, keep_qg, recv_qg, taps, us=6,
    )
    gc_other = over(gc_other)
    pay, kpre = call(block_kernel, [((nb, 2 * m + 32, LN), BF), small], own_b, ksum, *got_a)
    got = far(pay)
    down, kt, own_d, *out = call(
        turn_kernel,
        [((nb, 2 * m, LN), BF), small, share] + [((n, LN), BF)] * 3,
        got, kpre, keep_qg, recv_qg, scratch=[state], us=4,
    )
    got_c = near(out)
    (pay,) = call(back_block_kernel, [((nb, 3 * m + 32, LN), BF)], own_d, *got_c, down, taps_part)
    got = far(pay)
    s_own, e1, e2, e3, taps_own, back = call(
        prefix_kernel,
        [share] + [((2 * n + 16, LN), BF)] * 3 + [((4, LN), F32), ((nb, m, LN), BF)],
        got, own_b, *got_a, scratch=[((NEAR, 4, LN), F32)],
    )
    got_e = near((e1, e2, e3))
    mine, other, pay, gks = call(
        attend_kernel,
        [pair, pair, ((nb, m + 48, LN), BF), small],
        *got_e, s_own, kt, keep_qg, recv_qg, local, taps_own, back, scratch=[state, small], us=4,
    )
    got = far(pay)
    whole = ((t, width), BF)
    attended, query_grad = call(merge_kernel, [whole, whole], mine, over(other), us=3)
    g0, *out = call(suffix_kernel, [((n + 32 + 8 * nb, LN), BF)] * 4, got, own_d, *got_c, gks)
    gs = [g0] + near(out)
    key_grad, value_grad, taps_grad = call(
        finish_kernel,
        [whole, whole, (conv_taps.shape, F32)],
        *gs, *[over(x) for x in gs], keep_kv, send_kv, gc_mine, gc_other,
        scratch=[state] + [((nb, NEAR, 4, LN), F32)] * 2, us=5,
    )
    return (
        attended.reshape(shape),
        query_grad.reshape(shape),
        key_grad.reshape(shape),
        value_grad.reshape(shape),
        taps_grad,
    )


def solution(mesh):
    frame = P(("groups", "tm"), "space", None, None)
    return jax.shard_map(
        shards,
        mesh=mesh,
        in_specs=(frame, frame, frame, frame, P()),
        out_specs=(frame, frame, frame, frame, P("groups", None, None)),
        check_vma=False,
    )
```

time: 250 us -> 216 us (0.86)
  blocking collectives: 69.9 us -> 33.3 us
  Pallas kernels: 41.7 us -> 15.8 us
  starting transfers between devices: 75.9 us -> 96.5 us
  waiting for transfers between devices: 46.7 us -> 58.9 us
  local copies, waits for them, and re-layouts: 13.5 us -> 10.2 us
    all_to_all x2 -> x1, blocking collectives: 69.9 us -> 33.3 us  [far(): return lax.all_to_all(x, 'tm', 0, 0, axis_index_groups=across, tiled=True)]
    pallas_call x6 -> x0, Pallas kernels: 22.9 us -> none  [with_scratch(): pl.pallas_call(kernel, out_shape=[jax.ShapeDtypeStruct(s, d) for s, d in...]
    all_to_all x1 -> x2, waiting for transfers between devices: 27.1 us -> 37.9 us  [far(): return lax.all_to_all(x, 'tm', 0, 0, axis_index_groups=across, tiled=True)]
    ppermute x6 -> x8, starting transfers between devices: 27.3 us -> 34.7 us  [over(): return lax.ppermute(x, 'space', [(0, 1), (1, 0)])]
    ppermute x12, starting transfers between devices: 37 us -> 44.1 us  [near(): lax.ppermute(a, 'tm', [(i, i ^ k) for i in range(frames)])]
    all_to_all x1 -> x2, starting transfers between devices: 11.6 us -> 17.8 us  [far(): return lax.all_to_all(x, 'tm', 0, 0, axis_index_groups=across, tiled=True)]
    reshape x2 -> x0, local copies, waits for them, and re-layouts: 3.19 us -> none  [the longest x1 1.6 us: shards(): conv_taps.reshape(9, width)]
    squeeze x4 -> x0, local copies, waits for them, and re-layouts: 3.04 us -> none  [the longest x1 1.03 us: shards(): key[1]]
  transfers between devices with their start and end apart: 19 -> 22, of which waited for: 7 -> 10; matrix products, arithmetic and copies ran while one was open for 1% -> 0% of each run, Pallas kernels for 5% -> 3%
where the time goes in v2:
time: 216 us
  starting transfers between devices  96.5 us (45%)
  waiting for transfers between devices  58.9 us (27%)
  blocking collectives  33.3 us (15%)
  Pallas kernels  15.8 us (7%)
  local copies, waits for them, and re-layouts  10.2 us (5%)
    ppermute x12, starting transfers between devices, near(): lax.ppermute(a, 'tm', [(i, i ^ k) for i in range(frames)])  44.1 us
    all_to_all x2, waiting for transfers between devices, far(): return lax.all_to_all(x, 'tm', 0, 0, axis_index_groups=across, tiled=True)  37.9 us
    ppermute x8, starting transfers between devices, over(): return lax.ppermute(x, 'space', [(0, 1), (1, 0)])  34.7 us
    all_to_all x1, blocking collectives, far(): return lax.all_to_all(x, 'tm', 0, 0, axis_index_groups=across, tiled=True)  33.3 us
    all_to_all x2, starting transfers between devices, far(): return lax.all_to_all(x, 'tm', 0, 0, axis_index_groups=across, tiled=True)  17.8 us
    ppermute x12, waiting for transfers between devices, near(): lax.ppermute(a, 'tm', [(i, i ^ k) for i in range(frames)])  17.5 us
    pallas_call x12, Pallas kernels, call(): pl.pallas_call(kernel, out_shape=[jax.ShapeDtypeStruct(s, d) for s, d in...  15.8 us
    unnamed x50, local copies, waits for them, and re-layouts  10.2 us
  transfers between devices with their start and end apart: 22, of which 10 were waited for; matrix products, arithmetic and copies ran while one was open for 0% of the time, Pallas kernels for 3%

profile of v2, /device:TPU:37, one launch (start us, length us, event | category | flops | bytes accessed | tf_op | source)
XLA Modules:
  0.0 215.6 jit_solution(10783887078581073325)
XLA Ops:
  0.6 1.1 copy-done
  1.7 1.1 copy-done.1
  3.5 20.5 %collective-permute-start = (bf16[2,128,1280]{2,1,0:T(8,128)(2,1)S(1)}, bf16[2,128,1280]{2,1,0:T(8,128)(2,1)S(1)}, u32[]{:S(2)}, u32[]{:S(2)}) collective-permute-start(bf16[2,128,1280]{2,1,0:T(8,128)(2,1)S(1)} %get-tuple-element.47.send), channel_id=1, source_target_pairs={{0,1},{1,0},{2,3},{3,2},{4,5},{5,4},{6,7},{7,6},{8,9},{9,8},{10,11... | collective-permute-start | bytes 1966088 | tf_op jit(solution)/shard_map/ppermute | solution.py:488
  24.1 1.7 collective-permute-done.recv.recv_v
  26.7 3.4 %collective-permute-start.3 = (bf16[544,128]{1,0:T(8,128)(2,1)S(1)}, bf16[544,128]{1,0:T(8,128)(2,1)S(1)}, u32[]{:S(2)}, u32[]{:S(2)}) collective-permute-start(bf16[544,128]{1,0:T(8,128)(2,1)S(1)} %get-tuple-element.52), channel_id=1, source_target_pairs={{0,6},{2,4},{4,2},{6,0},{8,14},{10,12},{12,10},{14,8},{16,22},{18,... | collective-permute-start | bytes 417800 | tf_op jit(solution)/shard_map/ppermute | solution.py:492
  30.0 2.4 %collective-permute-done.1.a1 = bf16[544,128]{1,0:T(8,128)(2,1)S(1)} collective-permute-done((bf16[544,128]{1,0:T(8,128)(2,1)S(1)}, bf16[544,128]{1,0:T(8,128)(2,1)S(1)}, u32[]{:S(2)}, u32[]{:S(2)}) %collective-permute-start.1) | collective-permute-done | bytes 139296 | tf_op jit(solution)/shard_map/ppermute | solution.py:492
  32.4 6.0 %collective-permute-done.2.a2 = bf16[544,128]{1,0:T(8,128)(2,1)S(1)} collective-permute-done((bf16[544,128]{1,0:T(8,128)(2,1)S(1)}, bf16[544,128]{1,0:T(8,128)(2,1)S(1)}, u32[]{:S(2)}, u32[]{:S(2)}) %collective-permute-start.2) | collective-permute-done | bytes 139296 | tf_op jit(solution)/shard_map/ppermute | solution.py:492
  39.2 12.6 %all-to-all-start = ((bf16[8,96,128]{2,1,0:T(8,128)(2,1)}), bf16[8,96,128]{2,1,0:T(8,128)(2,1)S(1)}, u32[]{:S(2)}, u32[]{:S(2)}) async-start(bf16[8,96,128]{2,1,0:T(8,128)(2,1)} %get-tuple-element.53), calls=%async_computation | async-start | bytes 393216 | tf_op jit(solution)/shard_map/all_to_all | solution.py:497
  54.1 3.1 %collective-permute-start.4 = (bf16[2,128,1280]{2,1,0:T(8,128)(2,1)S(1)}, bf16[2,128,1280]{2,1,0:T(8,128)(2,1)S(1)}, u32[]{:S(2)}, u32[]{:S(2)}) collective-permute-start(bf16[2,128,1280]{2,1,0:T(8,128)(2,1)S(1)} %get-tuple-element.56), channel_id=1, source_target_pairs={{0,1},{1,0},{2,3},{3,2},{4,5},{5,4},{6,7},{7,6},{8,9},{9,8},{10,11... | collective-permute-start | bytes 1966088 | tf_op jit(solution)/shard_map/ppermute | solution.py:488
  57.2 1.7 collective-permute-done.4.recv.recv_g
  58.9 16.0 %all-to-all-done.got = bf16[8,96,128]{2,1,0:T(8,128)(2,1)S(1)} async-done(((bf16[8,96,128]{2,1,0:T(8,128)(2,1)}), bf16[8,96,128]{2,1,0:T(8,128)(2,1)S(1)}, u32[]{:S(2)}, u32[]{:S(2)}) %all-to-all-start) | async-done | bytes 196640 | tf_op jit(solution)/shard_map/all_to_all | solution.py:497
  75.0 1.1 copy-done.19
  76.1 2.5 %shard_map.96 = (bf16[8,64,128]{2,1,0:T(8,128)(2,1)S(1)}, f32[16,128]{1,0:T(8,128)S(1)}, f32[256,128]{1,0:T(8,128)S(1)}, bf16[256,128]{1,0:T(8,128)(2,1)S(1)}, b...) custom-call(bf16[8,96,128]{2,1,0:T(8,128)(2,1)S(1)} %all-to-all-done.got, ...), custom_call_target="tpu_custom_call" | custom-call | flops 4000000000 | bytes 1000000 | tf_op jit(solution)/shard_map/pallas_call | solution.py:24
  78.6 12.6 %collective-permute-start.5 = (bf16[256,128]{1,0:T(8,128)(2,1)S(1)}, bf16[256,128]{1,0:T(8,128)(2,1)S(1)}, u32[]{:S(2)}, u32[]{:S(2)}) collective-permute-start(bf16[256,128]{1,0:T(8,128)(2,1)S(1)} %get-tuple-element.58), channel_id=1, source_target_pairs={{0,2},{2,0},{4,6},{6,4},{8,10},{10,8},{12,14},{14,12},{16,18},{18,... | collective-permute-start | bytes 196616 | tf_op jit(solution)/shard_map/ppermute | solution.py:492
  91.2 1.3 collective-permute-start.6
  92.5 1.0 collective-permute-start.7
  93.6 3.0 %shard_map.97 = (f32[256,1280]{1,0:T(8,128)S(1)}, f32[128,1280]{1,0:T(8,128)S(1)}, f32[128,1280]{1,0:T(8,128)S(1)}, f32[128,128]{1,0:T(8,128)S(1)}) custom-call(bf16[2,128,1280]{2,1,0:T(8,128)(2,1)S(1)} %copy-done.14, bf16[2,128,1280]{2,1,0:T(8,128)(2,1)S(1)} %collective-permute-done.recv.recv_v, bf16[2,128,1280]{2,1,0:T(8,128)(2,1)S(1)} %copy-done.20, ...), custom_call_target="tpu_custom_call" | custom-call | flops 6000000000 | bytes 1000000 | tf_op jit(solution)/shard_map/pallas_call | solution.py:24
  99.3 33.3 %all_to_all.15.got = bf16[8,128,128]{2,1,0:T(8,128)(2,1)S(1)} all-to-all(bf16[8,128,128]{2,1,0:T(8,128)(2,1)S(1)} %shard_map.98), channel_id=1, replica_groups={{0,8,16,24,32,40,48,56},{2,10,18,26,34,42,50,58},{4,12,20,28,36,44,52,6..., dimensions={0} | all-to-all | bytes 524288 | tf_op jit(solution)/shard_map/all_to_all | solution.py:497
  132.9 11.5 %collective-permute-start.8 = (bf16[528,128]{1,0:T(8,128)(2,1)S(1)}, bf16[528,128]{1,0:T(8,128)(2,1)S(1)}, u32[]{:S(2)}, u32[]{:S(2)}) collective-permute-start(bf16[528,128]{1,0:T(8,128)(2,1)S(1)} %get-tuple-element.64), channel_id=1, source_target_pairs={{0,2},{2,0},{4,6},{6,4},{8,10},{10,8},{12,14},{14,12},{16,18},{18,... | collective-permute-start | bytes 405512 | tf_op jit(solution)/shard_map/ppermute | solution.py:492
  145.3 1.3 collective-permute-start.10
  146.8 2.4 %collective-permute-done.9.e2 = bf16[528,128]{1,0:T(8,128)(2,1)S(1)} collective-permute-done((bf16[528,128]{1,0:T(8,128)(2,1)S(1)}, bf16[528,128]{1,0:T(8,128)(2,1)S(1)}, u32[]{:S(2)}, u32[]{:S(2)}) %collective-permute-start.9) | collective-permute-done | bytes 135200 | tf_op jit(solution)/shard_map/ppermute | solution.py:492
  149.3 6.0 %collective-permute-done.10.e3 = bf16[528,128]{1,0:T(8,128)(2,1)S(1)} collective-permute-done((bf16[528,128]{1,0:T(8,128)(2,1)S(1)}, bf16[528,128]{1,0:T(8,128)(2,1)S(1)}, u32[]{:S(2)}, u32[]{:S(2)}) %collective-permute-start.10) | collective-permute-done | bytes 135200 | tf_op jit(solution)/shard_map/ppermute | solution.py:492
  155.2 2.9 %shard_map.100 = (bf16[2,128,1280]{2,1,0:T(8,128)(2,1)S(1)}, bf16[2,128,1280]{2,1,0:T(8,128)(2,1)S(1)}, bf16[8,80,128]{2,1,0:T(8,128)(2,1)}, f32[16,128]{1,0:T(8,128)S(1)}) custom-call(bf16[528,128]{1,0:T(8,128)(2,1)S(1)} %collective-permute-done.8.e1, bf16[528,128]{1,0:T(8,128)(2,1)S(1)} %collective-permute-done.9.e2, ...), custom_call_target="tpu_custom_call" | custom-call | flops 4000000000 | bytes 1000000 | tf_op jit(solution)/shard_map/pallas_call | solution.py:24
  159.0 5.2 %all-to-all-start.2 = ((bf16[8,80,128]{2,1,0:T(8,128)(2,1)}), bf16[8,80,128]{2,1,0:T(8,128)(2,1)S(1)}, u32[]{:S(2)}, u32[]{:S(2)}) async-start(bf16[8,80,128]{2,1,0:T(8,128)(2,1)} %get-tuple-element.76), calls=%async_computation.2 | async-start | bytes 327680 | tf_op jit(solution)/shard_map/all_to_all | solution.py:497
  164.2 2.5 %collective-permute-start.11 = (bf16[2,128,1280]{2,1,0:T(8,128)(2,1)S(1)}, bf16[2,128,1280]{2,1,0:T(8,128)(2,1)S(1)}, u32[]{:S(2)}, u32[]{:S(2)}) collective-permute-start(bf16[2,128,1280]{2,1,0:T(8,128)(2,1)S(1)} %get-tuple-element.73), channel_id=1, source_target_pairs={{0,1},{1,0},{2,3},{3,2},{4,5},{5,4},{6,7},{7,6},{8,9},{9,8},{10,11... | collective-permute-start | bytes 1966088 | tf_op jit(solution)/shard_map/ppermute | solution.py:488
  166.9 21.9 %all-to-all-done.2.got = bf16[8,80,128]{2,1,0:T(8,128)(2,1)S(1)} async-done(((bf16[8,80,128]{2,1,0:T(8,128)(2,1)}), bf16[8,80,128]{2,1,0:T(8,128)(2,1)S(1)}, u32[]{:S(2)}, u32[]{:S(2)}) %all-to-all-start.2) | async-done | bytes 163872 | tf_op jit(solution)/shard_map/all_to_all | solution.py:497
  191.5 5.5 %collective-permute-start.12 = (bf16[352,128]{1,0:T(8,128)(2,1)S(1)}, bf16[352,128]{1,0:T(8,128)(2,1)S(1)}, u32[]{:S(2)}, u32[]{:S(2)}) collective-permute-start(bf16[352,128]{1,0:T(8,128)(2,1)S(1)} %get-tuple-element.79), channel_id=1, source_target_pairs={{0,2},{2,0},{4,6},{6,4},{8,10},{10,8},{12,14},{14,12},{16,18},{18,... | collective-permute-start | bytes 270344 | tf_op jit(solution)/shard_map/ppermute | solution.py:492
  197.1 5.1 %collective-permute-start.13 = (bf16[352,128]{1,0:T(8,128)(2,1)S(1)}, bf16[352,128]{1,0:T(8,128)(2,1)S(1)}, u32[]{:S(2)}, u32[]{:S(2)}) collective-permute-start(bf16[352,128]{1,0:T(8,128)(2,1)S(1)} %get-tuple-element.80), channel_id=1, source_target_pairs={{0,4},{2,6},{4,0},{6,2},{8,12},{10,14},{12,8},{14,10},{16,20},{18,... | collective-permute-start | bytes 270344 | tf_op jit(solution)/shard_map/ppermute | solution.py:492
  203.2 3.3 %collective-permute-start.15 = (bf16[352,128]{1,0:T(8,128)(2,1)S(1)}, bf16[352,128]{1,0:T(8,128)(2,1)S(1)}, u32[]{:S(2)}, u32[]{:S(2)}) collective-permute-start(bf16[352,128]{1,0:T(8,128)(2,1)S(1)} %get-tuple-element.78.g0), channel_id=1, source_target_pairs={{0,1},{1,0},{2,3},{3,2},{4,5},{5,4},{6,7},{7,6},{8,9},{9,8},{10,11... | collective-permute-start | bytes 270344 | tf_op jit(solution)/shard_map/ppermute | solution.py:488
  206.8 4.8 %collective-permute-start.17 = (bf16[352,128]{1,0:T(8,128)(2,1)S(1)}, bf16[352,128]{1,0:T(8,128)(2,1)S(1)}, u32[]{:S(2)}, u32[]{:S(2)}) collective-permute-start(bf16[352,128]{1,0:T(8,128)(2,1)S(1)} %collective-permute-done.13.g2), channel_id=1, source_target_pairs={{0,1},{1,0},{2,3},{3,2},{4,5},{5,4},{6,7},{7,6},{8,9},{9,8},{10,11... | collective-permute-start | bytes 270344 | tf_op jit(solution)/shard_map/ppermute | solution.py:488
  211.7 1.5 shard_map.101
  213.2 2.4 %shard_map.103 = (bf16[128,2240]{1,0:T(8,128)(2,1)}, bf16[128,2240]{1,0:T(8,128)(2,1)}, f32[3,3,2240]{2,1,0:T(4,128)}) custom-call(bf16[352,128]{1,0:T(8,128)(2,1)S(1)} %get-tuple-element.78.g0, bf16[352,128]{1,0:T(8,128)(2,1)S(1)} %collective-permute-done.12.g1, bf16[352,128]{1,0:T(8,128)(2,1)S(1)} %collective-permute-done.13.g2, ...), custom_call_target="tpu_custom_call" | custom-call | flops 5000000000 | bytes 1000000 | tf_op jit(solution)/shard_map/pallas_call | solution.py:24
  (75 shorter events, 13.8 us)
Async XLA Ops:
  3.5 22.8 %copy-start.13 = (bf16[2,128,1280]{2,1,0:T(8,128)(2,1)}, bf16[2,128,1280]{2,1,0:T(8,128)(2,1)S(1)}, u32[]{:S(2)}) copy-start(bf16[2,128,1280]{2,1,0:T(8,128)(2,1)S(1)} %get-tuple-element.46.keep.keep_v) | copy-start | bytes 1966084
  3.5 22.3 %collective-permute-start = (bf16[2,128,1280]{2,1,0:T(8,128)(2,1)S(1)}, bf16[2,128,1280]{2,1,0:T(8,128)(2,1)S(1)}, u32[]{:S(2)}, u32[]{:S(2)}) collective-permute-start(bf16[2,128,1280]{2,1,0:T(8,128)(2,1)S(1)} %get-tuple-element.47.send), channel_id=1, source_target_pairs={{0,1},{1,0},{2,3},{3,2},{4,5},{5,4},{6,7},{7,6},{8,9},{9,8},{10,11... | collective-permute-start | bytes 1966088 | tf_op jit(solution)/shard_map/ppermute | solution.py:488
  26.4 6.1 %collective-permute-start.1 = (bf16[544,128]{1,0:T(8,128)(2,1)S(1)}, bf16[544,128]{1,0:T(8,128)(2,1)S(1)}, u32[]{:S(2)}, u32[]{:S(2)}) collective-permute-start(bf16[544,128]{1,0:T(8,128)(2,1)S(1)} %get-tuple-element.50), channel_id=1, source_target_pairs={{0,2},{2,0},{4,6},{6,4},{8,10},{10,8},{12,14},{14,12},{16,18},{18,... | collective-permute-start | bytes 417800 | tf_op jit(solution)/shard_map/ppermute | solution.py:492
  26.5 11.9 %collective-permute-start.2 = (bf16[544,128]{1,0:T(8,128)(2,1)S(1)}, bf16[544,128]{1,0:T(8,128)(2,1)S(1)}, u32[]{:S(2)}, u32[]{:S(2)}) collective-permute-start(bf16[544,128]{1,0:T(8,128)(2,1)S(1)} %get-tuple-element.51), channel_id=1, source_target_pairs={{0,4},{2,6},{4,0},{6,2},{8,12},{10,14},{12,8},{14,10},{16,20},{18,... | collective-permute-start | bytes 417800 | tf_op jit(solution)/shard_map/ppermute | solution.py:492
  26.7 11.8 %collective-permute-start.3 = (bf16[544,128]{1,0:T(8,128)(2,1)S(1)}, bf16[544,128]{1,0:T(8,128)(2,1)S(1)}, u32[]{:S(2)}, u32[]{:S(2)}) collective-permute-start(bf16[544,128]{1,0:T(8,128)(2,1)S(1)} %get-tuple-element.52), channel_id=1, source_target_pairs={{0,6},{2,4},{4,2},{6,0},{8,14},{10,12},{12,10},{14,8},{16,22},{18,... | collective-permute-start | bytes 417800 | tf_op jit(solution)/shard_map/ppermute | solution.py:492
  38.4 13.4 %copy-start.2 = (bf16[1,4,32,2240]{3,2,1,0:T(8,128)(2,1)S(1)}, bf16[1,4,32,2240]{3,2,1,0:T(8,128)(2,1)}, u32[]{:S(2)}) copy-start(bf16[1,4,32,2240]{3,2,1,0:T(8,128)(2,1)} %param.5) | copy-start | bytes 1720324
  38.4 13.4 %copy-start.3 = (bf16[1,4,32,2240]{3,2,1,0:T(8,128)(2,1)S(1)}, bf16[1,4,32,2240]{3,2,1,0:T(8,128)(2,1)}, u32[]{:S(2)}) copy-start(bf16[1,4,32,2240]{3,2,1,0:T(8,128)(2,1)} %param.8) | copy-start | bytes 1720324
  38.4 13.4 %copy-start.4 = (f32[3,3,2240]{2,1,0:T(4,128)S(1)}, f32[3,3,2240]{2,1,0:T(4,128)}, u32[]{:S(2)}) copy-start(f32[3,3,2240]{2,1,0:T(4,128)} %taps.1) | copy-start | bytes 241924
  39.2 35.8 %all-to-all-start = ((bf16[8,96,128]{2,1,0:T(8,128)(2,1)}), bf16[8,96,128]{2,1,0:T(8,128)(2,1)S(1)}, u32[]{:S(2)}, u32[]{:S(2)}) async-start(bf16[8,96,128]{2,1,0:T(8,128)(2,1)} %get-tuple-element.53), calls=%async_computation | async-start | bytes 393216 | tf_op jit(solution)/shard_map/all_to_all | solution.py:497
  54.1 4.8 %collective-permute-start.4 = (bf16[2,128,1280]{2,1,0:T(8,128)(2,1)S(1)}, bf16[2,128,1280]{2,1,0:T(8,128)(2,1)S(1)}, u32[]{:S(2)}, u32[]{:S(2)}) collective-permute-start(bf16[2,128,1280]{2,1,0:T(8,128)(2,1)S(1)} %get-tuple-element.56), channel_id=1, source_target_pairs={{0,1},{1,0},{2,3},{3,2},{4,5},{5,4},{6,7},{7,6},{8,9},{9,8},{10,11... | collective-permute-start | bytes 1966088 | tf_op jit(solution)/shard_map/ppermute | solution.py:488
  76.1 17.5 %copy-start.14 = (bf16[2,128,1280]{2,1,0:T(8,128)(2,1)S(1)}, bf16[2,128,1280]{2,1,0:T(8,128)(2,1)}, u32[]{:S(2)}) copy-start(bf16[2,128,1280]{2,1,0:T(8,128)(2,1)} %copy-done.13) | copy-start | bytes 1966084
  76.1 17.5 %copy-start.20 = (bf16[2,128,1280]{2,1,0:T(8,128)(2,1)S(1)}, bf16[2,128,1280]{2,1,0:T(8,128)(2,1)}, u32[]{:S(2)}) copy-start(bf16[2,128,1280]{2,1,0:T(8,128)(2,1)} %copy-done.18) | copy-start | bytes 1966084
  76.1 17.5 %copy-start.24 = (f32[3,3,1280]{2,1,0:T(4,128)S(1)}, f32[3,3,1280]{2,1,0:T(4,128)}, u32[]{:S(2)}) copy-start(f32[3,3,1280]{2,1,0:T(4,128)} %copy-done.23) | copy-start | bytes 138244
  78.6 19.3 %copy-start.11 = (f32[256,128]{1,0:T(8,128)}, f32[256,128]{1,0:T(8,128)S(1)}, u32[]{:S(2)}) copy-start(f32[256,128]{1,0:T(8,128)S(1)} %get-tuple-element.57.own) | copy-start | bytes 393220
  78.6 18.8 %collective-permute-start.5 = (bf16[256,128]{1,0:T(8,128)(2,1)S(1)}, bf16[256,128]{1,0:T(8,128)(2,1)S(1)}, u32[]{:S(2)}, u32[]{:S(2)}) collective-permute-start(bf16[256,128]{1,0:T(8,128)(2,1)S(1)} %get-tuple-element.58), channel_id=1, source_target_pairs={{0,2},{2,0},{4,6},{6,4},{8,10},{10,8},{12,14},{14,12},{16,18},{18,... | collective-permute-start | bytes 196616 | tf_op jit(solution)/shard_map/ppermute | solution.py:492
  91.2 6.3 %collective-permute-start.6 = (bf16[256,128]{1,0:T(8,128)(2,1)S(1)}, bf16[256,128]{1,0:T(8,128)(2,1)S(1)}, u32[]{:S(2)}, u32[]{:S(2)}) collective-permute-start(bf16[256,128]{1,0:T(8,128)(2,1)S(1)} %get-tuple-element.59), channel_id=1, source_target_pairs={{0,4},{2,6},{4,0},{6,2},{8,12},{10,14},{12,8},{14,10},{16,20},{18,... | collective-permute-start | bytes 196616 | tf_op jit(solution)/shard_map/ppermute | solution.py:492
  92.5 5.4 %collective-permute-start.7 = (bf16[256,128]{1,0:T(8,128)(2,1)S(1)}, bf16[256,128]{1,0:T(8,128)(2,1)S(1)}, u32[]{:S(2)}, u32[]{:S(2)}) collective-permute-start(bf16[256,128]{1,0:T(8,128)(2,1)S(1)} %get-tuple-element.60), channel_id=1, source_target_pairs={{0,6},{2,4},{4,2},{6,0},{8,14},{10,12},{12,10},{14,8},{16,22},{18,... | collective-permute-start | bytes 196616 | tf_op jit(solution)/shard_map/ppermute | solution.py:492
  97.9 34.6 %copy-start.10 = (f32[256,128]{1,0:T(8,128)S(1)}, f32[256,128]{1,0:T(8,128)}, u32[]{:S(2)}) copy-start(f32[256,128]{1,0:T(8,128)} %copy-done.9) | copy-start | bytes 393220
  132.9 14.0 %collective-permute-start.8 = (bf16[528,128]{1,0:T(8,128)(2,1)S(1)}, bf16[528,128]{1,0:T(8,128)(2,1)S(1)}, u32[]{:S(2)}, u32[]{:S(2)}) collective-permute-start(bf16[528,128]{1,0:T(8,128)(2,1)S(1)} %get-tuple-element.64), channel_id=1, source_target_pairs={{0,2},{2,0},{4,6},{6,4},{8,10},{10,8},{12,14},{14,12},{16,18},{18,... | collective-permute-start | bytes 405512 | tf_op jit(solution)/shard_map/ppermute | solution.py:492
  144.4 4.9 %collective-permute-start.9 = (bf16[528,128]{1,0:T(8,128)(2,1)S(1)}, bf16[528,128]{1,0:T(8,128)(2,1)S(1)}, u32[]{:S(2)}, u32[]{:S(2)}) collective-permute-start(bf16[528,128]{1,0:T(8,128)(2,1)S(1)} %get-tuple-element.65), channel_id=1, source_target_pairs={{0,4},{2,6},{4,0},{6,2},{8,12},{10,14},{12,8},{14,10},{16,20},{18,... | collective-permute-start | bytes 405512 | tf_op jit(solution)/shard_map/ppermute | solution.py:492
  145.3 9.9 %collective-permute-start.10 = (bf16[528,128]{1,0:T(8,128)(2,1)S(1)}, bf16[528,128]{1,0:T(8,128)(2,1)S(1)}, u32[]{:S(2)}, u32[]{:S(2)}) collective-permute-start(bf16[528,128]{1,0:T(8,128)(2,1)S(1)} %get-tuple-element.66), channel_id=1, source_target_pairs={{0,6},{2,4},{4,2},{6,0},{8,14},{10,12},{12,10},{14,8},{16,22},{18,... | collective-permute-start | bytes 405512 | tf_op jit(solution)/shard_map/ppermute | solution.py:492
  159.0 29.8 %all-to-all-start.2 = ((bf16[8,80,128]{2,1,0:T(8,128)(2,1)}), bf16[8,80,128]{2,1,0:T(8,128)(2,1)S(1)}, u32[]{:S(2)}, u32[]{:S(2)}) async-start(bf16[8,80,128]{2,1,0:T(8,128)(2,1)} %get-tuple-element.76), calls=%async_computation.2 | async-start | bytes 327680 | tf_op jit(solution)/shard_map/all_to_all | solution.py:497
  164.2 39.0 %collective-permute-start.11 = (bf16[2,128,1280]{2,1,0:T(8,128)(2,1)S(1)}, bf16[2,128,1280]{2,1,0:T(8,128)(2,1)S(1)}, u32[]{:S(2)}, u32[]{:S(2)}) collective-permute-start(bf16[2,128,1280]{2,1,0:T(8,128)(2,1)S(1)} %get-tuple-element.73), channel_id=1, source_target_pairs={{0,1},{1,0},{2,3},{3,2},{4,5},{5,4},{6,7},{7,6},{8,9},{9,8},{10,11... | collective-permute-start | bytes 1966088 | tf_op jit(solution)/shard_map/ppermute | solution.py:488
  166.7 46.5 %collective-permute-start.19 = (f32[128,1280]{1,0:T(8,128)S(1)}, f32[128,1280]{1,0:T(8,128)S(1)}, u32[]{:S(2)}, u32[]{:S(2)}) collective-permute-start(f32[128,1280]{1,0:T(8,128)S(1)} %get-tuple-element.83), channel_id=1, source_target_pairs={{0,1},{1,0},{2,3},{3,2},{4,5},{5,4},{6,7},{7,6},{8,9},{9,8},{10,11... | collective-permute-start | bytes 1966088 | tf_op jit(solution)/shard_map/ppermute | solution.py:488
  191.3 20.3 %copy-start.17 = (bf16[2,128,1280]{2,1,0:T(8,128)(2,1)S(1)}, bf16[2,128,1280]{2,1,0:T(8,128)(2,1)}, u32[]{:S(2)}) copy-start(bf16[2,128,1280]{2,1,0:T(8,128)(2,1)} %copy-done.16) | copy-start | bytes 1966084
  191.5 15.0 %collective-permute-start.12 = (bf16[352,128]{1,0:T(8,128)(2,1)S(1)}, bf16[352,128]{1,0:T(8,128)(2,1)S(1)}, u32[]{:S(2)}, u32[]{:S(2)}) collective-permute-start(bf16[352,128]{1,0:T(8,128)(2,1)S(1)} %get-tuple-element.79), channel_id=1, source_target_pairs={{0,2},{2,0},{4,6},{6,4},{8,10},{10,8},{12,14},{14,12},{16,18},{18,... | collective-permute-start | bytes 270344 | tf_op jit(solution)/shard_map/ppermute | solution.py:492
  197.1 9.8 %collective-permute-start.13 = (bf16[352,128]{1,0:T(8,128)(2,1)S(1)}, bf16[352,128]{1,0:T(8,128)(2,1)S(1)}, u32[]{:S(2)}, u32[]{:S(2)}) collective-permute-start(bf16[352,128]{1,0:T(8,128)(2,1)S(1)} %get-tuple-element.80), channel_id=1, source_target_pairs={{0,4},{2,6},{4,0},{6,2},{8,12},{10,14},{12,8},{14,10},{16,20},{18,... | collective-permute-start | bytes 270344 | tf_op jit(solution)/shard_map/ppermute | solution.py:492
  202.2 9.4 %collective-permute-start.14 = (bf16[352,128]{1,0:T(8,128)(2,1)S(1)}, bf16[352,128]{1,0:T(8,128)(2,1)S(1)}, u32[]{:S(2)}, u32[]{:S(2)}) collective-permute-start(bf16[352,128]{1,0:T(8,128)(2,1)S(1)} %get-tuple-element.81), channel_id=1, source_target_pairs={{0,6},{2,4},{4,2},{6,0},{8,14},{10,12},{12,10},{14,8},{16,22},{18,... | collective-permute-start | bytes 270344 | tf_op jit(solution)/shard_map/ppermute | solution.py:492
  203.2 9.9 %collective-permute-start.15 = (bf16[352,128]{1,0:T(8,128)(2,1)S(1)}, bf16[352,128]{1,0:T(8,128)(2,1)S(1)}, u32[]{:S(2)}, u32[]{:S(2)}) collective-permute-start(bf16[352,128]{1,0:T(8,128)(2,1)S(1)} %get-tuple-element.78.g0), channel_id=1, source_target_pairs={{0,1},{1,0},{2,3},{3,2},{4,5},{5,4},{6,7},{7,6},{8,9},{9,8},{10,11... | collective-permute-start | bytes 270344 | tf_op jit(solution)/shard_map/ppermute | solution.py:488
  206.5 6.7 %collective-permute-start.16 = (bf16[352,128]{1,0:T(8,128)(2,1)S(1)}, bf16[352,128]{1,0:T(8,128)(2,1)S(1)}, u32[]{:S(2)}, u32[]{:S(2)}) collective-permute-start(bf16[352,128]{1,0:T(8,128)(2,1)S(1)} %collective-permute-done.12.g1), channel_id=1, source_target_pairs={{0,1},{1,0},{2,3},{3,2},{4,5},{5,4},{6,7},{7,6},{8,9},{9,8},{10,11... | collective-permute-start | bytes 270344 | tf_op jit(solution)/shard_map/ppermute | solution.py:488
  206.8 6.3 %collective-permute-start.17 = (bf16[352,128]{1,0:T(8,128)(2,1)S(1)}, bf16[352,128]{1,0:T(8,128)(2,1)S(1)}, u32[]{:S(2)}, u32[]{:S(2)}) collective-permute-start(bf16[352,128]{1,0:T(8,128)(2,1)S(1)} %collective-permute-done.13.g2), channel_id=1, source_target_pairs={{0,1},{1,0},{2,3},{3,2},{4,5},{5,4},{6,7},{7,6},{8,9},{9,8},{10,11... | collective-permute-start | bytes 270344 | tf_op jit(solution)/shard_map/ppermute | solution.py:488
  211.6 1.6 collective-permute-start.18
  (15 other events, 26.2 us)

commit v3 on v2

--- a/solution.py
+++ b/solution.py
@@ -20,15 +20,15 @@
 VMEM_LIMIT = 16 << 20
 
 
-def call(kernel, outs, *args, scratch=(), us=1):
+def call(kernel, outs, *args, scratch=(), us=1, space=pltpu.VMEM):
     return pl.pallas_call(
         kernel,
         out_shape=[jax.ShapeDtypeStruct(s, d) for s, d in outs],
-        in_specs=[pl.BlockSpec(memory_space=pltpu.VMEM)] * len(args),
+        in_specs=[pl.BlockSpec(memory_space=space)] * len(args),
         out_specs=[pl.BlockSpec(memory_space=pltpu.VMEM)] * len(outs),
-        scratch_shapes=[pltpu.VMEM(s, d) for s, d in scratch],
+        scratch_shapes=[pltpu.VMEM(*s) if isinstance(s, tuple) else s for s in scratch],
         interpret=INTERPRET,
-        cost_estimate=pl.CostEstimate(flops=us * 10**9, bytes_accessed=10**6, transcendentals=0),
+        cost_estimate=pl.CostEstimate(flops=us * 6 * 10**9, bytes_accessed=10**6, transcendentals=0),
         compiler_params=pltpu.CompilerParams(vmem_limit_bytes=VMEM_LIMIT),
     )(*args)
 
@@ -149,8 +149,13 @@
             send[j, :, col(i)] = lax.select(first, b, a).astype(BF)
 
 
-def spread_kv_kernel(k, v, keep, send):
-    spread((k, v), (True, False), keep, send)
+def spread_kv_kernel(k, v, keep, send, buf, sems):
+    copies = [pltpu.make_async_copy(x, buf.at[j], sems.at[j]) for j, x in enumerate((k, v))]
+    for c in copies:
+        c.start()
+    for j, c in enumerate(copies):
+        c.wait()
+        spread((buf.at[j],), (j == 0,), keep.at[j : j + 1], send.at[j : j + 1])
 
 
 def spread_qg_kernel(q, g, taps, after, keep, send, taps_out):
@@ -215,44 +220,95 @@
     return pl.ds(pl.multiple_of((p ^ k) * n, n), n)
 
 
-def partial_kernel(keep, recv, own, ksum, a1, a2, a3, state):
+def put_rows(ref, *arrays):
+    at = 0
+    for x in arrays:
+        ref[at : at + x.shape[0], :] = x
+        at += x.shape[0]
+    if at < ref.shape[0]:
+        ref[at:, :] = jnp.zeros((ref.shape[0] - at, LN), F32)
+
+
+def split(x):
+    hi = x.astype(BF).astype(F32)
+    return hi, x - hi
+
+
+def vectors(block):
+    x = block.astype(F32)
+    return x[0:HC] + x[HC : 2 * HC], x[2 * HC : 3 * HC]
+
+
+def partial_kernel(keep, recv, own, ksum, mean, a1, a2, a3, state, rows):
     p = place()[1]
-    ksum[...] = jnp.zeros_like(ksum)
-    mats = []
+    mats, sums, means = [], [], []
     for i in range(HC):
-        keys = both(keep, recv, 0, i)
-        mats.append(mm(keys, both(keep, recv, 1, i), TN)[:HD])
-        ksum[i : i + 1, :] = jnp.sum(keys.astype(F32), axis=0, keepdims=True)
+        keys, v = both(keep, recv, 0, i), both(keep, recv, 1, i).astype(F32)
+        mid = (jnp.sum(v, axis=0, keepdims=True) * (1.0 / v.shape[0])).astype(BF).astype(F32)
+        hi, lo = halves(v - mid)
+        x = mm(keys, jnp.concatenate([hi, lo], axis=1), TN)[:HD]
+        mats.append(x[:, :LN] + x[:, LN:])
+        sums.append(jnp.sum(keys.astype(F32), axis=0, keepdims=True))
+        means.append(mid)
     pack(state, mats)
     n = ROWS // NEAR
     own[...] = state[rows_at(p, 0, n), :]
-    khi, klo = halves(ksum[...])
+    put_rows(ksum, *sums)
+    put_rows(mean, *means)
+    put_rows(rows, *split(ksum[0:HC, :]), mean[0:HC, :])
+    block = rows[...].astype(BF)
     for k, ref in enumerate((a1, a2, a3), 1):
-        hi, lo = halves(state[rows_at(p, k, n), :])
-        ref[0:n, :] = hi
-        ref[n : 2 * n, :] = lo
-        ref[2 * n : 2 * n + 16, :] = khi
-        ref[2 * n + 16 : 2 * n + 32, :] = klo
-
-
-def block_kernel(own, ksum, a1, a2, a3, pay, kpre):
+        ref[0:n, :] = state[rows_at(p, k, n), :].astype(BF)
+        ref[n:, :] = block
+
+
+def products(sums, means, i):
+    free = jnp.zeros((-len(sums) % 8, LN), F32)
+    a = jnp.concatenate([x[i : i + 1] for x in sums] + [free], axis=0)
+    b = jnp.concatenate([x[i : i + 1] for x in means] + [free], axis=0)
+    return lax.dot_general(
+        a, b, (TN, ((), ())), precision=lax.Precision.HIGHEST, preferred_element_type=F32
+    )[:HD]
+
+
+def block_kernel(own, ksum, mean, a1, a2, a3, pay, kpre, state, rows):
     p = place()[1]
     n = ROWS // NEAR
-    total, ktot, kp = own[...], ksum[...], ksum[...]
+    total, kp = own[...], ksum[0:HC, :]
+    sums, means = [ksum[0:HC, :]], [mean[0:HC, :]]
     for k, ref in enumerate((a1, a2, a3), 1):
-        total = total + joined(ref[0:n, :], ref[n : 2 * n, :])
-        ks = joined(ref[2 * n : 2 * n + 16, :], ref[2 * n + 16 : 2 * n + 32, :])
-        ktot = ktot + ks
+        total = total + ref[0:n, :].astype(F32)
+        ks, mid = vectors(ref[n:, :])
+        sums.append(ks)
+        means.append(mid)
         kp = kp + flag((p ^ k) <= p) * ks
     kpre[...] = kp
-    khi, klo = halves(ktot)
+    mid = (sum(means) * (1.0 / NEAR)).astype(BF).astype(F32)
+    pack(state, [products(sums, [x - mid for x in means], i) for i in range(HC)])
+    total = total + state[rows_at(p, 0, n), :]
+    put_rows(rows, *split(sum(sums)), mid)
+    block = rows[...].astype(BF)
     m = n // pay.shape[0]
     for b in range(pay.shape[0]):
-        hi, lo = halves(total[m * b : m * (b + 1)])
-        pay[b, 0:m, :] = hi
-        pay[b, m : 2 * m, :] = lo
-        pay[b, 2 * m : 2 * m + 16, :] = khi
-        pay[b, 2 * m + 16 : 2 * m + 32, :] = klo
+        pay[b, 0:m, :] = total[m * b : m * (b + 1)].astype(BF)
+        pay[b, m:, :] = block
+
+
+def rank_kernel(got, ksum, mean, a1, a2, a3, rank):
+    _, p, mine = place()
+    n = ROWS // NEAR
+    m = n // got.shape[0]
+    sums, means = [ksum[0:HC, :]], [mean[0:HC, :]]
+    for k, ref in enumerate((a1, a2, a3), 1):
+        ks, mid = vectors(ref[n:, :])
+        sums.append(flag((p ^ k) <= p) * ks)
+        means.append(mid)
+    for b in range(got.shape[0]):
+        ks, mid = vectors(got[b, m:, :])
+        sums.append(flag(b < mine) * ks)
+        means.append(mid)
+    for i in range(HC):
+        rank[HD * i : HD * (i + 1), :] = products(sums, means, i)
 
 
 def reciprocal_of(q, kt, i):
@@ -269,11 +325,9 @@
     m = n // nb
     run, key_total = jnp.zeros((m, LN), F32), kpre[...]
     for b in range(nb):
-        hi, lo = halves(run)
-        down[b, 0:m, :] = hi
-        down[b, m : 2 * m, :] = lo
-        run = run + joined(got[b, 0:m, :], got[b, m : 2 * m, :])
-        ks = joined(got[b, 2 * m : 2 * m + 16, :], got[b, 2 * m + 16 : 2 * m + 32, :])
+        down[b] = run.astype(BF)
+        run = run + got[b, 0:m, :].astype(F32)
+        ks, _ = vectors(got[b, m:, :])
         key_total = key_total + flag(b < mine) * ks
     kt[...] = key_total
     mats = []
@@ -289,45 +343,35 @@
         ref[...] = state[rows_at(p, k, n), :].astype(BF)
 
 
-def back_block_kernel(own, c1, c2, c3, down, taps, pay):
+def back_block_kernel(own, c1, c2, c3, down, taps, pay, rows):
     nb = pay.shape[0]
     m = ROWS // NEAR // nb
     total = own[...]
     for ref in (c1, c2, c3):
         total = total + ref[...].astype(F32)
     for b in range(nb):
-        pay[b, 0 : 2 * m, :] = down[b]
-        pay[b, 2 * m : 3 * m, :] = total[m * b : m * (b + 1)].astype(BF)
-        hi, lo = halves(taps[16 * b : 16 * (b + 1), :])
-        pay[b, 3 * m : 3 * m + 16, :] = hi
-        pay[b, 3 * m + 16 : 3 * m + 32, :] = lo
-
-
-def four_rows(x):
-    hi = x.astype(BF).astype(F32)
-    return jnp.concatenate([hi, x - hi, jnp.zeros((8, LN), F32)], axis=0).astype(BF)
-
-
-def of_four(x):
-    x = x.astype(F32)
-    return x[0:4] + x[4:8]
-
-
-def prefix_kernel(got, own, a1, a2, a3, s_own, e1, e2, e3, taps_own, back, taps):
+        pay[b, 0:m, :] = down[b]
+        pay[b, m : 2 * m, :] = total[m * b : m * (b + 1)].astype(BF)
+        put_rows(rows, *split(taps[12 * b : 12 * (b + 1), :]))
+        pay[b, 2 * m :, :] = rows[...].astype(BF)
+
+
+def prefix_kernel(got, own, a1, a2, a3, s_own, e1, e2, e3, taps_own, back, taps, rows):
     p = place()[1]
     nb = got.shape[0]
     n = ROWS // NEAR
     m = n // nb
-    base = jnp.concatenate([joined(got[b, 0:m, :], got[b, m : 2 * m, :]) for b in range(nb)], axis=0)
+    base = jnp.concatenate([got[b, 0:m, :].astype(F32) for b in range(nb)], axis=0)
     run = jnp.zeros((m, LN), F32)
-    t = jnp.zeros((16, LN), F32)
+    t = jnp.zeros((12, LN), F32)
     for b in reversed(range(nb)):
         back[b] = run.astype(BF)
-        run = run + got[b, 2 * m : 3 * m, :].astype(F32)
-        t = t + joined(got[b, 3 * m : 3 * m + 16, :], got[b, 3 * m + 16 : 3 * m + 32, :])
+        run = run + got[b, m : 2 * m, :].astype(F32)
+        x = got[b, 2 * m :, :].astype(F32)
+        t = t + (x[0:12] + x[12:24])
     for j in range(NEAR):
-        taps[j] = t[4 * j : 4 * (j + 1)]
-    parts = [own[...]] + [joined(r[0:n, :], r[n : 2 * n, :]) for r in (a1, a2, a3)]
+        taps[j] = t[3 * j : 3 * (j + 1)]
+    parts = [own[...]] + [r[0:n, :].astype(F32) for r in (a1, a2, a3)]
     for k, ref in enumerate((s_own, e1, e2, e3)):
         x = base
         for j in range(NEAR):
@@ -335,15 +379,14 @@
         if k == 0:
             ref[...] = x
         else:
-            hi, lo = halves(x)
-            ref[0:n, :] = hi
-            ref[n : 2 * n, :] = lo
-            ref[2 * n : 2 * n + 16, :] = four_rows(taps[p ^ k])
+            ref[0:n, :] = x.astype(BF)
+            put_rows(rows, *split(taps[p ^ k]))
+            ref[n:, :] = rows[...].astype(BF)
     taps_own[...] = taps[p]
 
 
 def attend_kernel(
-    e1, e2, e3, s_own, kt, keep, recv, local, taps_own, back, mine, other, pay, gks_out, state, gks
+    e1, e2, e3, s_own, rank, kt, keep, recv, local, taps_own, back, mine, other, pay, gks, state, rows
 ):
     p = place()[1]
     nb = pay.shape[0]
@@ -353,15 +396,15 @@
     state[rows_at(p, 0, n), :] = s_own[...]
     taps = taps_own[...]
     for k, ref in enumerate((e1, e2, e3), 1):
-        state[rows_at(p, k, n), :] = joined(ref[0:n, :], ref[n : 2 * n, :])
-        taps = taps + of_four(ref[2 * n : 2 * n + 16, :])
+        state[rows_at(p, k, n), :] = ref[0:n, :].astype(F32)
+        x = ref[n:, :].astype(F32)
+        taps = taps + (x[0:3] + x[3:6])
     mats = unpack(state)
     key_total = kt[...]
-    gks[...] = jnp.zeros_like(gks)
     ones = jnp.ones((2 * LN, LN), BF)
     for i in range(HC):
         q, g = both(keep, recv, 0, i), both(keep, recv, 1, i)
-        hi, lo = halves(pad_rows(mats[i]))
+        hi, lo = halves(pad_rows(mats[i] + rank[HD * i : HD * (i + 1), :]))
         recip = reciprocal_of(q, key_total, i)
         out = mm(jnp.concatenate([q, q], axis=1), jnp.concatenate([hi, lo], axis=0), NN) * recip
         x = (out + local[:, col(i)]).astype(BF)
@@ -375,53 +418,48 @@
         mine[1, :, col(i)] = x[:half]
         other[1, :, col(i)] = x[half:]
         gks[i : i + 1, :] = jnp.sum(gden * qf, axis=0, keepdims=True)
-    gks_out[...] = gks[...]
-    khi, klo = halves(gks[...])
-    four = four_rows(taps)
+    put_rows(rows, *split(gks[...]), *split(taps))
+    block = rows[...].astype(BF)
     for b in range(nb):
         pay[b, 0:m, :] = back[b]
-        pay[b, m : m + 16, :] = khi
-        pay[b, m + 16 : m + 32, :] = klo
-        pay[b, m + 32 : m + 48, :] = four
-
-
-def suffix_kernel(got, own, c1, c2, c3, gks, g0, g1, g2, g3):
+        pay[b, m:, :] = block
+
+
+def suffix_kernel(got, own, c1, c2, c3, gks, g0, g1, g2, g3, rows):
     _, p, mine = place()
     nb = got.shape[0]
     n = ROWS // NEAR
     m = n // nb
     base = jnp.concatenate([got[b, 0:m, :].astype(F32) for b in range(nb)], axis=0)
-    later = jnp.zeros((16, LN), F32)
+    later = jnp.zeros((HC, LN), F32)
+    taps = []
     for b in range(nb):
-        ks = joined(got[b, m : m + 16, :], got[b, m + 16 : m + 32, :])
-        later = later + flag(b > mine) * ks
-    taps = jnp.concatenate([of_four(got[b, m + 32 : m + 48, :]) for b in range(nb)], axis=0)
-    thi, tlo = halves(taps)
+        x = got[b, m:, :].astype(F32)
+        later = later + flag(b > mine) * (x[0:HC] + x[HC : 2 * HC])
+        taps.append(x[2 * HC : 2 * HC + 3] + x[2 * HC + 3 : 2 * HC + 6])
+    his, los = zip(*(split(x) for x in taps))
     parts = [own[...]] + [r[...].astype(F32) for r in (c1, c2, c3)]
-    nt = taps.shape[0]
     for k, ref in enumerate((g0, g1, g2, g3)):
         x = base
         for j in range(NEAR):
             x = x + flag((p ^ j) >= (p ^ k)) * parts[j]
         ref[0:n, :] = x.astype(BF)
-        hi, lo = halves(later + flag(p >= (p ^ k)) * gks[...])
-        ref[n : n + 16, :] = hi
-        ref[n + 16 : n + 32, :] = lo
-        ref[n + 32 : n + 32 + nt, :] = thi
-        ref[n + 32 + nt : n + 32 + 2 * nt, :] = tlo
+        put_rows(rows, *split(later + flag(p >= (p ^ k)) * gks[...]), *his, *los)
+        ref[n:, :] = rows[...].astype(BF)
 
 
 def assembled(refs, state, taps):
     p = place()[1]
     n = ROWS // NEAR
-    nt = (refs[0].shape[0] - n - 32) // 2
-    total = jnp.zeros((16, LN), F32)
+    nb = taps.shape[0]
+    total = jnp.zeros((HC, LN), F32)
     for k, ref in enumerate(refs):
         state[rows_at(p, k, n), :] = ref[0:n, :].astype(F32)
-        total = total + joined(ref[n : n + 16, :], ref[n + 16 : n + 32, :])
-        part = joined(ref[n + 32 : n + 32 + nt, :], ref[n + 32 + nt : n + 32 + 2 * nt, :])
-        for b in range(nt // 4):
-            taps[b, p ^ k] = part[4 * b : 4 * (b + 1)]
+        x = ref[n:, :].astype(F32)
+        total = total + (x[0:HC] + x[HC : 2 * HC])
+        for b in range(nb):
+            at = 2 * HC + 3 * b
+            taps[b, p ^ k] = x[at : at + 3] + x[at + 3 * nb : at + 3 * nb + 3]
     return unpack(state), total
 
 
@@ -454,7 +492,7 @@
                 lines = []
                 for b in range(3):
                     r = 9 * i + 3 * a + b
-                    lines.append(scratch[r // 16, (r % 16) // 4, r % 4 : r % 4 + 1, :])
+                    lines.append(scratch[r // 12, (r % 12) // 3, r % 3 : r % 3 + 1, :])
                 heads.append(jnp.concatenate(lines, axis=0))
             rows.append(heads)
         gather_heads(first, rows[0], rows[1], taps.at[a])
@@ -502,12 +540,20 @@
     pair = ((2, t, WC), BF)
     share = ((n, LN), F32)
     small = ((16, LN), F32)
+    row = ((HC, LN), F32)
     state = ((ROWS, LN), F32)
 
-    keep_kv, send_kv = call(spread_kv_kernel, [pair, pair], k, v, us=3)
+    keep_kv, send_kv = call(
+        spread_kv_kernel,
+        [pair, pair],
+        k, v, us=1, space=pltpu.HBM,
+        scratch=[((2, t, width), BF), pltpu.SemaphoreType.DMA((2,))],
+    )
     recv_kv = over(send_kv)
-    own_b, ksum, *out = call(
-        partial_kernel, [share, small] + [((2 * n + 32, LN), BF)] * 3, keep_kv, recv_kv, scratch=[state], us=3
+    own_b, ksum, mean, *out = call(
+        partial_kernel,
+        [share, small, small] + [((n + 32, LN), BF)] * 3,
+        keep_kv, recv_kv, scratch=[state, ((32, LN), F32)], us=1,
     )
     got_a = near(out)
     keep_qg, send_qg, taps = call(
@@ -516,41 +562,56 @@
     recv_qg = over(send_qg)
     local, gc_mine, gc_other, taps_part = call(
         conv_kernel,
-        [((2 * t, WC), F32), ((t, WC), F32), ((t, WC), F32), ((LN, LN), F32)],
+        [((2 * t, WC), F32), ((t, WC), F32), ((t, WC), F32), ((96, LN), F32)],
         keep_kv, recv_kv, keep_qg, recv_qg, taps, us=6,
     )
     gc_other = over(gc_other)
-    pay, kpre = call(block_kernel, [((nb, 2 * m + 32, LN), BF), small], own_b, ksum, *got_a)
+    pay, kpre = call(
+        block_kernel,
+        [((nb, m + 32, LN), BF), row],
+        own_b, ksum, mean, *got_a, scratch=[state, ((32, LN), F32)],
+    )
     got = far(pay)
     down, kt, own_d, *out = call(
         turn_kernel,
-        [((nb, 2 * m, LN), BF), small, share] + [((n, LN), BF)] * 3,
+        [((nb, m, LN), BF), row, share] + [((n, LN), BF)] * 3,
         got, kpre, keep_qg, recv_qg, scratch=[state], us=4,
     )
     got_c = near(out)
-    (pay,) = call(back_block_kernel, [((nb, 3 * m + 32, LN), BF)], own_d, *got_c, down, taps_part)
+    (pay,) = call(
+        back_block_kernel,
+        [((nb, 2 * m + 24, LN), BF)],
+        own_d, *got_c, down, taps_part, scratch=[((24, LN), F32)],
+    )
+    (rank,) = call(rank_kernel, [((HC * HD, LN), F32)], got, ksum, mean, *got_a, us=2)
     got = far(pay)
     s_own, e1, e2, e3, taps_own, back = call(
         prefix_kernel,
-        [share] + [((2 * n + 16, LN), BF)] * 3 + [((4, LN), F32), ((nb, m, LN), BF)],
-        got, own_b, *got_a, scratch=[((NEAR, 4, LN), F32)],
+        [share] + [((n + 16, LN), BF)] * 3 + [((3, LN), F32), ((nb, m, LN), BF)],
+        got, own_b, *got_a, scratch=[((NEAR, 3, LN), F32), ((16, LN), F32)],
     )
     got_e = near((e1, e2, e3))
     mine, other, pay, gks = call(
         attend_kernel,
-        [pair, pair, ((nb, m + 48, LN), BF), small],
-        *got_e, s_own, kt, keep_qg, recv_qg, local, taps_own, back, scratch=[state, small], us=4,
+        [pair, pair, ((nb, m + 32, LN), BF), row],
+        *got_e, s_own, rank, kt, keep_qg, recv_qg, local, taps_own, back,
+        scratch=[state, ((32, LN), F32)], us=4,
     )
     got = far(pay)
     whole = ((t, width), BF)
     attended, query_grad = call(merge_kernel, [whole, whole], mine, over(other), us=3)
-    g0, *out = call(suffix_kernel, [((n + 32 + 8 * nb, LN), BF)] * 4, got, own_d, *got_c, gks)
+    tail = -(-(2 * HC + 6 * nb) // 8) * 8
+    g0, *out = call(
+        suffix_kernel,
+        [((n + tail, LN), BF)] * 4,
+        got, own_d, *got_c, gks, scratch=[((tail, LN), F32)],
+    )
     gs = [g0] + near(out)
     key_grad, value_grad, taps_grad = call(
         finish_kernel,
         [whole, whole, (conv_taps.shape, F32)],
         *gs, *[over(x) for x in gs], keep_kv, send_kv, gc_mine, gc_other,
-        scratch=[state] + [((nb, NEAR, 4, LN), F32)] * 2, us=5,
+        scratch=[state] + [((nb, NEAR, 3, LN), F32)] * 2, us=5,
     )
     return (
         attended.reshape(shape),

time: 216 us -> 188 us (0.87)
  starting transfers between devices: 96.5 us -> 77.5 us
  waiting for transfers between devices: 58.9 us -> 51.8 us
  local copies, waits for them, and re-layouts: 10.2 us -> 4.94 us
    ppermute x12, starting transfers between devices: 44.1 us -> 23.6 us  [near(): lax.ppermute(a, 'tm', [(i, i ^ k) for i in range(frames)])]
    ppermute x12, waiting for transfers between devices: 17.5 us -> 7.24 us  [near(): lax.ppermute(a, 'tm', [(i, i ^ k) for i in range(frames)])]
    unnamed x50 -> x28, local copies, waits for them, and re-layouts: 10.2 us -> 4.94 us
    all_to_all x2, waiting for transfers between devices: 37.9 us -> 41.1 us  [far(): return lax.all_to_all(x, 'tm', 0, 0, axis_index_groups=across, tiled=True)]
    pallas_call x12 -> x13, Pallas kernels: 15.8 us -> 17.8 us  [call(): pl.pallas_call(kernel, out_shape=[jax.ShapeDtypeStruct(s, d) for s, d in...]
  transfers between devices with their start and end apart: 22 -> 22, of which waited for: 10 -> 8; matrix products, arithmetic and copies ran while one was open for 0% -> 0% of each run, Pallas kernels for 3% -> 3%
where the time goes in v3:
time: 188 us
  starting transfers between devices  77.5 us (41%)
  waiting for transfers between devices  51.8 us (28%)
  blocking collectives  34.8 us (19%)
  Pallas kernels  17.8 us (9%)
  local copies, waits for them, and re-layouts  4.94 us (3%)
    all_to_all x2, waiting for transfers between devices, far(): return lax.all_to_all(x, 'tm', 0, 0, axis_index_groups=across, tiled=True)  41.1 us
    all_to_all x1, blocking collectives, far(): return lax.all_to_all(x, 'tm', 0, 0, axis_index_groups=across, tiled=True)  34.8 us
    ppermute x8, starting transfers between devices, over(): return lax.ppermute(x, 'space', [(0, 1), (1, 0)])  34.5 us
    ppermute x12, starting transfers between devices, near(): lax.ppermute(a, 'tm', [(i, i ^ k) for i in range(frames)])  23.6 us
    all_to_all x2, starting transfers between devices, far(): return lax.all_to_all(x, 'tm', 0, 0, axis_index_groups=across, tiled=True)  19.3 us
    pallas_call x13, Pallas kernels, call(): pl.pallas_call(kernel, out_shape=[jax.ShapeDtypeStruct(s, d) for s, d in...  17.8 us
    ppermute x12, waiting for transfers between devices, near(): lax.ppermute(a, 'tm', [(i, i ^ k) for i in range(frames)])  7.24 us
    unnamed x28, local copies, waits for them, and re-layouts  4.94 us
  transfers between devices with their start and end apart: 22, of which 8 were waited for; matrix products, arithmetic and copies ran while one was open for 0% of the time, Pallas kernels for 3%

profile of v3, /device:TPU:37, one launch (start us, length us, event | category | flops | bytes accessed | tf_op | source)
XLA Modules:
  0.0 187.6 jit_solution(12136822504769885853)
XLA Ops:
  0.6 1.1 copy-done.2
  1.7 1.1 copy-done.3
  2.8 1.0 shard_map.92
  3.8 20.5 %collective-permute-start = (bf16[2,128,1280]{2,1,0:T(8,128)(2,1)S(1)}, bf16[2,128,1280]{2,1,0:T(8,128)(2,1)S(1)}, u32[]{:S(2)}, u32[]{:S(2)}) collective-permute-start(bf16[2,128,1280]{2,1,0:T(8,128)(2,1)S(1)} %get-tuple-element.48.send), channel_id=1, source_target_pairs={{0,1},{1,0},{2,3},{3,2},{4,5},{5,4},{6,7},{7,6},{8,9},{9,8},{10,11... | collective-permute-start | bytes 1966088 | tf_op jit(solution)/shard_map/ppermute | solution.py:526
  24.4 1.7 collective-permute-done.recv.recv_v
  27.2 3.4 %collective-permute-start.3 = (bf16[288,128]{1,0:T(8,128)(2,1)S(1)}, bf16[288,128]{1,0:T(8,128)(2,1)S(1)}, u32[]{:S(2)}, u32[]{:S(2)}) collective-permute-start(bf16[288,128]{1,0:T(8,128)(2,1)S(1)} %get-tuple-element.54), channel_id=1, source_target_pairs={{0,6},{2,4},{4,2},{6,0},{8,14},{10,12},{12,10},{14,8},{16,22},{18,... | collective-permute-start | bytes 221192 | tf_op jit(solution)/shard_map/ppermute | solution.py:530
  31.4 2.3 %collective-permute-done.3.a3 = bf16[288,128]{1,0:T(8,128)(2,1)S(1)} collective-permute-done((bf16[288,128]{1,0:T(8,128)(2,1)S(1)}, bf16[288,128]{1,0:T(8,128)(2,1)S(1)}, u32[]{:S(2)}, u32[]{:S(2)}) %collective-permute-start.3) | collective-permute-done | bytes 73760 | tf_op jit(solution)/shard_map/ppermute | solution.py:530
  33.7 1.5 shard_map.94
  35.2 13.3 %all-to-all-start = ((bf16[8,64,128]{2,1,0:T(8,128)(2,1)}), bf16[8,64,128]{2,1,0:T(8,128)(2,1)S(1)}, u32[]{:S(2)}, u32[]{:S(2)}) async-start(bf16[8,64,128]{2,1,0:T(8,128)(2,1)} %get-tuple-element.55), calls=%async_computation | async-start | bytes 262144 | tf_op jit(solution)/shard_map/all_to_all | solution.py:535
  50.3 3.0 %collective-permute-start.4 = (bf16[2,128,1280]{2,1,0:T(8,128)(2,1)S(1)}, bf16[2,128,1280]{2,1,0:T(8,128)(2,1)S(1)}, u32[]{:S(2)}, u32[]{:S(2)}) collective-permute-start(bf16[2,128,1280]{2,1,0:T(8,128)(2,1)S(1)} %get-tuple-element.58), channel_id=1, source_target_pairs={{0,1},{1,0},{2,3},{3,2},{4,5},{5,4},{6,7},{7,6},{8,9},{9,8},{10,11... | collective-permute-start | bytes 1966088 | tf_op jit(solution)/shard_map/ppermute | solution.py:526
  53.2 1.7 collective-permute-done.4.recv.recv_g
  54.9 17.8 %all-to-all-done.got = bf16[8,64,128]{2,1,0:T(8,128)(2,1)S(1)} async-done(((bf16[8,64,128]{2,1,0:T(8,128)(2,1)}), bf16[8,64,128]{2,1,0:T(8,128)(2,1)S(1)}, u32[]{:S(2)}, u32[]{:S(2)}) %all-to-all-start) | async-done | bytes 131104 | tf_op jit(solution)/shard_map/all_to_all | solution.py:535
  72.7 1.1 copy-done.10
  73.8 2.5 %shard_map.96 = (bf16[8,32,128]{2,1,0:T(8,128)(2,1)S(1)}, f32[10,128]{1,0:T(8,128)S(1)}, f32[256,128]{1,0:T(8,128)S(1)}, bf16[256,128]{1,0:T(8,128)(2,1)S(1)}, b...) custom-call(bf16[8,64,128]{2,1,0:T(8,128)(2,1)S(1)} %all-to-all-done.got, ...), custom_call_target="tpu_custom_call" | custom-call | flops 24000000000 | bytes 1000000 | tf_op jit(solution)/shard_map/pallas_call | solution.py:24
  76.3 4.9 %collective-permute-start.5 = (bf16[256,128]{1,0:T(8,128)(2,1)S(1)}, bf16[256,128]{1,0:T(8,128)(2,1)S(1)}, u32[]{:S(2)}, u32[]{:S(2)}) collective-permute-start(bf16[256,128]{1,0:T(8,128)(2,1)S(1)} %get-tuple-element.60), channel_id=1, source_target_pairs={{0,2},{2,0},{4,6},{6,4},{8,10},{10,8},{12,14},{14,12},{16,18},{18,... | collective-permute-start | bytes 196616 | tf_op jit(solution)/shard_map/ppermute | solution.py:530
  81.2 1.5 collective-permute-start.6
  82.8 1.0 collective-permute-start.7
  83.8 3.0 %shard_map.97 = (f32[256,1280]{1,0:T(8,128)S(1)}, f32[128,1280]{1,0:T(8,128)S(1)}, f32[128,1280]{1,0:T(8,128)S(1)}, f32[96,128]{1,0:T(8,128)S(1)}) custom-call(bf16[2,128,1280]{2,1,0:T(8,128)(2,1)S(1)} %get-tuple-element.47.keep.keep_v, bf16[2,128,1280]{2,1,0:T(8,128)(2,1)S(1)} %collective-permute-done.recv.recv_v, bf16[2,128,1280]{2,1,0:T(8,128)(2,1)S(1)} %copy-done.10, ...), custom_call_target="tpu_custom_call" | custom-call | flops 35999997952 | bytes 1000000 | tf_op jit(solution)/shard_map/pallas_call | solution.py:24
  87.8 34.8 %all_to_all.15.got = bf16[8,88,128]{2,1,0:T(8,128)(2,1)S(1)} all-to-all(bf16[8,88,128]{2,1,0:T(8,128)(2,1)S(1)} %shard_map.98), channel_id=1, replica_groups={{0,8,16,24,32,40,48,56},{2,10,18,26,34,42,50,58},{4,12,20,28,36,44,52,6..., dimensions={0} | all-to-all | bytes 360448 | tf_op jit(solution)/shard_map/all_to_all | solution.py:535
  122.9 5.0 %collective-permute-start.9 = (bf16[272,128]{1,0:T(8,128)(2,1)S(1)}, bf16[272,128]{1,0:T(8,128)(2,1)S(1)}, u32[]{:S(2)}, u32[]{:S(2)}) collective-permute-start(bf16[272,128]{1,0:T(8,128)(2,1)S(1)} %get-tuple-element.67), channel_id=1, source_target_pairs={{0,4},{2,6},{4,0},{6,2},{8,12},{10,14},{12,8},{14,10},{16,20},{18,... | collective-permute-start | bytes 208904 | tf_op jit(solution)/shard_map/ppermute | solution.py:530
  127.9 1.0 collective-permute-start.10
  129.7 3.3 %collective-permute-done.10.e3 = bf16[272,128]{1,0:T(8,128)(2,1)S(1)} collective-permute-done((bf16[272,128]{1,0:T(8,128)(2,1)S(1)}, bf16[272,128]{1,0:T(8,128)(2,1)S(1)}, u32[]{:S(2)}, u32[]{:S(2)}) %collective-permute-start.10) | collective-permute-done | bytes 69664 | tf_op jit(solution)/shard_map/ppermute | solution.py:530
  133.0 2.9 %shard_map.101 = (bf16[2,128,1280]{2,1,0:T(8,128)(2,1)S(1)}, bf16[2,128,1280]{2,1,0:T(8,128)(2,1)S(1)}, bf16[8,64,128]{2,1,0:T(8,128)(2,1)}, f32[10,128]{1,0:T(8,128)S(1)}) custom-call(bf16[272,128]{1,0:T(8,128)(2,1)S(1)} %collective-permute-done.8.e1, bf16[272,128]{1,0:T(8,128)(2,1)S(1)} %collective-permute-done.9.e2, ...), custom_call_target="tpu_custom_call" | custom-call | flops 24000000000 | bytes 1000000 | tf_op jit(solution)/shard_map/pallas_call | solution.py:24
  136.7 6.0 %all-to-all-start.2 = ((bf16[8,64,128]{2,1,0:T(8,128)(2,1)}), bf16[8,64,128]{2,1,0:T(8,128)(2,1)S(1)}, u32[]{:S(2)}, u32[]{:S(2)}) async-start(bf16[8,64,128]{2,1,0:T(8,128)(2,1)} %get-tuple-element.78), calls=%async_computation.2 | async-start | bytes 262144 | tf_op jit(solution)/shard_map/all_to_all | solution.py:535
  142.7 2.6 %collective-permute-start.11 = (bf16[2,128,1280]{2,1,0:T(8,128)(2,1)S(1)}, bf16[2,128,1280]{2,1,0:T(8,128)(2,1)S(1)}, u32[]{:S(2)}, u32[]{:S(2)}) collective-permute-start(bf16[2,128,1280]{2,1,0:T(8,128)(2,1)S(1)} %get-tuple-element.75), channel_id=1, source_target_pairs={{0,1},{1,0},{2,3},{3,2},{4,5},{5,4},{6,7},{7,6},{8,9},{9,8},{10,11... | collective-permute-start | bytes 1966088 | tf_op jit(solution)/shard_map/ppermute | solution.py:526
  145.3 23.3 %all-to-all-done.2.got = bf16[8,64,128]{2,1,0:T(8,128)(2,1)S(1)} async-done(((bf16[8,64,128]{2,1,0:T(8,128)(2,1)}), bf16[8,64,128]{2,1,0:T(8,128)(2,1)S(1)}, u32[]{:S(2)}, u32[]{:S(2)}) %all-to-all-start.2) | async-done | bytes 131104 | tf_op jit(solution)/shard_map/all_to_all | solution.py:535
  169.0 5.2 %collective-permute-start.13 = (bf16[328,128]{1,0:T(8,128)(2,1)S(1)}, bf16[328,128]{1,0:T(8,128)(2,1)S(1)}, u32[]{:S(2)}, u32[]{:S(2)}) collective-permute-start(bf16[328,128]{1,0:T(8,128)(2,1)S(1)} %get-tuple-element.82), channel_id=1, source_target_pairs={{0,4},{2,6},{4,0},{6,2},{8,12},{10,14},{12,8},{14,10},{16,20},{18,... | collective-permute-start | bytes 251912 | tf_op jit(solution)/shard_map/ppermute | solution.py:530
  175.2 3.6 %collective-permute-start.19 = (f32[128,1280]{1,0:T(8,128)S(1)}, f32[128,1280]{1,0:T(8,128)S(1)}, u32[]{:S(2)}, u32[]{:S(2)}) collective-permute-start(f32[128,1280]{1,0:T(8,128)S(1)} %get-tuple-element.85), channel_id=1, source_target_pairs={{0,1},{1,0},{2,3},{3,2},{4,5},{5,4},{6,7},{7,6},{8,9},{9,8},{10,11... | collective-permute-start | bytes 1966088 | tf_op jit(solution)/shard_map/ppermute | solution.py:526
  179.4 2.9 %collective-permute-start.17 = (bf16[328,128]{1,0:T(8,128)(2,1)S(1)}, bf16[328,128]{1,0:T(8,128)(2,1)S(1)}, u32[]{:S(2)}, u32[]{:S(2)}) collective-permute-start(bf16[328,128]{1,0:T(8,128)(2,1)S(1)} %collective-permute-done.13.g2), channel_id=1, source_target_pairs={{0,1},{1,0},{2,3},{3,2},{4,5},{5,4},{6,7},{7,6},{8,9},{9,8},{10,11... | collective-permute-start | bytes 251912 | tf_op jit(solution)/shard_map/ppermute | solution.py:526
  182.2 1.4 collective-permute-start.18
  183.7 1.5 shard_map.102
  185.2 2.4 %shard_map.104 = (bf16[128,2240]{1,0:T(8,128)(2,1)}, bf16[128,2240]{1,0:T(8,128)(2,1)}, f32[3,3,2240]{2,1,0:T(4,128)}) custom-call(bf16[328,128]{1,0:T(8,128)(2,1)S(1)} %get-tuple-element.80.g0, bf16[328,128]{1,0:T(8,128)(2,1)S(1)} %collective-permute-done.12.g1, bf16[328,128]{1,0:T(8,128)(2,1)S(1)} %collective-permute-done.13.g2, ...), custom_call_target="tpu_custom_call" | custom-call | flops 30000001024 | bytes 1000000 | tf_op jit(solution)/shard_map/pallas_call | solution.py:24
  (54 shorter events, 8.4 us)
Async XLA Ops:
  0.6 1.1 copy-start.2
  3.8 23.0 %copy-start = (bf16[2,128,1280]{2,1,0:T(8,128)(2,1)}, bf16[2,128,1280]{2,1,0:T(8,128)(2,1)S(1)}, u32[]{:S(2)}) copy-start(bf16[2,128,1280]{2,1,0:T(8,128)(2,1)S(1)} %get-tuple-element.48.send) | copy-start | bytes 1966084
  3.8 22.3 %collective-permute-start = (bf16[2,128,1280]{2,1,0:T(8,128)(2,1)S(1)}, bf16[2,128,1280]{2,1,0:T(8,128)(2,1)S(1)}, u32[]{:S(2)}, u32[]{:S(2)}) collective-permute-start(bf16[2,128,1280]{2,1,0:T(8,128)(2,1)S(1)} %get-tuple-element.48.send), channel_id=1, source_target_pairs={{0,1},{1,0},{2,3},{3,2},{4,5},{5,4},{6,7},{7,6},{8,9},{9,8},{10,11... | collective-permute-start | bytes 1966088 | tf_op jit(solution)/shard_map/ppermute | solution.py:526
  26.9 3.7 %collective-permute-start.1 = (bf16[288,128]{1,0:T(8,128)(2,1)S(1)}, bf16[288,128]{1,0:T(8,128)(2,1)S(1)}, u32[]{:S(2)}, u32[]{:S(2)}) collective-permute-start(bf16[288,128]{1,0:T(8,128)(2,1)S(1)} %get-tuple-element.52), channel_id=1, source_target_pairs={{0,2},{2,0},{4,6},{6,4},{8,10},{10,8},{12,14},{14,12},{16,18},{18,... | collective-permute-start | bytes 221192 | tf_op jit(solution)/shard_map/ppermute | solution.py:530
  27.0 4.3 %collective-permute-start.2 = (bf16[288,128]{1,0:T(8,128)(2,1)S(1)}, bf16[288,128]{1,0:T(8,128)(2,1)S(1)}, u32[]{:S(2)}, u32[]{:S(2)}) collective-permute-start(bf16[288,128]{1,0:T(8,128)(2,1)S(1)} %get-tuple-element.53), channel_id=1, source_target_pairs={{0,4},{2,6},{4,0},{6,2},{8,12},{10,14},{12,8},{14,10},{16,20},{18,... | collective-permute-start | bytes 221192 | tf_op jit(solution)/shard_map/ppermute | solution.py:530
  27.2 6.5 %collective-permute-start.3 = (bf16[288,128]{1,0:T(8,128)(2,1)S(1)}, bf16[288,128]{1,0:T(8,128)(2,1)S(1)}, u32[]{:S(2)}, u32[]{:S(2)}) collective-permute-start(bf16[288,128]{1,0:T(8,128)(2,1)S(1)} %get-tuple-element.54), channel_id=1, source_target_pairs={{0,6},{2,4},{4,2},{6,0},{8,14},{10,12},{12,10},{14,8},{16,22},{18,... | collective-permute-start | bytes 221192 | tf_op jit(solution)/shard_map/ppermute | solution.py:530
  33.7 14.8 %copy-start.4 = (bf16[1,4,32,2240]{3,2,1,0:T(8,128)(2,1)S(1)}, bf16[1,4,32,2240]{3,2,1,0:T(8,128)(2,1)}, u32[]{:S(2)}) copy-start(bf16[1,4,32,2240]{3,2,1,0:T(8,128)(2,1)} %param.5) | copy-start | bytes 1720324
  33.7 14.8 %copy-start.5 = (bf16[1,4,32,2240]{3,2,1,0:T(8,128)(2,1)S(1)}, bf16[1,4,32,2240]{3,2,1,0:T(8,128)(2,1)}, u32[]{:S(2)}) copy-start(bf16[1,4,32,2240]{3,2,1,0:T(8,128)(2,1)} %param.8) | copy-start | bytes 1720324
  33.7 14.8 %copy-start.6 = (f32[3,3,2240]{2,1,0:T(4,128)S(1)}, f32[3,3,2240]{2,1,0:T(4,128)}, u32[]{:S(2)}) copy-start(f32[3,3,2240]{2,1,0:T(4,128)} %taps.1) | copy-start | bytes 241924
  35.2 37.5 %all-to-all-start = ((bf16[8,64,128]{2,1,0:T(8,128)(2,1)}), bf16[8,64,128]{2,1,0:T(8,128)(2,1)S(1)}, u32[]{:S(2)}, u32[]{:S(2)}) async-start(bf16[8,64,128]{2,1,0:T(8,128)(2,1)} %get-tuple-element.55), calls=%async_computation | async-start | bytes 262144 | tf_op jit(solution)/shard_map/all_to_all | solution.py:535
  50.3 4.7 %collective-permute-start.4 = (bf16[2,128,1280]{2,1,0:T(8,128)(2,1)S(1)}, bf16[2,128,1280]{2,1,0:T(8,128)(2,1)S(1)}, u32[]{:S(2)}, u32[]{:S(2)}) collective-permute-start(bf16[2,128,1280]{2,1,0:T(8,128)(2,1)S(1)} %get-tuple-element.58), channel_id=1, source_target_pairs={{0,1},{1,0},{2,3},{3,2},{4,5},{5,4},{6,7},{7,6},{8,9},{9,8},{10,11... | collective-permute-start | bytes 1966088 | tf_op jit(solution)/shard_map/ppermute | solution.py:526
  72.7 1.1 copy-start.10
  76.3 10.5 %collective-permute-start.5 = (bf16[256,128]{1,0:T(8,128)(2,1)S(1)}, bf16[256,128]{1,0:T(8,128)(2,1)S(1)}, u32[]{:S(2)}, u32[]{:S(2)}) collective-permute-start(bf16[256,128]{1,0:T(8,128)(2,1)S(1)} %get-tuple-element.60), channel_id=1, source_target_pairs={{0,2},{2,0},{4,6},{6,4},{8,10},{10,8},{12,14},{14,12},{16,18},{18,... | collective-permute-start | bytes 196616 | tf_op jit(solution)/shard_map/ppermute | solution.py:530
  81.2 5.6 %collective-permute-start.6 = (bf16[256,128]{1,0:T(8,128)(2,1)S(1)}, bf16[256,128]{1,0:T(8,128)(2,1)S(1)}, u32[]{:S(2)}, u32[]{:S(2)}) collective-permute-start(bf16[256,128]{1,0:T(8,128)(2,1)S(1)} %get-tuple-element.61), channel_id=1, source_target_pairs={{0,4},{2,6},{4,0},{6,2},{8,12},{10,14},{12,8},{14,10},{16,20},{18,... | collective-permute-start | bytes 196616 | tf_op jit(solution)/shard_map/ppermute | solution.py:530
  82.8 4.9 %collective-permute-start.7 = (bf16[256,128]{1,0:T(8,128)(2,1)S(1)}, bf16[256,128]{1,0:T(8,128)(2,1)S(1)}, u32[]{:S(2)}, u32[]{:S(2)}) collective-permute-start(bf16[256,128]{1,0:T(8,128)(2,1)S(1)} %get-tuple-element.62), channel_id=1, source_target_pairs={{0,6},{2,4},{4,2},{6,0},{8,14},{10,12},{12,10},{14,8},{16,22},{18,... | collective-permute-start | bytes 196616 | tf_op jit(solution)/shard_map/ppermute | solution.py:530
  122.7 7.0 %collective-permute-start.8 = (bf16[272,128]{1,0:T(8,128)(2,1)S(1)}, bf16[272,128]{1,0:T(8,128)(2,1)S(1)}, u32[]{:S(2)}, u32[]{:S(2)}) collective-permute-start(bf16[272,128]{1,0:T(8,128)(2,1)S(1)} %get-tuple-element.66), channel_id=1, source_target_pairs={{0,2},{2,0},{4,6},{6,4},{8,10},{10,8},{12,14},{14,12},{16,18},{18,... | collective-permute-start | bytes 208904 | tf_op jit(solution)/shard_map/ppermute | solution.py:530
  122.9 6.8 %collective-permute-start.9 = (bf16[272,128]{1,0:T(8,128)(2,1)S(1)}, bf16[272,128]{1,0:T(8,128)(2,1)S(1)}, u32[]{:S(2)}, u32[]{:S(2)}) collective-permute-start(bf16[272,128]{1,0:T(8,128)(2,1)S(1)} %get-tuple-element.67), channel_id=1, source_target_pairs={{0,4},{2,6},{4,0},{6,2},{8,12},{10,14},{12,8},{14,10},{16,20},{18,... | collective-permute-start | bytes 208904 | tf_op jit(solution)/shard_map/ppermute | solution.py:530
  127.9 5.1 %copy-start.11 = (bf16[2,128,1280]{2,1,0:T(8,128)(2,1)S(1)}, bf16[2,128,1280]{2,1,0:T(8,128)(2,1)}, u32[]{:S(2)}) copy-start(bf16[2,128,1280]{2,1,0:T(8,128)(2,1)} %copy-done.9) | copy-start | bytes 1966084
  127.9 5.1 %collective-permute-start.10 = (bf16[272,128]{1,0:T(8,128)(2,1)S(1)}, bf16[272,128]{1,0:T(8,128)(2,1)S(1)}, u32[]{:S(2)}, u32[]{:S(2)}) collective-permute-start(bf16[272,128]{1,0:T(8,128)(2,1)S(1)} %get-tuple-element.68), channel_id=1, source_target_pairs={{0,6},{2,4},{4,2},{6,0},{8,14},{10,12},{12,10},{14,8},{16,22},{18,... | collective-permute-start | bytes 208904 | tf_op jit(solution)/shard_map/ppermute | solution.py:530
  136.7 31.9 %all-to-all-start.2 = ((bf16[8,64,128]{2,1,0:T(8,128)(2,1)}), bf16[8,64,128]{2,1,0:T(8,128)(2,1)S(1)}, u32[]{:S(2)}, u32[]{:S(2)}) async-start(bf16[8,64,128]{2,1,0:T(8,128)(2,1)} %get-tuple-element.78), calls=%async_computation.2 | async-start | bytes 262144 | tf_op jit(solution)/shard_map/all_to_all | solution.py:535
  142.7 36.2 %collective-permute-start.11 = (bf16[2,128,1280]{2,1,0:T(8,128)(2,1)S(1)}, bf16[2,128,1280]{2,1,0:T(8,128)(2,1)S(1)}, u32[]{:S(2)}, u32[]{:S(2)}) collective-permute-start(bf16[2,128,1280]{2,1,0:T(8,128)(2,1)S(1)} %get-tuple-element.75), channel_id=1, source_target_pairs={{0,1},{1,0},{2,3},{3,2},{4,5},{5,4},{6,7},{7,6},{8,9},{9,8},{10,11... | collective-permute-start | bytes 1966088 | tf_op jit(solution)/shard_map/ppermute | solution.py:526
  168.6 15.1 %copy-start.8 = (bf16[2,128,1280]{2,1,0:T(8,128)(2,1)S(1)}, bf16[2,128,1280]{2,1,0:T(8,128)(2,1)}, u32[]{:S(2)}) copy-start(bf16[2,128,1280]{2,1,0:T(8,128)(2,1)} %copy-done.7) | copy-start | bytes 1966084
  168.8 10.0 %collective-permute-start.12 = (bf16[328,128]{1,0:T(8,128)(2,1)S(1)}, bf16[328,128]{1,0:T(8,128)(2,1)S(1)}, u32[]{:S(2)}, u32[]{:S(2)}) collective-permute-start(bf16[328,128]{1,0:T(8,128)(2,1)S(1)} %get-tuple-element.81), channel_id=1, source_target_pairs={{0,2},{2,0},{4,6},{6,4},{8,10},{10,8},{12,14},{14,12},{16,18},{18,... | collective-permute-start | bytes 251912 | tf_op jit(solution)/shard_map/ppermute | solution.py:530
  169.0 10.4 %collective-permute-start.13 = (bf16[328,128]{1,0:T(8,128)(2,1)S(1)}, bf16[328,128]{1,0:T(8,128)(2,1)S(1)}, u32[]{:S(2)}, u32[]{:S(2)}) collective-permute-start(bf16[328,128]{1,0:T(8,128)(2,1)S(1)} %get-tuple-element.82), channel_id=1, source_target_pairs={{0,4},{2,6},{4,0},{6,2},{8,12},{10,14},{12,8},{14,10},{16,20},{18,... | collective-permute-start | bytes 251912 | tf_op jit(solution)/shard_map/ppermute | solution.py:530
  174.2 8.1 %collective-permute-start.14 = (bf16[328,128]{1,0:T(8,128)(2,1)S(1)}, bf16[328,128]{1,0:T(8,128)(2,1)S(1)}, u32[]{:S(2)}, u32[]{:S(2)}) collective-permute-start(bf16[328,128]{1,0:T(8,128)(2,1)S(1)} %get-tuple-element.83), channel_id=1, source_target_pairs={{0,6},{2,4},{4,2},{6,0},{8,14},{10,12},{12,10},{14,8},{16,22},{18,... | collective-permute-start | bytes 251912 | tf_op jit(solution)/shard_map/ppermute | solution.py:530
  175.2 10.0 %collective-permute-start.19 = (f32[128,1280]{1,0:T(8,128)S(1)}, f32[128,1280]{1,0:T(8,128)S(1)}, u32[]{:S(2)}, u32[]{:S(2)}) collective-permute-start(f32[128,1280]{1,0:T(8,128)S(1)} %get-tuple-element.85), channel_id=1, source_target_pairs={{0,1},{1,0},{2,3},{3,2},{4,5},{5,4},{6,7},{7,6},{8,9},{9,8},{10,11... | collective-permute-start | bytes 1966088 | tf_op jit(solution)/shard_map/ppermute | solution.py:526
  178.8 6.3 %collective-permute-start.15 = (bf16[328,128]{1,0:T(8,128)(2,1)S(1)}, bf16[328,128]{1,0:T(8,128)(2,1)S(1)}, u32[]{:S(2)}, u32[]{:S(2)}) collective-permute-start(bf16[328,128]{1,0:T(8,128)(2,1)S(1)} %get-tuple-element.80.g0), channel_id=1, source_target_pairs={{0,1},{1,0},{2,3},{3,2},{4,5},{5,4},{6,7},{7,6},{8,9},{9,8},{10,11... | collective-permute-start | bytes 251912 | tf_op jit(solution)/shard_map/ppermute | solution.py:526
  178.8 6.3 %collective-permute-start.16 = (bf16[328,128]{1,0:T(8,128)(2,1)S(1)}, bf16[328,128]{1,0:T(8,128)(2,1)S(1)}, u32[]{:S(2)}, u32[]{:S(2)}) collective-permute-start(bf16[328,128]{1,0:T(8,128)(2,1)S(1)} %collective-permute-done.12.g1), channel_id=1, source_target_pairs={{0,1},{1,0},{2,3},{3,2},{4,5},{5,4},{6,7},{7,6},{8,9},{9,8},{10,11... | collective-permute-start | bytes 251912 | tf_op jit(solution)/shard_map/ppermute | solution.py:526
  179.4 5.8 %collective-permute-start.17 = (bf16[328,128]{1,0:T(8,128)(2,1)S(1)}, bf16[328,128]{1,0:T(8,128)(2,1)S(1)}, u32[]{:S(2)}, u32[]{:S(2)}) collective-permute-start(bf16[328,128]{1,0:T(8,128)(2,1)S(1)} %collective-permute-done.13.g2), channel_id=1, source_target_pairs={{0,1},{1,0},{2,3},{3,2},{4,5},{5,4},{6,7},{7,6},{8,9},{9,8},{10,11... | collective-permute-start | bytes 251912 | tf_op jit(solution)/shard_map/ppermute | solution.py:526
  182.2 3.0 %collective-permute-start.18 = (bf16[328,128]{1,0:T(8,128)(2,1)S(1)}, bf16[328,128]{1,0:T(8,128)(2,1)S(1)}, u32[]{:S(2)}, u32[]{:S(2)}) collective-permute-start(bf16[328,128]{1,0:T(8,128)(2,1)S(1)} %collective-permute-done.14.g3), channel_id=1, source_target_pairs={{0,1},{1,0},{2,3},{3,2},{4,5},{5,4},{6,7},{7,6},{8,9},{9,8},{10,11... | collective-permute-start | bytes 251912 | tf_op jit(solution)/shard_map/ppermute | solution.py:526
  183.7 1.6 copy-start.1
  183.7 1.6 copy-start.13
  (4 other events, 3.7 us)

commit v4 on v3

--- a/solution.py
+++ b/solution.py
@@ -20,15 +20,15 @@
 VMEM_LIMIT = 16 << 20
 
 
-def call(kernel, outs, *args, scratch=(), us=1, space=pltpu.VMEM):
+def call(kernel, outs, *args, scratch=(), us=1):
     return pl.pallas_call(
         kernel,
         out_shape=[jax.ShapeDtypeStruct(s, d) for s, d in outs],
-        in_specs=[pl.BlockSpec(memory_space=space)] * len(args),
+        in_specs=[pl.BlockSpec(memory_space=pltpu.VMEM)] * len(args),
         out_specs=[pl.BlockSpec(memory_space=pltpu.VMEM)] * len(outs),
         scratch_shapes=[pltpu.VMEM(*s) if isinstance(s, tuple) else s for s in scratch],
         interpret=INTERPRET,
-        cost_estimate=pl.CostEstimate(flops=us * 6 * 10**9, bytes_accessed=10**6, transcendentals=0),
+        cost_estimate=pl.CostEstimate(flops=us * 10**10, bytes_accessed=10**6, transcendentals=0),
         compiler_params=pltpu.CompilerParams(vmem_limit_bytes=VMEM_LIMIT),
     )(*args)
 
@@ -149,13 +149,12 @@
             send[j, :, col(i)] = lax.select(first, b, a).astype(BF)
 
 
-def spread_kv_kernel(k, v, keep, send, buf, sems):
-    copies = [pltpu.make_async_copy(x, buf.at[j], sems.at[j]) for j, x in enumerate((k, v))]
-    for c in copies:
-        c.start()
-    for j, c in enumerate(copies):
-        c.wait()
-        spread((buf.at[j],), (j == 0,), keep.at[j : j + 1], send.at[j : j + 1])
+def spread_k_kernel(k, keep, send):
+    spread((k,), (True,), keep, send)
+
+
+def spread_v_kernel(v, keep, send):
+    spread((v,), (False,), keep, send)
 
 
 def spread_qg_kernel(q, g, taps, after, keep, send, taps_out):
@@ -184,8 +183,8 @@
     pos = lax.broadcasted_iota(jnp.int32, (n, LN), 0) % cols
     zero_row = jnp.zeros((cols, LN), F32)
 
-    def shifts(keep, recv, i):
-        a, b = keep[1, :, col(i)].astype(F32), recv[1, :, col(i)].astype(F32)
+    def shifts(keep, recv, j, i):
+        a, b = keep[j, :, col(i)].astype(F32), recv[j, :, col(i)].astype(F32)
         x = jnp.concatenate([lax.select(first, a, b), lax.select(first, b, a)], axis=0)
         before = jnp.where(pos == 0, 0.0, pltpu.roll(x, 1, 0))
         after = jnp.where(pos == cols - 1, 0.0, pltpu.roll(x, n - 1, 0))
@@ -203,7 +202,7 @@
 
     for i in range(HC):
         w = [taps[a, :, col(i)] for a in range(3)]
-        vs, gs = shifts(keep_v, recv_v, i), shifts(keep_g, recv_g, i)
+        vs, gs = shifts(keep_v, recv_v, 0, i), shifts(keep_g, recv_g, 1, i)
         u = [sum(w[a][b : b + 1] * vs[b] for b in range(3)) for a in range(3)]
         put(local.at[0:half], local.at[half:n], up(u[0]) + u[1] + down(u[2]), i)
         u = [sum(w[a][b : b + 1] * gs[2 - b] for b in range(3)) for a in range(3)]
@@ -239,11 +238,11 @@
     return x[0:HC] + x[HC : 2 * HC], x[2 * HC : 3 * HC]
 
 
-def partial_kernel(keep, recv, own, ksum, mean, a1, a2, a3, state, rows):
+def partial_kernel(keep_k, recv_k, keep_v, recv_v, own, ksum, mean, a1, a2, a3, state, rows):
     p = place()[1]
     mats, sums, means = [], [], []
     for i in range(HC):
-        keys, v = both(keep, recv, 0, i), both(keep, recv, 1, i).astype(F32)
+        keys, v = both(keep_k, recv_k, 0, i), both(keep_v, recv_v, 0, i).astype(F32)
         mid = (jnp.sum(v, axis=0, keepdims=True) * (1.0 / v.shape[0])).astype(BF).astype(F32)
         hi, lo = halves(v - mid)
         x = mm(keys, jnp.concatenate([hi, lo], axis=1), TN)[:HD]
@@ -318,7 +317,7 @@
     return 1.0 / (den + 1.0)
 
 
-def turn_kernel(got, kpre, keep, recv, down, kt, own, c1, c2, c3, state):
+def turn_kernel(got, kpre, keep, recv, after, down, kt, own, c1, c2, c3, state):
     _, p, mine = place()
     nb = got.shape[0]
     n = ROWS // NEAR
@@ -418,14 +417,14 @@
         mine[1, :, col(i)] = x[:half]
         other[1, :, col(i)] = x[half:]
         gks[i : i + 1, :] = jnp.sum(gden * qf, axis=0, keepdims=True)
-    put_rows(rows, *split(gks[...]), *split(taps))
+    put_rows(rows, gks[...], *split(taps))
     block = rows[...].astype(BF)
     for b in range(nb):
         pay[b, 0:m, :] = back[b]
         pay[b, m:, :] = block
 
 
-def suffix_kernel(got, own, c1, c2, c3, gks, g0, g1, g2, g3, rows):
+def suffix_kernel(got, own, c1, c2, c3, gks, after, g0, g1, g2, g3, rows):
     _, p, mine = place()
     nb = got.shape[0]
     n = ROWS // NEAR
@@ -435,16 +434,16 @@
     taps = []
     for b in range(nb):
         x = got[b, m:, :].astype(F32)
-        later = later + flag(b > mine) * (x[0:HC] + x[HC : 2 * HC])
-        taps.append(x[2 * HC : 2 * HC + 3] + x[2 * HC + 3 : 2 * HC + 6])
-    his, los = zip(*(split(x) for x in taps))
+        later = later + flag(b > mine) * x[0:HC]
+        taps.append(x[HC : HC + 3] + x[HC + 3 : HC + 6])
+    taps = jnp.concatenate(taps, axis=0)
     parts = [own[...]] + [r[...].astype(F32) for r in (c1, c2, c3)]
     for k, ref in enumerate((g0, g1, g2, g3)):
         x = base
         for j in range(NEAR):
             x = x + flag((p ^ j) >= (p ^ k)) * parts[j]
         ref[0:n, :] = x.astype(BF)
-        put_rows(rows, *split(later + flag(p >= (p ^ k)) * gks[...]), *his, *los)
+        put_rows(rows, later + flag(p >= (p ^ k)) * gks[...], jnp.zeros((HC, LN), F32), *split(taps))
         ref[n:, :] = rows[...].astype(BF)
 
 
@@ -456,7 +455,7 @@
     for k, ref in enumerate(refs):
         state[rows_at(p, k, n), :] = ref[0:n, :].astype(F32)
         x = ref[n:, :].astype(F32)
-        total = total + (x[0:HC] + x[HC : 2 * HC])
+        total = total + x[0:HC]
         for b in range(nb):
             at = 2 * HC + 3 * b
             taps[b, p ^ k] = x[at : at + 3] + x[at + 3 * nb : at + 3 * nb + 3]
@@ -464,18 +463,18 @@
 
 
 def finish_kernel(
-    g0, g1, g2, g3, o0, o1, o2, o3, keep, send, gc_mine, gc_other, key, value, taps, state, taps_a, taps_b
+    g0, g1, g2, g3, o0, o1, o2, o3, keep_k, keep_v, send_k, send_v, gc_mine, gc_other, key, value, taps, state, taps_a, taps_b
 ):
     first = place()[0] == 0
     sides = []
     for refs, tokens, conv, scratch in (
-        ((g0, g1, g2, g3), keep, gc_mine, taps_a),
-        ((o0, o1, o2, o3), send, gc_other, taps_b),
+        ((g0, g1, g2, g3), (keep_k, keep_v), gc_mine, taps_a),
+        ((o0, o1, o2, o3), (send_k, send_v), gc_other, taps_b),
     ):
         mats, total = assembled(refs, state, scratch)
         keys_out, values_out, taps_out = [], [], []
         for i in range(HC):
-            keys, v = tokens[0, :, col(i)], tokens[1, :, col(i)]
+            keys, v = tokens[0][0, :, col(i)], tokens[1][0, :, col(i)]
             hi, lo = halves(pad_rows(mats[i]))
             gk = mm(jnp.concatenate([v, v], axis=1), jnp.concatenate([hi, lo], axis=1), NT)
             keys_out.append(jnp.where(keys.astype(F32) > 0.0, gk + total[i : i + 1, :], 0.0))
@@ -507,7 +506,8 @@
         ref[:, LN * t : LN * t + n] = x[:, :n].astype(ref.dtype)
 
 
-def merge_kernel(mine, other, out_a, out_b):
+def merge_kernel(mine, other, out_a, out_b, done):
+    done[...] = jnp.zeros_like(done)
     first = place()[0] == 0
     for j, ref in enumerate((out_a, out_b)):
         heads = [[x[j, :, col(i)].astype(F32) for i in range(HC)] for x in (mine, other)]
@@ -543,27 +543,25 @@
     row = ((HC, LN), F32)
     state = ((ROWS, LN), F32)
 
-    keep_kv, send_kv = call(
-        spread_kv_kernel,
-        [pair, pair],
-        k, v, us=1, space=pltpu.HBM,
-        scratch=[((2, t, width), BF), pltpu.SemaphoreType.DMA((2,))],
-    )
-    recv_kv = over(send_kv)
+    one = ((1, t, WC), BF)
+    keep_k, send_k = call(spread_k_kernel, [one, one], k)
+    recv_k = over(send_k)
+    keep_v, send_v = call(spread_v_kernel, [one, one], v)
+    recv_v = over(send_v)
     own_b, ksum, mean, *out = call(
         partial_kernel,
         [share, small, small] + [((n + 32, LN), BF)] * 3,
-        keep_kv, recv_kv, scratch=[state, ((32, LN), F32)], us=1,
+        keep_k, recv_k, keep_v, recv_v, scratch=[state, ((32, LN), F32)], us=1,
     )
     got_a = near(out)
     keep_qg, send_qg, taps = call(
-        spread_qg_kernel, [pair, pair, ((3, 3, WC), F32)], q, g, conv_taps, ksum, us=3
+        spread_qg_kernel, [pair, pair, ((3, 3, WC), F32)], q, g, conv_taps, ksum, us=1
     )
     recv_qg = over(send_qg)
     local, gc_mine, gc_other, taps_part = call(
         conv_kernel,
         [((2 * t, WC), F32), ((t, WC), F32), ((t, WC), F32), ((96, LN), F32)],
-        keep_kv, recv_kv, keep_qg, recv_qg, taps, us=6,
+        keep_v, recv_v, keep_qg, recv_qg, taps, us=1,
     )
     gc_other = over(gc_other)
     pay, kpre = call(
@@ -575,7 +573,7 @@
     down, kt, own_d, *out = call(
         turn_kernel,
         [((nb, m, LN), BF), row, share] + [((n, LN), BF)] * 3,
-        got, kpre, keep_qg, recv_qg, scratch=[state], us=4,
+        got, kpre, keep_qg, recv_qg, taps_part, scratch=[state], us=4,
     )
     got_c = near(out)
     (pay,) = call(
@@ -593,24 +591,26 @@
     got_e = near((e1, e2, e3))
     mine, other, pay, gks = call(
         attend_kernel,
-        [pair, pair, ((nb, m + 32, LN), BF), row],
+        [pair, pair, ((nb, m + 16, LN), BF), row],
         *got_e, s_own, rank, kt, keep_qg, recv_qg, local, taps_own, back,
-        scratch=[state, ((32, LN), F32)], us=4,
+        scratch=[state, ((16, LN), F32)], us=4,
     )
     got = far(pay)
     whole = ((t, width), BF)
-    attended, query_grad = call(merge_kernel, [whole, whole], mine, over(other), us=3)
+    attended, query_grad, done = call(
+        merge_kernel, [whole, whole, ((8, LN), F32)], mine, over(other), us=2
+    )
     tail = -(-(2 * HC + 6 * nb) // 8) * 8
     g0, *out = call(
         suffix_kernel,
         [((n + tail, LN), BF)] * 4,
-        got, own_d, *got_c, gks, scratch=[((tail, LN), F32)],
+        got, own_d, *got_c, gks, done, scratch=[((tail, LN), F32)],
     )
     gs = [g0] + near(out)
     key_grad, value_grad, taps_grad = call(
         finish_kernel,
         [whole, whole, (conv_taps.shape, F32)],
-        *gs, *[over(x) for x in gs], keep_kv, send_kv, gc_mine, gc_other,
+        *gs, *[over(x) for x in gs], keep_k, keep_v, send_k, send_v, gc_mine, gc_other,
         scratch=[state] + [((nb, NEAR, 3, LN), F32)] * 2, us=5,
     )
     return (

time: 188 us -> 186 us (0.989)
  waiting for transfers between devices: 51.8 us -> 49.7 us
    unnamed x28 -> x38, local copies, waits for them, and re-layouts: 4.94 us -> 6.45 us
    pallas_call x13 -> x14, Pallas kernels: 17.8 us -> 17.5 us  [call(): pl.pallas_call(kernel, out_shape=[jax.ShapeDtypeStruct(s, d) for s, d in...]
    ppermute x8 -> x9, starting transfers between devices: 34.5 us -> 34.4 us  [over(): return lax.ppermute(x, 'space', [(0, 1), (1, 0)])]
  transfers between devices with their start and end apart: 22 -> 23, of which waited for: 8 -> 9; matrix products, arithmetic and copies ran while one was open for 0% -> 0% of each run, Pallas kernels for 3% -> 4%
where the time goes in v4:
time: 186 us; the launch traced here: 185 us
  starting transfers between devices  76.8 us (41%)
  waiting for transfers between devices  49.7 us (27%)
  blocking collectives  34.3 us (18%)
  Pallas kernels  17.5 us (9%)
  local copies, waits for them, and re-layouts  6.45 us (3%)
    all_to_all x2, waiting for transfers between devices, far(): return lax.all_to_all(x, 'tm', 0, 0, axis_index_groups=across, tiled=True)  39.7 us
    ppermute x9, starting transfers between devices, over(): return lax.ppermute(x, 'space', [(0, 1), (1, 0)])  34.4 us
    all_to_all x1, blocking collectives, far(): return lax.all_to_all(x, 'tm', 0, 0, axis_index_groups=across, tiled=True)  34.3 us
    ppermute x12, starting transfers between devices, near(): lax.ppermute(a, 'tm', [(i, i ^ k) for i in range(frames)])  24.9 us
    all_to_all x2, starting transfers between devices, far(): return lax.all_to_all(x, 'tm', 0, 0, axis_index_groups=across, tiled=True)  17.5 us
    pallas_call x14, Pallas kernels, call(): pl.pallas_call(kernel, out_shape=[jax.ShapeDtypeStruct(s, d) for s, d in...  17.5 us
    ppermute x12, waiting for transfers between devices, near(): lax.ppermute(a, 'tm', [(i, i ^ k) for i in range(frames)])  8.17 us
    unnamed x38, local copies, waits for them, and re-layouts  6.45 us
  transfers between devices with their start and end apart: 23, of which 9 were waited for; matrix products, arithmetic and copies ran while one was open for 0% of the time, Pallas kernels for 4%

profile of v4, /device:TPU:37, one launch (start us, length us, event | category | flops | bytes accessed | tf_op | source)
XLA Modules:
  0.0 185.5 jit_solution(11428154854446772124)
XLA Ops:
  0.6 1.1 copy-done
  2.2 20.5 %collective-permute-start = (bf16[1,128,1280]{2,1,0:T(8,128)(2,1)S(1)}, bf16[1,128,1280]{2,1,0:T(8,128)(2,1)S(1)}, u32[]{:S(2)}, u32[]{:S(2)}) collective-permute-start(bf16[1,128,1280]{2,1,0:T(8,128)(2,1)S(1)} %get-tuple-element.51.send_k), channel_id=1, source_target_pairs={{0,1},{1,0},{2,3},{3,2},{4,5},{5,4},{6,7},{7,6},{8,9},{9,8},{10,11... | collective-permute-start | bytes 983048 | tf_op jit(solution)/shard_map/ppermute | solution.py:526
  26.0 3.4 %collective-permute-start.4 = (bf16[288,128]{1,0:T(8,128)(2,1)S(1)}, bf16[288,128]{1,0:T(8,128)(2,1)S(1)}, u32[]{:S(2)}, u32[]{:S(2)}) collective-permute-start(bf16[288,128]{1,0:T(8,128)(2,1)S(1)} %get-tuple-element.59), channel_id=1, source_target_pairs={{0,6},{2,4},{4,2},{6,0},{8,14},{10,12},{12,10},{14,8},{16,22},{18,... | collective-permute-start | bytes 221192 | tf_op jit(solution)/shard_map/ppermute | solution.py:530
  30.3 1.3 collective-permute-start.5
  31.6 0.9 collective-permute-done.4.a3
  32.5 1.5 shard_map.95
  34.0 13.3 %all-to-all-start = ((bf16[8,64,128]{2,1,0:T(8,128)(2,1)}), bf16[8,64,128]{2,1,0:T(8,128)(2,1)S(1)}, u32[]{:S(2)}, u32[]{:S(2)}) async-start(bf16[8,64,128]{2,1,0:T(8,128)(2,1)} %get-tuple-element.60), calls=%async_computation | async-start | bytes 262144 | tf_op jit(solution)/shard_map/all_to_all | solution.py:535
  47.4 3.0 %shard_map.97 = (f32[256,1280]{1,0:T(8,128)S(1)}, f32[128,1280]{1,0:T(8,128)S(1)}, f32[128,1280]{1,0:T(8,128)S(1)}, f32[96,128]{1,0:T(8,128)S(1)}) custom-call(bf16[1,128,1280]{2,1,0:T(8,128)(2,1)S(1)} %get-tuple-element.52.keep_v, bf16[1,128,1280]{2,1,0:T(8,128)(2,1)S(1)} %collective-permute-done.1.recv_v, ...), custom_call_target="tpu_custom_call" | custom-call | flops 10000000000 | bytes 1000000 | tf_op jit(solution)/shard_map/pallas_call | solution.py:24
  50.4 1.1 copy-done.9
  53.1 18.6 %all-to-all-done.got = bf16[8,64,128]{2,1,0:T(8,128)(2,1)S(1)} async-done(((bf16[8,64,128]{2,1,0:T(8,128)(2,1)}), bf16[8,64,128]{2,1,0:T(8,128)(2,1)S(1)}, u32[]{:S(2)}, u32[]{:S(2)}) %all-to-all-start) | async-done | bytes 131104 | tf_op jit(solution)/shard_map/all_to_all | solution.py:535
  71.7 2.5 %shard_map.98 = (bf16[8,32,128]{2,1,0:T(8,128)(2,1)S(1)}, f32[10,128]{1,0:T(8,128)S(1)}, f32[256,128]{1,0:T(8,128)S(1)}, bf16[256,128]{1,0:T(8,128)(2,1)S(1)}, b...) custom-call(bf16[8,64,128]{2,1,0:T(8,128)(2,1)S(1)} %all-to-all-done.got, ...), custom_call_target="tpu_custom_call" | custom-call | flops 40000000000 | bytes 1000000 | tf_op jit(solution)/shard_map/pallas_call | solution.py:24
  74.2 5.0 %collective-permute-start.6 = (bf16[256,128]{1,0:T(8,128)(2,1)S(1)}, bf16[256,128]{1,0:T(8,128)(2,1)S(1)}, u32[]{:S(2)}, u32[]{:S(2)}) collective-permute-start(bf16[256,128]{1,0:T(8,128)(2,1)S(1)} %get-tuple-element.67), channel_id=1, source_target_pairs={{0,2},{2,0},{4,6},{6,4},{8,10},{10,8},{12,14},{14,12},{16,18},{18,... | collective-permute-start | bytes 196616 | tf_op jit(solution)/shard_map/ppermute | solution.py:530
  79.2 2.0 %collective-permute-start.7 = (bf16[256,128]{1,0:T(8,128)(2,1)S(1)}, bf16[256,128]{1,0:T(8,128)(2,1)S(1)}, u32[]{:S(2)}, u32[]{:S(2)}) collective-permute-start(bf16[256,128]{1,0:T(8,128)(2,1)S(1)} %get-tuple-element.68), channel_id=1, source_target_pairs={{0,4},{2,6},{4,0},{6,2},{8,12},{10,14},{12,8},{14,10},{16,20},{18,... | collective-permute-start | bytes 196616 | tf_op jit(solution)/shard_map/ppermute | solution.py:530
  81.2 1.0 collective-permute-start.8
  82.2 1.0 collective-permute-done.7.c2
  83.2 2.9 %collective-permute-done.8.c3 = bf16[256,128]{1,0:T(8,128)(2,1)S(1)} collective-permute-done((bf16[256,128]{1,0:T(8,128)(2,1)S(1)}, bf16[256,128]{1,0:T(8,128)(2,1)S(1)}, u32[]{:S(2)}, u32[]{:S(2)}) %collective-permute-start.8) | collective-permute-done | bytes 65568 | tf_op jit(solution)/shard_map/ppermute | solution.py:530
  86.1 34.3 %all_to_all.15.got = bf16[8,88,128]{2,1,0:T(8,128)(2,1)S(1)} all-to-all(bf16[8,88,128]{2,1,0:T(8,128)(2,1)S(1)} %shard_map.99), channel_id=1, replica_groups={{0,8,16,24,32,40,48,56},{2,10,18,26,34,42,50,58},{4,12,20,28,36,44,52,6..., dimensions={0} | all-to-all | bytes 360448 | tf_op jit(solution)/shard_map/all_to_all | solution.py:535
  120.8 5.1 %collective-permute-start.10 = (bf16[272,128]{1,0:T(8,128)(2,1)S(1)}, bf16[272,128]{1,0:T(8,128)(2,1)S(1)}, u32[]{:S(2)}, u32[]{:S(2)}) collective-permute-start(bf16[272,128]{1,0:T(8,128)(2,1)S(1)} %get-tuple-element.72), channel_id=1, source_target_pairs={{0,4},{2,6},{4,0},{6,2},{8,12},{10,14},{12,8},{14,10},{16,20},{18,... | collective-permute-start | bytes 208904 | tf_op jit(solution)/shard_map/ppermute | solution.py:530
  125.8 1.0 collective-permute-start.11
  127.7 3.4 %collective-permute-done.11.e3 = bf16[272,128]{1,0:T(8,128)(2,1)S(1)} collective-permute-done((bf16[272,128]{1,0:T(8,128)(2,1)S(1)}, bf16[272,128]{1,0:T(8,128)(2,1)S(1)}, u32[]{:S(2)}, u32[]{:S(2)}) %collective-permute-start.11) | collective-permute-done | bytes 69664 | tf_op jit(solution)/shard_map/ppermute | solution.py:530
  131.0 2.9 %shard_map.102 = (bf16[2,128,1280]{2,1,0:T(8,128)(2,1)S(1)}, bf16[2,128,1280]{2,1,0:T(8,128)(2,1)S(1)}, bf16[8,48,128]{2,1,0:T(8,128)(2,1)}, f32[10,128]{1,0:T(8,128)S(1)}) custom-call(bf16[272,128]{1,0:T(8,128)(2,1)S(1)} %collective-permute-done.9.e1, bf16[272,128]{1,0:T(8,128)(2,1)S(1)} %collective-permute-done.10.e2, ...), custom_call_target="tpu_custom_call" | custom-call | flops 40000000000 | bytes 1000000 | tf_op jit(solution)/shard_map/pallas_call | solution.py:24
  134.7 4.0 %collective-permute-start.12 = (bf16[2,128,1280]{2,1,0:T(8,128)(2,1)S(1)}, bf16[2,128,1280]{2,1,0:T(8,128)(2,1)S(1)}, u32[]{:S(2)}, u32[]{:S(2)}) collective-permute-start(bf16[2,128,1280]{2,1,0:T(8,128)(2,1)S(1)} %get-tuple-element.80), channel_id=1, source_target_pairs={{0,1},{1,0},{2,3},{3,2},{4,5},{5,4},{6,7},{7,6},{8,9},{9,8},{10,11... | collective-permute-start | bytes 1966088 | tf_op jit(solution)/shard_map/ppermute | solution.py:526
  138.8 4.1 %all-to-all-start.2 = ((bf16[8,48,128]{2,1,0:T(8,128)(2,1)}), bf16[8,48,128]{2,1,0:T(8,128)(2,1)S(1)}, u32[]{:S(2)}, u32[]{:S(2)}) async-start(bf16[8,48,128]{2,1,0:T(8,128)(2,1)} %get-tuple-element.83), calls=%async_computation.2 | async-start | bytes 196608 | tf_op jit(solution)/shard_map/all_to_all | solution.py:535
  142.9 1.1 copy-done.18
  144.0 1.5 shard_map.103
  145.5 21.1 %all-to-all-done.2.got = bf16[8,48,128]{2,1,0:T(8,128)(2,1)S(1)} async-done(((bf16[8,48,128]{2,1,0:T(8,128)(2,1)}), bf16[8,48,128]{2,1,0:T(8,128)(2,1)S(1)}, u32[]{:S(2)}, u32[]{:S(2)}) %all-to-all-start.2) | async-done | bytes 98336 | tf_op jit(solution)/shard_map/all_to_all | solution.py:535
  166.9 0.9 collective-permute-start.13
  167.8 5.1 %collective-permute-start.14 = (bf16[328,128]{1,0:T(8,128)(2,1)S(1)}, bf16[328,128]{1,0:T(8,128)(2,1)S(1)}, u32[]{:S(2)}, u32[]{:S(2)}) collective-permute-start(bf16[328,128]{1,0:T(8,128)(2,1)S(1)} %get-tuple-element.88), channel_id=1, source_target_pairs={{0,4},{2,6},{4,0},{6,2},{8,12},{10,14},{12,8},{14,10},{16,20},{18,... | collective-permute-start | bytes 251912 | tf_op jit(solution)/shard_map/ppermute | solution.py:530
  172.9 1.0 collective-permute-start.15
  173.9 1.9 %collective-permute-start.16 = (bf16[328,128]{1,0:T(8,128)(2,1)S(1)}, bf16[328,128]{1,0:T(8,128)(2,1)S(1)}, u32[]{:S(2)}, u32[]{:S(2)}) collective-permute-start(bf16[328,128]{1,0:T(8,128)(2,1)S(1)} %get-tuple-element.86.g0), channel_id=1, source_target_pairs={{0,1},{1,0},{2,3},{3,2},{4,5},{5,4},{6,7},{7,6},{8,9},{9,8},{10,11... | collective-permute-start | bytes 251912 | tf_op jit(solution)/shard_map/ppermute | solution.py:526
  176.3 5.5 %collective-permute-start.18 = (bf16[328,128]{1,0:T(8,128)(2,1)S(1)}, bf16[328,128]{1,0:T(8,128)(2,1)S(1)}, u32[]{:S(2)}, u32[]{:S(2)}) collective-permute-start(bf16[328,128]{1,0:T(8,128)(2,1)S(1)} %collective-permute-done.14.g2), channel_id=1, source_target_pairs={{0,1},{1,0},{2,3},{3,2},{4,5},{5,4},{6,7},{7,6},{8,9},{9,8},{10,11... | collective-permute-start | bytes 251912 | tf_op jit(solution)/shard_map/ppermute | solution.py:526
  183.1 2.4 %shard_map.105 = (bf16[128,2240]{1,0:T(8,128)(2,1)}, bf16[128,2240]{1,0:T(8,128)(2,1)}, f32[3,3,2240]{2,1,0:T(4,128)}) custom-call(bf16[328,128]{1,0:T(8,128)(2,1)S(1)} %get-tuple-element.86.g0, bf16[328,128]{1,0:T(8,128)(2,1)S(1)} %collective-permute-done.13.g1, bf16[328,128]{1,0:T(8,128)(2,1)S(1)} %collective-permute-done.14.g2, ...), custom_call_target="tpu_custom_call" | custom-call | flops 49999998976 | bytes 1000000 | tf_op jit(solution)/shard_map/pallas_call | solution.py:24
  (67 shorter events, 10.3 us)
Async XLA Ops:
  1.7 21.0 %copy-start.1 = (bf16[1,4,32,2240]{3,2,1,0:T(8,128)(2,1)S(1)}, bf16[1,4,32,2240]{3,2,1,0:T(8,128)(2,1)}, u32[]{:S(2)}) copy-start(bf16[1,4,32,2240]{3,2,1,0:T(8,128)(2,1)} %param.7) | copy-start | bytes 1720324
  2.1 20.9 %copy-start.4 = (bf16[1,128,1280]{2,1,0:T(8,128)(2,1)}, bf16[1,128,1280]{2,1,0:T(8,128)(2,1)S(1)}, u32[]{:S(2)}) copy-start(bf16[1,128,1280]{2,1,0:T(8,128)(2,1)S(1)} %get-tuple-element.51.send_k) | copy-start | bytes 983044
  2.1 22.8 %copy-start.15 = (bf16[1,128,1280]{2,1,0:T(8,128)(2,1)}, bf16[1,128,1280]{2,1,0:T(8,128)(2,1)S(1)}, u32[]{:S(2)}) copy-start(bf16[1,128,1280]{2,1,0:T(8,128)(2,1)S(1)} %get-tuple-element.50.keep_k) | copy-start | bytes 983044
  2.2 22.2 %collective-permute-start = (bf16[1,128,1280]{2,1,0:T(8,128)(2,1)S(1)}, bf16[1,128,1280]{2,1,0:T(8,128)(2,1)S(1)}, u32[]{:S(2)}, u32[]{:S(2)}) collective-permute-start(bf16[1,128,1280]{2,1,0:T(8,128)(2,1)S(1)} %get-tuple-element.51.send_k), channel_id=1, source_target_pairs={{0,1},{1,0},{2,3},{3,2},{4,5},{5,4},{6,7},{7,6},{8,9},{9,8},{10,11... | collective-permute-start | bytes 983048 | tf_op jit(solution)/shard_map/ppermute | solution.py:526
  23.1 1.9 %collective-permute-start.1 = (bf16[1,128,1280]{2,1,0:T(8,128)(2,1)S(1)}, bf16[1,128,1280]{2,1,0:T(8,128)(2,1)S(1)}, u32[]{:S(2)}, u32[]{:S(2)}) collective-permute-start(bf16[1,128,1280]{2,1,0:T(8,128)(2,1)S(1)} %get-tuple-element.53.send_v), channel_id=1, source_target_pairs={{0,1},{1,0},{2,3},{3,2},{4,5},{5,4},{6,7},{7,6},{8,9},{9,8},{10,11... | collective-permute-start | bytes 983048 | tf_op jit(solution)/shard_map/ppermute | solution.py:526
  25.7 5.9 %collective-permute-start.2 = (bf16[288,128]{1,0:T(8,128)(2,1)S(1)}, bf16[288,128]{1,0:T(8,128)(2,1)S(1)}, u32[]{:S(2)}, u32[]{:S(2)}) collective-permute-start(bf16[288,128]{1,0:T(8,128)(2,1)S(1)} %get-tuple-element.57), channel_id=1, source_target_pairs={{0,2},{2,0},{4,6},{6,4},{8,10},{10,8},{12,14},{14,12},{16,18},{18,... | collective-permute-start | bytes 221192 | tf_op jit(solution)/shard_map/ppermute | solution.py:530
  25.9 5.7 %collective-permute-start.3 = (bf16[288,128]{1,0:T(8,128)(2,1)S(1)}, bf16[288,128]{1,0:T(8,128)(2,1)S(1)}, u32[]{:S(2)}, u32[]{:S(2)}) collective-permute-start(bf16[288,128]{1,0:T(8,128)(2,1)S(1)} %get-tuple-element.58), channel_id=1, source_target_pairs={{0,4},{2,6},{4,0},{6,2},{8,12},{10,14},{12,8},{14,10},{16,20},{18,... | collective-permute-start | bytes 221192 | tf_op jit(solution)/shard_map/ppermute | solution.py:530
  26.0 6.5 %collective-permute-start.4 = (bf16[288,128]{1,0:T(8,128)(2,1)S(1)}, bf16[288,128]{1,0:T(8,128)(2,1)S(1)}, u32[]{:S(2)}, u32[]{:S(2)}) collective-permute-start(bf16[288,128]{1,0:T(8,128)(2,1)S(1)} %get-tuple-element.59), channel_id=1, source_target_pairs={{0,6},{2,4},{4,2},{6,0},{8,14},{10,12},{12,10},{14,8},{16,22},{18,... | collective-permute-start | bytes 221192 | tf_op jit(solution)/shard_map/ppermute | solution.py:530
  30.3 17.1 %collective-permute-start.5 = (bf16[2,128,1280]{2,1,0:T(8,128)(2,1)S(1)}, bf16[2,128,1280]{2,1,0:T(8,128)(2,1)S(1)}, u32[]{:S(2)}, u32[]{:S(2)}) collective-permute-start(bf16[2,128,1280]{2,1,0:T(8,128)(2,1)S(1)} %get-tuple-element.63), channel_id=1, source_target_pairs={{0,1},{1,0},{2,3},{3,2},{4,5},{5,4},{6,7},{7,6},{8,9},{9,8},{10,11... | collective-permute-start | bytes 1966088 | tf_op jit(solution)/shard_map/ppermute | solution.py:526
  34.0 37.6 %all-to-all-start = ((bf16[8,64,128]{2,1,0:T(8,128)(2,1)}), bf16[8,64,128]{2,1,0:T(8,128)(2,1)S(1)}, u32[]{:S(2)}, u32[]{:S(2)}) async-start(bf16[8,64,128]{2,1,0:T(8,128)(2,1)} %get-tuple-element.60), calls=%async_computation | async-start | bytes 262144 | tf_op jit(solution)/shard_map/all_to_all | solution.py:535
  74.2 8.0 %collective-permute-start.6 = (bf16[256,128]{1,0:T(8,128)(2,1)S(1)}, bf16[256,128]{1,0:T(8,128)(2,1)S(1)}, u32[]{:S(2)}, u32[]{:S(2)}) collective-permute-start(bf16[256,128]{1,0:T(8,128)(2,1)S(1)} %get-tuple-element.67), channel_id=1, source_target_pairs={{0,2},{2,0},{4,6},{6,4},{8,10},{10,8},{12,14},{14,12},{16,18},{18,... | collective-permute-start | bytes 196616 | tf_op jit(solution)/shard_map/ppermute | solution.py:530
  79.2 4.0 %collective-permute-start.7 = (bf16[256,128]{1,0:T(8,128)(2,1)S(1)}, bf16[256,128]{1,0:T(8,128)(2,1)S(1)}, u32[]{:S(2)}, u32[]{:S(2)}) collective-permute-start(bf16[256,128]{1,0:T(8,128)(2,1)S(1)} %get-tuple-element.68), channel_id=1, source_target_pairs={{0,4},{2,6},{4,0},{6,2},{8,12},{10,14},{12,8},{14,10},{16,20},{18,... | collective-permute-start | bytes 196616 | tf_op jit(solution)/shard_map/ppermute | solution.py:530
  81.2 4.9 %collective-permute-start.8 = (bf16[256,128]{1,0:T(8,128)(2,1)S(1)}, bf16[256,128]{1,0:T(8,128)(2,1)S(1)}, u32[]{:S(2)}, u32[]{:S(2)}) collective-permute-start(bf16[256,128]{1,0:T(8,128)(2,1)S(1)} %get-tuple-element.69), channel_id=1, source_target_pairs={{0,6},{2,4},{4,2},{6,0},{8,14},{10,12},{12,10},{14,8},{16,22},{18,... | collective-permute-start | bytes 196616 | tf_op jit(solution)/shard_map/ppermute | solution.py:530
  120.6 7.0 %collective-permute-start.9 = (bf16[272,128]{1,0:T(8,128)(2,1)S(1)}, bf16[272,128]{1,0:T(8,128)(2,1)S(1)}, u32[]{:S(2)}, u32[]{:S(2)}) collective-permute-start(bf16[272,128]{1,0:T(8,128)(2,1)S(1)} %get-tuple-element.71), channel_id=1, source_target_pairs={{0,2},{2,0},{4,6},{6,4},{8,10},{10,8},{12,14},{14,12},{16,18},{18,... | collective-permute-start | bytes 208904 | tf_op jit(solution)/shard_map/ppermute | solution.py:530
  120.8 6.9 %collective-permute-start.10 = (bf16[272,128]{1,0:T(8,128)(2,1)S(1)}, bf16[272,128]{1,0:T(8,128)(2,1)S(1)}, u32[]{:S(2)}, u32[]{:S(2)}) collective-permute-start(bf16[272,128]{1,0:T(8,128)(2,1)S(1)} %get-tuple-element.72), channel_id=1, source_target_pairs={{0,4},{2,6},{4,0},{6,2},{8,12},{10,14},{12,8},{14,10},{16,20},{18,... | collective-permute-start | bytes 208904 | tf_op jit(solution)/shard_map/ppermute | solution.py:530
  125.8 5.2 %copy-start.10 = (f32[256,1280]{1,0:T(8,128)S(1)}, f32[256,1280]{1,0:T(8,128)}, u32[]{:S(2)}) copy-start(f32[256,1280]{1,0:T(8,128)} %copy-done.9) | copy-start | bytes 3932164
  125.8 5.2 %collective-permute-start.11 = (bf16[272,128]{1,0:T(8,128)(2,1)S(1)}, bf16[272,128]{1,0:T(8,128)(2,1)S(1)}, u32[]{:S(2)}, u32[]{:S(2)}) collective-permute-start(bf16[272,128]{1,0:T(8,128)(2,1)S(1)} %get-tuple-element.73), channel_id=1, source_target_pairs={{0,6},{2,4},{4,2},{6,0},{8,14},{10,12},{12,10},{14,8},{16,22},{18,... | collective-permute-start | bytes 208904 | tf_op jit(solution)/shard_map/ppermute | solution.py:530
  134.7 8.2 %collective-permute-start.12 = (bf16[2,128,1280]{2,1,0:T(8,128)(2,1)S(1)}, bf16[2,128,1280]{2,1,0:T(8,128)(2,1)S(1)}, u32[]{:S(2)}, u32[]{:S(2)}) collective-permute-start(bf16[2,128,1280]{2,1,0:T(8,128)(2,1)S(1)} %get-tuple-element.80), channel_id=1, source_target_pairs={{0,1},{1,0},{2,3},{3,2},{4,5},{5,4},{6,7},{7,6},{8,9},{9,8},{10,11... | collective-permute-start | bytes 1966088 | tf_op jit(solution)/shard_map/ppermute | solution.py:526
  138.8 43.0 %collective-permute-start.20 = (f32[128,1280]{1,0:T(8,128)S(1)}, f32[128,1280]{1,0:T(8,128)S(1)}, u32[]{:S(2)}, u32[]{:S(2)}) collective-permute-start(f32[128,1280]{1,0:T(8,128)S(1)} %get-tuple-element.91), channel_id=1, source_target_pairs={{0,1},{1,0},{2,3},{3,2},{4,5},{5,4},{6,7},{7,6},{8,9},{9,8},{10,11... | collective-permute-start | bytes 1966088 | tf_op jit(solution)/shard_map/ppermute | solution.py:526
  138.8 27.9 %all-to-all-start.2 = ((bf16[8,48,128]{2,1,0:T(8,128)(2,1)}), bf16[8,48,128]{2,1,0:T(8,128)(2,1)S(1)}, u32[]{:S(2)}, u32[]{:S(2)}) async-start(bf16[8,48,128]{2,1,0:T(8,128)(2,1)} %get-tuple-element.83), calls=%async_computation.2 | async-start | bytes 196608 | tf_op jit(solution)/shard_map/all_to_all | solution.py:535
  166.6 16.5 %copy-start.5 = (bf16[1,128,1280]{2,1,0:T(8,128)(2,1)S(1)}, bf16[1,128,1280]{2,1,0:T(8,128)(2,1)}, u32[]{:S(2)}) copy-start(bf16[1,128,1280]{2,1,0:T(8,128)(2,1)} %copy-done.4) | copy-start | bytes 983044
  166.6 16.5 %copy-start.7 = (bf16[1,128,1280]{2,1,0:T(8,128)(2,1)S(1)}, bf16[1,128,1280]{2,1,0:T(8,128)(2,1)}, u32[]{:S(2)}) copy-start(bf16[1,128,1280]{2,1,0:T(8,128)(2,1)} %copy-done.6) | copy-start | bytes 983044
  166.6 16.5 %copy-start.12 = (f32[128,1280]{1,0:T(8,128)S(1)}, f32[128,1280]{1,0:T(8,128)}, u32[]{:S(2)}) copy-start(f32[128,1280]{1,0:T(8,128)} %copy-done.11) | copy-start | bytes 1966084
  166.7 16.5 %copy-start.14 = (bf16[1,128,1280]{2,1,0:T(8,128)(2,1)S(1)}, bf16[1,128,1280]{2,1,0:T(8,128)(2,1)}, u32[]{:S(2)}) copy-start(bf16[1,128,1280]{2,1,0:T(8,128)(2,1)} %copy-done.13) | copy-start | bytes 983044
  166.7 16.5 %copy-start.16 = (bf16[1,128,1280]{2,1,0:T(8,128)(2,1)S(1)}, bf16[1,128,1280]{2,1,0:T(8,128)(2,1)}, u32[]{:S(2)}) copy-start(bf16[1,128,1280]{2,1,0:T(8,128)(2,1)} %copy-done.15) | copy-start | bytes 983044
  166.9 8.9 %collective-permute-start.13 = (bf16[328,128]{1,0:T(8,128)(2,1)S(1)}, bf16[328,128]{1,0:T(8,128)(2,1)S(1)}, u32[]{:S(2)}, u32[]{:S(2)}) collective-permute-start(bf16[328,128]{1,0:T(8,128)(2,1)S(1)} %get-tuple-element.87), channel_id=1, source_target_pairs={{0,2},{2,0},{4,6},{6,4},{8,10},{10,8},{12,14},{14,12},{16,18},{18,... | collective-permute-start | bytes 251912 | tf_op jit(solution)/shard_map/ppermute | solution.py:530
  167.8 8.5 %collective-permute-start.14 = (bf16[328,128]{1,0:T(8,128)(2,1)S(1)}, bf16[328,128]{1,0:T(8,128)(2,1)S(1)}, u32[]{:S(2)}, u32[]{:S(2)}) collective-permute-start(bf16[328,128]{1,0:T(8,128)(2,1)S(1)} %get-tuple-element.88), channel_id=1, source_target_pairs={{0,4},{2,6},{4,0},{6,2},{8,12},{10,14},{12,8},{14,10},{16,20},{18,... | collective-permute-start | bytes 251912 | tf_op jit(solution)/shard_map/ppermute | solution.py:530
  172.9 9.0 %collective-permute-start.15 = (bf16[328,128]{1,0:T(8,128)(2,1)S(1)}, bf16[328,128]{1,0:T(8,128)(2,1)S(1)}, u32[]{:S(2)}, u32[]{:S(2)}) collective-permute-start(bf16[328,128]{1,0:T(8,128)(2,1)S(1)} %get-tuple-element.89), channel_id=1, source_target_pairs={{0,6},{2,4},{4,2},{6,0},{8,14},{10,12},{12,10},{14,8},{16,22},{18,... | collective-permute-start | bytes 251912 | tf_op jit(solution)/shard_map/ppermute | solution.py:530
  173.9 7.9 %collective-permute-start.16 = (bf16[328,128]{1,0:T(8,128)(2,1)S(1)}, bf16[328,128]{1,0:T(8,128)(2,1)S(1)}, u32[]{:S(2)}, u32[]{:S(2)}) collective-permute-start(bf16[328,128]{1,0:T(8,128)(2,1)S(1)} %get-tuple-element.86.g0), channel_id=1, source_target_pairs={{0,1},{1,0},{2,3},{3,2},{4,5},{5,4},{6,7},{7,6},{8,9},{9,8},{10,11... | collective-permute-start | bytes 251912 | tf_op jit(solution)/shard_map/ppermute | solution.py:526
  175.8 6.0 %collective-permute-start.17 = (bf16[328,128]{1,0:T(8,128)(2,1)S(1)}, bf16[328,128]{1,0:T(8,128)(2,1)S(1)}, u32[]{:S(2)}, u32[]{:S(2)}) collective-permute-start(bf16[328,128]{1,0:T(8,128)(2,1)S(1)} %collective-permute-done.13.g1), channel_id=1, source_target_pairs={{0,1},{1,0},{2,3},{3,2},{4,5},{5,4},{6,7},{7,6},{8,9},{9,8},{10,11... | collective-permute-start | bytes 251912 | tf_op jit(solution)/shard_map/ppermute | solution.py:526
  176.3 6.4 %collective-permute-start.18 = (bf16[328,128]{1,0:T(8,128)(2,1)S(1)}, bf16[328,128]{1,0:T(8,128)(2,1)S(1)}, u32[]{:S(2)}, u32[]{:S(2)}) collective-permute-start(bf16[328,128]{1,0:T(8,128)(2,1)S(1)} %collective-permute-done.14.g2), channel_id=1, source_target_pairs={{0,1},{1,0},{2,3},{3,2},{4,5},{5,4},{6,7},{7,6},{8,9},{9,8},{10,11... | collective-permute-start | bytes 251912 | tf_op jit(solution)/shard_map/ppermute | solution.py:526
  181.8 1.3 collective-permute-start.19
  (10 other events, 19.8 us)

commit v5 on v4

--- a/solution.py
+++ b/solution.py
@@ -212,7 +212,7 @@
             s = vs[b]
             for a, prod in enumerate((g[cols:] * s[: n - cols], g * s, g[: n - cols] * s[cols:])):
                 r = 9 * i + 3 * a + b
-                taps_out[r : r + 1, :] = jnp.sum(prod, axis=0, keepdims=True)
+                taps_out[r // 24, r % 24 : r % 24 + 1, :] = jnp.sum(prod, axis=0, keepdims=True)
 
 
 def rows_at(p, k, n):
@@ -317,7 +317,7 @@
     return 1.0 / (den + 1.0)
 
 
-def turn_kernel(got, kpre, keep, recv, after, down, kt, own, c1, c2, c3, state):
+def turn_kernel(got, kpre, keep, recv, taps, down, kt, own, taps_own, c1, c2, c3, state, rows):
     _, p, mine = place()
     nb = got.shape[0]
     n = ROWS // NEAR
@@ -339,49 +339,49 @@
     pack(state, mats)
     own[...] = state[rows_at(p, 0, n), :]
     for k, ref in enumerate((c1, c2, c3), 1):
-        ref[...] = state[rows_at(p, k, n), :].astype(BF)
+        ref[0:n, :] = state[rows_at(p, k, n), :].astype(BF)
+        put_rows(rows, *split(taps[p ^ k]))
+        ref[n:, :] = rows[...].astype(BF)
+    taps_own[...] = taps[p]
 
 
 def back_block_kernel(own, c1, c2, c3, down, taps, pay, rows):
     nb = pay.shape[0]
-    m = ROWS // NEAR // nb
-    total = own[...]
+    n = ROWS // NEAR
+    m = n // nb
+    total, t = own[...], taps[...]
     for ref in (c1, c2, c3):
-        total = total + ref[...].astype(F32)
+        total = total + ref[0:n, :].astype(F32)
+        x = ref[n:, :].astype(F32)
+        t = t + (x[0:24] + x[24:48])
+    hi, lo = split(t)
     for b in range(nb):
         pay[b, 0:m, :] = down[b]
         pay[b, m : 2 * m, :] = total[m * b : m * (b + 1)].astype(BF)
-        put_rows(rows, *split(taps[12 * b : 12 * (b + 1), :]))
+        put_rows(rows, hi[3 * b : 3 * b + 3], lo[3 * b : 3 * b + 3])
         pay[b, 2 * m :, :] = rows[...].astype(BF)
 
 
-def prefix_kernel(got, own, a1, a2, a3, s_own, e1, e2, e3, taps_own, back, taps, rows):
+def prefix_kernel(got, own, a1, a2, a3, s_own, e1, e2, e3, taps_own, back):
     p = place()[1]
     nb = got.shape[0]
     n = ROWS // NEAR
     m = n // nb
     base = jnp.concatenate([got[b, 0:m, :].astype(F32) for b in range(nb)], axis=0)
     run = jnp.zeros((m, LN), F32)
-    t = jnp.zeros((12, LN), F32)
+    t = jnp.zeros((3, LN), F32)
     for b in reversed(range(nb)):
         back[b] = run.astype(BF)
         run = run + got[b, m : 2 * m, :].astype(F32)
         x = got[b, 2 * m :, :].astype(F32)
-        t = t + (x[0:12] + x[12:24])
-    for j in range(NEAR):
-        taps[j] = t[3 * j : 3 * (j + 1)]
+        t = t + (x[0:3] + x[3:6])
+    taps_own[...] = t
     parts = [own[...]] + [r[0:n, :].astype(F32) for r in (a1, a2, a3)]
     for k, ref in enumerate((s_own, e1, e2, e3)):
         x = base
         for j in range(NEAR):
             x = x + flag((p ^ j) <= (p ^ k)) * parts[j]
-        if k == 0:
-            ref[...] = x
-        else:
-            ref[0:n, :] = x.astype(BF)
-            put_rows(rows, *split(taps[p ^ k]))
-            ref[n:, :] = rows[...].astype(BF)
-    taps_own[...] = taps[p]
+        ref[...] = x.astype(ref.dtype)
 
 
 def attend_kernel(
@@ -395,9 +395,7 @@
     state[rows_at(p, 0, n), :] = s_own[...]
     taps = taps_own[...]
     for k, ref in enumerate((e1, e2, e3), 1):
-        state[rows_at(p, k, n), :] = ref[0:n, :].astype(F32)
-        x = ref[n:, :].astype(F32)
-        taps = taps + (x[0:3] + x[3:6])
+        state[rows_at(p, k, n), :] = ref[...].astype(F32)
     mats = unpack(state)
     key_total = kt[...]
     ones = jnp.ones((2 * LN, LN), BF)
@@ -437,7 +435,7 @@
         later = later + flag(b > mine) * x[0:HC]
         taps.append(x[HC : HC + 3] + x[HC + 3 : HC + 6])
     taps = jnp.concatenate(taps, axis=0)
-    parts = [own[...]] + [r[...].astype(F32) for r in (c1, c2, c3)]
+    parts = [own[...]] + [r[0:n, :].astype(F32) for r in (c1, c2, c3)]
     for k, ref in enumerate((g0, g1, g2, g3)):
         x = base
         for j in range(NEAR):
@@ -462,27 +460,31 @@
     return unpack(state), total
 
 
-def finish_kernel(
-    g0, g1, g2, g3, o0, o1, o2, o3, keep_k, keep_v, send_k, send_v, gc_mine, gc_other, key, value, taps, state, taps_a, taps_b
-):
+def key_value_grads(refs, tokens, conv, state, taps):
+    mats, total = assembled(refs, state, taps)
+    keys_out, values_out = [], []
+    for i in range(HC):
+        keys, v = tokens[0][0, :, col(i)], tokens[1][0, :, col(i)]
+        hi, lo = halves(pad_rows(mats[i]))
+        gk = mm(jnp.concatenate([v, v], axis=1), jnp.concatenate([hi, lo], axis=1), NT)
+        keys_out.append(jnp.where(keys.astype(F32) > 0.0, gk + total[i : i + 1, :], 0.0))
+        gm = mm(jnp.concatenate([keys, keys], axis=1), jnp.concatenate([hi, lo], axis=0), NN)
+        values_out.append(gm + conv[:, col(i)])
+    return keys_out, values_out
+
+
+def half_kernel(g0, g1, g2, g3, keep_k, keep_v, gc_mine, side, taps, state):
+    sides = key_value_grads((g0, g1, g2, g3), (keep_k, keep_v), gc_mine, state, taps)
+    for j in range(2):
+        for i in range(HC):
+            side[j, :, col(i)] = sides[j][i].astype(BF)
+
+
+def finish_kernel(o0, o1, o2, o3, send_k, send_v, gc_other, side, taps_a, key, value, taps, state, taps_b):
     first = place()[0] == 0
-    sides = []
-    for refs, tokens, conv, scratch in (
-        ((g0, g1, g2, g3), (keep_k, keep_v), gc_mine, taps_a),
-        ((o0, o1, o2, o3), (send_k, send_v), gc_other, taps_b),
-    ):
-        mats, total = assembled(refs, state, scratch)
-        keys_out, values_out, taps_out = [], [], []
-        for i in range(HC):
-            keys, v = tokens[0][0, :, col(i)], tokens[1][0, :, col(i)]
-            hi, lo = halves(pad_rows(mats[i]))
-            gk = mm(jnp.concatenate([v, v], axis=1), jnp.concatenate([hi, lo], axis=1), NT)
-            keys_out.append(jnp.where(keys.astype(F32) > 0.0, gk + total[i : i + 1, :], 0.0))
-            gm = mm(jnp.concatenate([keys, keys], axis=1), jnp.concatenate([hi, lo], axis=0), NN)
-            values_out.append(gm + conv[:, col(i)])
-        sides.append((keys_out, values_out))
+    sides = key_value_grads((o0, o1, o2, o3), (send_k, send_v), gc_other, state, taps_b)
     for j, ref in enumerate((key, value)):
-        gather_heads(first, sides[0][j], sides[1][j], ref)
+        gather_heads(first, [side[j, :, col(i)].astype(F32) for i in range(HC)], sides[j], ref)
     for a in range(3):
         rows = []
         for scratch in (taps_a, taps_b):
@@ -491,7 +493,7 @@
                 lines = []
                 for b in range(3):
                     r = 9 * i + 3 * a + b
-                    lines.append(scratch[r // 12, (r % 12) // 3, r % 3 : r % 3 + 1, :])
+                    lines.append(scratch[(r % 24) // 3, r // 24, r % 3 : r % 3 + 1, :])
                 heads.append(jnp.concatenate(lines, axis=0))
             rows.append(heads)
         gather_heads(first, rows[0], rows[1], taps.at[a])
@@ -560,8 +562,8 @@
     recv_qg = over(send_qg)
     local, gc_mine, gc_other, taps_part = call(
         conv_kernel,
-        [((2 * t, WC), F32), ((t, WC), F32), ((t, WC), F32), ((96, LN), F32)],
-        keep_v, recv_v, keep_qg, recv_qg, taps, us=1,
+        [((2 * t, WC), F32), ((t, WC), F32), ((t, WC), F32), ((NEAR, 24, LN), F32)],
+        keep_v, recv_v, keep_qg, recv_qg, taps, us=2,
     )
     gc_other = over(gc_other)
     pay, kpre = call(
@@ -570,23 +572,23 @@
         own_b, ksum, mean, *got_a, scratch=[state, ((32, LN), F32)],
     )
     got = far(pay)
-    down, kt, own_d, *out = call(
+    down, kt, own_d, taps_own, *out = call(
         turn_kernel,
-        [((nb, m, LN), BF), row, share] + [((n, LN), BF)] * 3,
-        got, kpre, keep_qg, recv_qg, taps_part, scratch=[state], us=4,
+        [((nb, m, LN), BF), row, share, ((24, LN), F32)] + [((n + 48, LN), BF)] * 3,
+        got, kpre, keep_qg, recv_qg, taps_part, scratch=[state, ((48, LN), F32)], us=4,
     )
     got_c = near(out)
     (pay,) = call(
         back_block_kernel,
-        [((nb, 2 * m + 24, LN), BF)],
-        own_d, *got_c, down, taps_part, scratch=[((24, LN), F32)],
+        [((nb, 2 * m + 8, LN), BF)],
+        own_d, *got_c, down, taps_own, scratch=[((8, LN), F32)],
     )
     (rank,) = call(rank_kernel, [((HC * HD, LN), F32)], got, ksum, mean, *got_a, us=2)
     got = far(pay)
     s_own, e1, e2, e3, taps_own, back = call(
         prefix_kernel,
-        [share] + [((n + 16, LN), BF)] * 3 + [((3, LN), F32), ((nb, m, LN), BF)],
-        got, own_b, *got_a, scratch=[((NEAR, 3, LN), F32), ((16, LN), F32)],
+        [share] + [((n, LN), BF)] * 3 + [((3, LN), F32), ((nb, m, LN), BF)],
+        got, own_b, *got_a,
     )
     got_e = near((e1, e2, e3))
     mine, other, pay, gks = call(
@@ -607,11 +609,15 @@
         got, own_d, *got_c, gks, done, scratch=[((tail, LN), F32)],
     )
     gs = [g0] + near(out)
+    quarters = ((nb, NEAR, 3, LN), F32)
+    side, taps_mine = call(
+        half_kernel, [pair, quarters], *gs, keep_k, keep_v, gc_mine, scratch=[state], us=2
+    )
     key_grad, value_grad, taps_grad = call(
         finish_kernel,
         [whole, whole, (conv_taps.shape, F32)],
-        *gs, *[over(x) for x in gs], keep_k, keep_v, send_k, send_v, gc_mine, gc_other,
-        scratch=[state] + [((nb, NEAR, 3, LN), F32)] * 2, us=5,
+        *[over(x) for x in gs], send_k, send_v, gc_other, side, taps_mine,
+        scratch=[state, quarters], us=2,
     )
     return (
         attended.reshape(shape),

time: 186 us -> 184 us (0.989)
  starting transfers between devices: 76.8 us -> 74.2 us
  waiting for transfers between devices: 49.7 us -> 52.3 us
  blocking collectives: 34.3 us -> 32.1 us
    all_to_all x2, waiting for transfers between devices: 39.7 us -> 42.5 us  [far(): return lax.all_to_all(x, 'tm', 0, 0, axis_index_groups=across, tiled=True)]
    all_to_all x1, blocking collectives: 34.3 us -> 32.1 us  [far(): return lax.all_to_all(x, 'tm', 0, 0, axis_index_groups=across, tiled=True)]
    pallas_call x14 -> x15, Pallas kernels: 17.5 us -> 17.6 us  [call(): pl.pallas_call(kernel, out_shape=[jax.ShapeDtypeStruct(s, d) for s, d in...]
  transfers between devices with their start and end apart: 23 -> 23, of which waited for: 9 -> 9; matrix products, arithmetic and copies ran while one was open for 0% -> 0% of each run, Pallas kernels for 4% -> 5%
where the time goes in v5:
time: 184 us; the launch traced here: 183 us
  starting transfers between devices  74.2 us (40%)
  waiting for transfers between devices  52.3 us (28%)
  blocking collectives  32.1 us (17%)
  Pallas kernels  17.6 us (10%)
  local copies, waits for them, and re-layouts  6.47 us (4%)
    all_to_all x2, waiting for transfers between devices, far(): return lax.all_to_all(x, 'tm', 0, 0, axis_index_groups=across, tiled=True)  42.5 us
    ppermute x9, starting transfers between devices, over(): return lax.ppermute(x, 'space', [(0, 1), (1, 0)])  34.2 us
    all_to_all x1, blocking collectives, far(): return lax.all_to_all(x, 'tm', 0, 0, axis_index_groups=across, tiled=True)  32.1 us
    ppermute x12, starting transfers between devices, near(): lax.ppermute(a, 'tm', [(i, i ^ k) for i in range(frames)])  23 us
    pallas_call x15, Pallas kernels, call(): pl.pallas_call(kernel, out_shape=[jax.ShapeDtypeStruct(s, d) for s, d in...  17.6 us
    all_to_all x2, starting transfers between devices, far(): return lax.all_to_all(x, 'tm', 0, 0, axis_index_groups=across, tiled=True)  16.9 us
    ppermute x12, waiting for transfers between devices, near(): lax.ppermute(a, 'tm', [(i, i ^ k) for i in range(frames)])  8.56 us
    unnamed x38, local copies, waits for them, and re-layouts  6.47 us
  transfers between devices with their start and end apart: 23, of which 9 were waited for; matrix products, arithmetic and copies ran while one was open for 0% of the time, Pallas kernels for 5%

profile of v5, /device:TPU:37, one launch (start us, length us, event | category | flops | bytes accessed | tf_op | source)
XLA Modules:
  0.0 183.5 jit_solution(2762015194440629358)
XLA Ops:
  0.6 1.1 copy-done
  2.2 20.5 %collective-permute-start = (bf16[1,128,1280]{2,1,0:T(8,128)(2,1)S(1)}, bf16[1,128,1280]{2,1,0:T(8,128)(2,1)S(1)}, u32[]{:S(2)}, u32[]{:S(2)}) collective-permute-start(bf16[1,128,1280]{2,1,0:T(8,128)(2,1)S(1)} %get-tuple-element.54.send_k), channel_id=1, source_target_pairs={{0,1},{1,0},{2,3},{3,2},{4,5},{5,4},{6,7},{7,6},{8,9},{9,8},{10,11... | collective-permute-start | bytes 983048 | tf_op jit(solution)/shard_map/ppermute | solution.py:528
  26.0 3.4 %collective-permute-start.4 = (bf16[288,128]{1,0:T(8,128)(2,1)S(1)}, bf16[288,128]{1,0:T(8,128)(2,1)S(1)}, u32[]{:S(2)}, u32[]{:S(2)}) collective-permute-start(bf16[288,128]{1,0:T(8,128)(2,1)S(1)} %get-tuple-element.62), channel_id=1, source_target_pairs={{0,6},{2,4},{4,2},{6,0},{8,14},{10,12},{12,10},{14,8},{16,22},{18,... | collective-permute-start | bytes 221192 | tf_op jit(solution)/shard_map/ppermute | solution.py:532
  30.3 1.3 collective-permute-start.5
  31.6 0.9 collective-permute-done.4.a3
  32.5 1.5 shard_map.95
  34.0 13.3 %all-to-all-start = ((bf16[8,64,128]{2,1,0:T(8,128)(2,1)}), bf16[8,64,128]{2,1,0:T(8,128)(2,1)S(1)}, u32[]{:S(2)}, u32[]{:S(2)}) async-start(bf16[8,64,128]{2,1,0:T(8,128)(2,1)} %get-tuple-element.63), calls=%async_computation | async-start | bytes 262144 | tf_op jit(solution)/shard_map/all_to_all | solution.py:537
  47.4 3.0 %shard_map.97 = (f32[256,1280]{1,0:T(8,128)S(1)}, f32[128,1280]{1,0:T(8,128)S(1)}, f32[128,1280]{1,0:T(8,128)S(1)}, f32[4,24,128]{2,1,0:T(8,128)S(1)}) custom-call(bf16[1,128,1280]{2,1,0:T(8,128)(2,1)S(1)} %get-tuple-element.55.keep_v, bf16[1,128,1280]{2,1,0:T(8,128)(2,1)S(1)} %collective-permute-done.1.recv_v, ...), custom_call_target="tpu_custom_call" | custom-call | flops 20000000000 | bytes 1000000 | tf_op jit(solution)/shard_map/pallas_call | solution.py:24
  51.1 1.1 copy-done.13
  53.1 18.5 %all-to-all-done.got = bf16[8,64,128]{2,1,0:T(8,128)(2,1)S(1)} async-done(((bf16[8,64,128]{2,1,0:T(8,128)(2,1)}), bf16[8,64,128]{2,1,0:T(8,128)(2,1)S(1)}, u32[]{:S(2)}, u32[]{:S(2)}) %all-to-all-start) | async-done | bytes 131104 | tf_op jit(solution)/shard_map/all_to_all | solution.py:537
  71.5 2.5 %shard_map.98 = (bf16[8,32,128]{2,1,0:T(8,128)(2,1)S(1)}, f32[10,128]{1,0:T(8,128)S(1)}, f32[256,128]{1,0:T(8,128)S(1)}, f32[24,128]{1,0:T(8,128)S(1)}, bf16[304...) custom-call(bf16[8,64,128]{2,1,0:T(8,128)(2,1)S(1)} %all-to-all-done.got, ...), custom_call_target="tpu_custom_call" | custom-call | flops 40000000000 | bytes 1000000 | tf_op jit(solution)/shard_map/pallas_call | solution.py:24
  74.1 5.1 %collective-permute-start.6 = (bf16[304,128]{1,0:T(8,128)(2,1)S(1)}, bf16[304,128]{1,0:T(8,128)(2,1)S(1)}, u32[]{:S(2)}, u32[]{:S(2)}) collective-permute-start(bf16[304,128]{1,0:T(8,128)(2,1)S(1)} %get-tuple-element.70), channel_id=1, source_target_pairs={{0,2},{2,0},{4,6},{6,4},{8,10},{10,8},{12,14},{14,12},{16,18},{18,... | collective-permute-start | bytes 233480 | tf_op jit(solution)/shard_map/ppermute | solution.py:532
  79.2 1.9 %collective-permute-start.7 = (bf16[304,128]{1,0:T(8,128)(2,1)S(1)}, bf16[304,128]{1,0:T(8,128)(2,1)S(1)}, u32[]{:S(2)}, u32[]{:S(2)}) collective-permute-start(bf16[304,128]{1,0:T(8,128)(2,1)S(1)} %get-tuple-element.71), channel_id=1, source_target_pairs={{0,4},{2,6},{4,0},{6,2},{8,12},{10,14},{12,8},{14,10},{16,20},{18,... | collective-permute-start | bytes 233480 | tf_op jit(solution)/shard_map/ppermute | solution.py:532
  81.0 1.0 collective-permute-start.8
  82.1 1.2 collective-permute-done.7.c2
  83.3 2.9 %collective-permute-done.8.c3 = bf16[304,128]{1,0:T(8,128)(2,1)S(1)} collective-permute-done((bf16[304,128]{1,0:T(8,128)(2,1)S(1)}, bf16[304,128]{1,0:T(8,128)(2,1)S(1)}, u32[]{:S(2)}, u32[]{:S(2)}) %collective-permute-start.8) | collective-permute-done | bytes 77856 | tf_op jit(solution)/shard_map/ppermute | solution.py:532
  86.3 32.1 %all_to_all.15.got = bf16[8,72,128]{2,1,0:T(8,128)(2,1)S(1)} all-to-all(bf16[8,72,128]{2,1,0:T(8,128)(2,1)S(1)} %shard_map.99), channel_id=1, replica_groups={{0,8,16,24,32,40,48,56},{2,10,18,26,34,42,50,58},{4,12,20,28,36,44,52,6..., dimensions={0} | all-to-all | bytes 294912 | tf_op jit(solution)/shard_map/all_to_all | solution.py:537
  118.8 5.4 %collective-permute-start.10 = (bf16[256,128]{1,0:T(8,128)(2,1)S(1)}, bf16[256,128]{1,0:T(8,128)(2,1)S(1)}, u32[]{:S(2)}, u32[]{:S(2)}) collective-permute-start(bf16[256,128]{1,0:T(8,128)(2,1)S(1)} %get-tuple-element.76), channel_id=1, source_target_pairs={{0,4},{2,6},{4,0},{6,2},{8,12},{10,14},{12,8},{14,10},{16,20},{18,... | collective-permute-start | bytes 196616 | tf_op jit(solution)/shard_map/ppermute | solution.py:532
  124.1 1.0 collective-permute-start.11
  125.9 3.5 %collective-permute-done.11.e3 = bf16[256,128]{1,0:T(8,128)(2,1)S(1)} collective-permute-done((bf16[256,128]{1,0:T(8,128)(2,1)S(1)}, bf16[256,128]{1,0:T(8,128)(2,1)S(1)}, u32[]{:S(2)}, u32[]{:S(2)}) %collective-permute-start.11) | collective-permute-done | bytes 65568 | tf_op jit(solution)/shard_map/ppermute | solution.py:532
  129.4 2.9 %shard_map.102 = (bf16[2,128,1280]{2,1,0:T(8,128)(2,1)S(1)}, bf16[2,128,1280]{2,1,0:T(8,128)(2,1)S(1)}, bf16[8,48,128]{2,1,0:T(8,128)(2,1)}, f32[10,128]{1,0:T(8,128)S(1)}) custom-call(bf16[256,128]{1,0:T(8,128)(2,1)S(1)} %collective-permute-done.9.e1, bf16[256,128]{1,0:T(8,128)(2,1)S(1)} %collective-permute-done.10.e2, ...), custom_call_target="tpu_custom_call" | custom-call | flops 40000000000 | bytes 1000000 | tf_op jit(solution)/shard_map/pallas_call | solution.py:24
  132.3 0.9 copy-done.17
  133.2 3.6 %collective-permute-start.12 = (bf16[2,128,1280]{2,1,0:T(8,128)(2,1)S(1)}, bf16[2,128,1280]{2,1,0:T(8,128)(2,1)S(1)}, u32[]{:S(2)}, u32[]{:S(2)}) collective-permute-start(bf16[2,128,1280]{2,1,0:T(8,128)(2,1)S(1)} %get-tuple-element.84), channel_id=1, source_target_pairs={{0,1},{1,0},{2,3},{3,2},{4,5},{5,4},{6,7},{7,6},{8,9},{9,8},{10,11... | collective-permute-start | bytes 1966088 | tf_op jit(solution)/shard_map/ppermute | solution.py:528
  136.8 3.6 %all-to-all-start.2 = ((bf16[8,48,128]{2,1,0:T(8,128)(2,1)}), bf16[8,48,128]{2,1,0:T(8,128)(2,1)S(1)}, u32[]{:S(2)}, u32[]{:S(2)}) async-start(bf16[8,48,128]{2,1,0:T(8,128)(2,1)} %get-tuple-element.87), calls=%async_computation.2 | async-start | bytes 196608 | tf_op jit(solution)/shard_map/all_to_all | solution.py:537
  140.4 1.1 copy-done.18
  141.5 1.5 shard_map.103
  143.0 24.1 %all-to-all-done.2.got = bf16[8,48,128]{2,1,0:T(8,128)(2,1)S(1)} async-done(((bf16[8,48,128]{2,1,0:T(8,128)(2,1)}), bf16[8,48,128]{2,1,0:T(8,128)(2,1)S(1)}, u32[]{:S(2)}, u32[]{:S(2)}) %all-to-all-start.2) | async-done | bytes 98336 | tf_op jit(solution)/shard_map/all_to_all | solution.py:537
  167.7 3.3 %collective-permute-start.16 = (bf16[328,128]{1,0:T(8,128)(2,1)S(1)}, bf16[328,128]{1,0:T(8,128)(2,1)S(1)}, u32[]{:S(2)}, u32[]{:S(2)}) collective-permute-start(bf16[328,128]{1,0:T(8,128)(2,1)S(1)} %get-tuple-element.92), channel_id=1, source_target_pairs={{0,4},{2,6},{4,0},{6,2},{8,12},{10,14},{12,8},{14,10},{16,20},{18,... | collective-permute-start | bytes 251912 | tf_op jit(solution)/shard_map/ppermute | solution.py:532
  171.0 1.0 collective-permute-start.18
  172.0 1.1 collective-permute-start.20
  174.0 6.2 %collective-permute-start.17 = (bf16[328,128]{1,0:T(8,128)(2,1)S(1)}, bf16[328,128]{1,0:T(8,128)(2,1)S(1)}, u32[]{:S(2)}, u32[]{:S(2)}) collective-permute-start(bf16[328,128]{1,0:T(8,128)(2,1)S(1)} %collective-permute-done.16.g2), channel_id=1, source_target_pairs={{0,1},{1,0},{2,3},{3,2},{4,5},{5,4},{6,7},{7,6},{8,9},{9,8},{10,11... | collective-permute-start | bytes 251912 | tf_op jit(solution)/shard_map/ppermute | solution.py:528
  181.5 2.0 %shard_map.106 = (bf16[128,2240]{1,0:T(8,128)(2,1)}, bf16[128,2240]{1,0:T(8,128)(2,1)}, f32[3,3,2240]{2,1,0:T(4,128)}) custom-call(bf16[328,128]{1,0:T(8,128)(2,1)S(1)} %collective-permute-done.13.o0, bf16[328,128]{1,0:T(8,128)(2,1)S(1)} %collective-permute-done.15.o1, bf16[328,128]{1,0:T(8,128)(2,1)S(1)} %collective-permute-done.17.o2, ...), custom_call_target="tpu_custom_call" | custom-call | flops 20000000000 | bytes 1000000 | tf_op jit(solution)/shard_map/pallas_call | solution.py:24
  (68 shorter events, 10.1 us)
Async XLA Ops:
  1.7 21.0 %copy-start.1 = (bf16[1,4,32,2240]{3,2,1,0:T(8,128)(2,1)S(1)}, bf16[1,4,32,2240]{3,2,1,0:T(8,128)(2,1)}, u32[]{:S(2)}) copy-start(bf16[1,4,32,2240]{3,2,1,0:T(8,128)(2,1)} %param.7) | copy-start | bytes 1720324
  2.1 20.9 %copy-start.4 = (bf16[1,128,1280]{2,1,0:T(8,128)(2,1)}, bf16[1,128,1280]{2,1,0:T(8,128)(2,1)S(1)}, u32[]{:S(2)}) copy-start(bf16[1,128,1280]{2,1,0:T(8,128)(2,1)S(1)} %get-tuple-element.54.send_k) | copy-start | bytes 983044
  2.1 22.8 %copy-start.9 = (bf16[1,128,1280]{2,1,0:T(8,128)(2,1)}, bf16[1,128,1280]{2,1,0:T(8,128)(2,1)S(1)}, u32[]{:S(2)}) copy-start(bf16[1,128,1280]{2,1,0:T(8,128)(2,1)S(1)} %get-tuple-element.53.keep_k) | copy-start | bytes 983044
  2.2 22.2 %collective-permute-start = (bf16[1,128,1280]{2,1,0:T(8,128)(2,1)S(1)}, bf16[1,128,1280]{2,1,0:T(8,128)(2,1)S(1)}, u32[]{:S(2)}, u32[]{:S(2)}) collective-permute-start(bf16[1,128,1280]{2,1,0:T(8,128)(2,1)S(1)} %get-tuple-element.54.send_k), channel_id=1, source_target_pairs={{0,1},{1,0},{2,3},{3,2},{4,5},{5,4},{6,7},{7,6},{8,9},{9,8},{10,11... | collective-permute-start | bytes 983048 | tf_op jit(solution)/shard_map/ppermute | solution.py:528
  23.1 1.9 %collective-permute-start.1 = (bf16[1,128,1280]{2,1,0:T(8,128)(2,1)S(1)}, bf16[1,128,1280]{2,1,0:T(8,128)(2,1)S(1)}, u32[]{:S(2)}, u32[]{:S(2)}) collective-permute-start(bf16[1,128,1280]{2,1,0:T(8,128)(2,1)S(1)} %get-tuple-element.56.send_v), channel_id=1, source_target_pairs={{0,1},{1,0},{2,3},{3,2},{4,5},{5,4},{6,7},{7,6},{8,9},{9,8},{10,11... | collective-permute-start | bytes 983048 | tf_op jit(solution)/shard_map/ppermute | solution.py:528
  24.9 4.5 %copy-start.3 = (bf16[1,4,32,2240]{3,2,1,0:T(8,128)(2,1)S(1)}, bf16[1,4,32,2240]{3,2,1,0:T(8,128)(2,1)}, u32[]{:S(2)}) copy-start(bf16[1,4,32,2240]{3,2,1,0:T(8,128)(2,1)} %param.8) | copy-start | bytes 1720324
  24.9 4.5 %copy-start.8 = (f32[3,3,2240]{2,1,0:T(4,128)S(1)}, f32[3,3,2240]{2,1,0:T(4,128)}, u32[]{:S(2)}) copy-start(f32[3,3,2240]{2,1,0:T(4,128)} %taps.1) | copy-start | bytes 241924
  25.7 5.9 %collective-permute-start.2 = (bf16[288,128]{1,0:T(8,128)(2,1)S(1)}, bf16[288,128]{1,0:T(8,128)(2,1)S(1)}, u32[]{:S(2)}, u32[]{:S(2)}) collective-permute-start(bf16[288,128]{1,0:T(8,128)(2,1)S(1)} %get-tuple-element.60), channel_id=1, source_target_pairs={{0,2},{2,0},{4,6},{6,4},{8,10},{10,8},{12,14},{14,12},{16,18},{18,... | collective-permute-start | bytes 221192 | tf_op jit(solution)/shard_map/ppermute | solution.py:532
  25.9 5.7 %collective-permute-start.3 = (bf16[288,128]{1,0:T(8,128)(2,1)S(1)}, bf16[288,128]{1,0:T(8,128)(2,1)S(1)}, u32[]{:S(2)}, u32[]{:S(2)}) collective-permute-start(bf16[288,128]{1,0:T(8,128)(2,1)S(1)} %get-tuple-element.61), channel_id=1, source_target_pairs={{0,4},{2,6},{4,0},{6,2},{8,12},{10,14},{12,8},{14,10},{16,20},{18,... | collective-permute-start | bytes 221192 | tf_op jit(solution)/shard_map/ppermute | solution.py:532
  26.0 6.5 %collective-permute-start.4 = (bf16[288,128]{1,0:T(8,128)(2,1)S(1)}, bf16[288,128]{1,0:T(8,128)(2,1)S(1)}, u32[]{:S(2)}, u32[]{:S(2)}) collective-permute-start(bf16[288,128]{1,0:T(8,128)(2,1)S(1)} %get-tuple-element.62), channel_id=1, source_target_pairs={{0,6},{2,4},{4,2},{6,0},{8,14},{10,12},{12,10},{14,8},{16,22},{18,... | collective-permute-start | bytes 221192 | tf_op jit(solution)/shard_map/ppermute | solution.py:532
  30.3 17.1 %collective-permute-start.5 = (bf16[2,128,1280]{2,1,0:T(8,128)(2,1)S(1)}, bf16[2,128,1280]{2,1,0:T(8,128)(2,1)S(1)}, u32[]{:S(2)}, u32[]{:S(2)}) collective-permute-start(bf16[2,128,1280]{2,1,0:T(8,128)(2,1)S(1)} %get-tuple-element.66), channel_id=1, source_target_pairs={{0,1},{1,0},{2,3},{3,2},{4,5},{5,4},{6,7},{7,6},{8,9},{9,8},{10,11... | collective-permute-start | bytes 1966088 | tf_op jit(solution)/shard_map/ppermute | solution.py:528
  34.0 37.5 %all-to-all-start = ((bf16[8,64,128]{2,1,0:T(8,128)(2,1)}), bf16[8,64,128]{2,1,0:T(8,128)(2,1)S(1)}, u32[]{:S(2)}, u32[]{:S(2)}) async-start(bf16[8,64,128]{2,1,0:T(8,128)(2,1)} %get-tuple-element.63), calls=%async_computation | async-start | bytes 262144 | tf_op jit(solution)/shard_map/all_to_all | solution.py:537
  74.1 8.0 %collective-permute-start.6 = (bf16[304,128]{1,0:T(8,128)(2,1)S(1)}, bf16[304,128]{1,0:T(8,128)(2,1)S(1)}, u32[]{:S(2)}, u32[]{:S(2)}) collective-permute-start(bf16[304,128]{1,0:T(8,128)(2,1)S(1)} %get-tuple-element.70), channel_id=1, source_target_pairs={{0,2},{2,0},{4,6},{6,4},{8,10},{10,8},{12,14},{14,12},{16,18},{18,... | collective-permute-start | bytes 233480 | tf_op jit(solution)/shard_map/ppermute | solution.py:532
  79.2 4.1 %collective-permute-start.7 = (bf16[304,128]{1,0:T(8,128)(2,1)S(1)}, bf16[304,128]{1,0:T(8,128)(2,1)S(1)}, u32[]{:S(2)}, u32[]{:S(2)}) collective-permute-start(bf16[304,128]{1,0:T(8,128)(2,1)S(1)} %get-tuple-element.71), channel_id=1, source_target_pairs={{0,4},{2,6},{4,0},{6,2},{8,12},{10,14},{12,8},{14,10},{16,20},{18,... | collective-permute-start | bytes 233480 | tf_op jit(solution)/shard_map/ppermute | solution.py:532
  81.0 5.1 %collective-permute-start.8 = (bf16[304,128]{1,0:T(8,128)(2,1)S(1)}, bf16[304,128]{1,0:T(8,128)(2,1)S(1)}, u32[]{:S(2)}, u32[]{:S(2)}) collective-permute-start(bf16[304,128]{1,0:T(8,128)(2,1)S(1)} %get-tuple-element.72), channel_id=1, source_target_pairs={{0,6},{2,4},{4,2},{6,0},{8,14},{10,12},{12,10},{14,8},{16,22},{18,... | collective-permute-start | bytes 233480 | tf_op jit(solution)/shard_map/ppermute | solution.py:532
  118.5 7.4 %collective-permute-start.9 = (bf16[256,128]{1,0:T(8,128)(2,1)S(1)}, bf16[256,128]{1,0:T(8,128)(2,1)S(1)}, u32[]{:S(2)}, u32[]{:S(2)}) collective-permute-start(bf16[256,128]{1,0:T(8,128)(2,1)S(1)} %get-tuple-element.75), channel_id=1, source_target_pairs={{0,2},{2,0},{4,6},{6,4},{8,10},{10,8},{12,14},{14,12},{16,18},{18,... | collective-permute-start | bytes 196616 | tf_op jit(solution)/shard_map/ppermute | solution.py:532
  118.8 7.2 %collective-permute-start.10 = (bf16[256,128]{1,0:T(8,128)(2,1)S(1)}, bf16[256,128]{1,0:T(8,128)(2,1)S(1)}, u32[]{:S(2)}, u32[]{:S(2)}) collective-permute-start(bf16[256,128]{1,0:T(8,128)(2,1)S(1)} %get-tuple-element.76), channel_id=1, source_target_pairs={{0,4},{2,6},{4,0},{6,2},{8,12},{10,14},{12,8},{14,10},{16,20},{18,... | collective-permute-start | bytes 196616 | tf_op jit(solution)/shard_map/ppermute | solution.py:532
  124.1 5.3 %copy-start.14 = (f32[256,1280]{1,0:T(8,128)S(1)}, f32[256,1280]{1,0:T(8,128)}, u32[]{:S(2)}) copy-start(f32[256,1280]{1,0:T(8,128)} %copy-done.13) | copy-start | bytes 3932164
  124.1 5.3 %collective-permute-start.11 = (bf16[256,128]{1,0:T(8,128)(2,1)S(1)}, bf16[256,128]{1,0:T(8,128)(2,1)S(1)}, u32[]{:S(2)}, u32[]{:S(2)}) collective-permute-start(bf16[256,128]{1,0:T(8,128)(2,1)S(1)} %get-tuple-element.77), channel_id=1, source_target_pairs={{0,6},{2,4},{4,2},{6,0},{8,14},{10,12},{12,10},{14,8},{16,22},{18,... | collective-permute-start | bytes 196616 | tf_op jit(solution)/shard_map/ppermute | solution.py:532
  133.2 7.2 %collective-permute-start.12 = (bf16[2,128,1280]{2,1,0:T(8,128)(2,1)S(1)}, bf16[2,128,1280]{2,1,0:T(8,128)(2,1)S(1)}, u32[]{:S(2)}, u32[]{:S(2)}) collective-permute-start(bf16[2,128,1280]{2,1,0:T(8,128)(2,1)S(1)} %get-tuple-element.84), channel_id=1, source_target_pairs={{0,1},{1,0},{2,3},{3,2},{4,5},{5,4},{6,7},{7,6},{8,9},{9,8},{10,11... | collective-permute-start | bytes 1966088 | tf_op jit(solution)/shard_map/ppermute | solution.py:528
  136.8 30.3 %all-to-all-start.2 = ((bf16[8,48,128]{2,1,0:T(8,128)(2,1)}), bf16[8,48,128]{2,1,0:T(8,128)(2,1)S(1)}, u32[]{:S(2)}, u32[]{:S(2)}) async-start(bf16[8,48,128]{2,1,0:T(8,128)(2,1)} %get-tuple-element.87), calls=%async_computation.2 | async-start | bytes 196608 | tf_op jit(solution)/shard_map/all_to_all | solution.py:537
  167.1 13.2 %copy-start.10 = (bf16[1,128,1280]{2,1,0:T(8,128)(2,1)S(1)}, bf16[1,128,1280]{2,1,0:T(8,128)(2,1)}, u32[]{:S(2)}) copy-start(bf16[1,128,1280]{2,1,0:T(8,128)(2,1)} %copy-done.9) | copy-start | bytes 983044
  167.1 13.2 %copy-start.12 = (bf16[1,128,1280]{2,1,0:T(8,128)(2,1)S(1)}, bf16[1,128,1280]{2,1,0:T(8,128)(2,1)}, u32[]{:S(2)}) copy-start(bf16[1,128,1280]{2,1,0:T(8,128)(2,1)} %copy-done.11) | copy-start | bytes 983044
  167.1 13.2 %copy-start.16 = (f32[128,1280]{1,0:T(8,128)S(1)}, f32[128,1280]{1,0:T(8,128)}, u32[]{:S(2)}) copy-start(f32[128,1280]{1,0:T(8,128)} %copy-done.15) | copy-start | bytes 1966084
  167.3 5.9 %collective-permute-start.14 = (bf16[328,128]{1,0:T(8,128)(2,1)S(1)}, bf16[328,128]{1,0:T(8,128)(2,1)S(1)}, u32[]{:S(2)}, u32[]{:S(2)}) collective-permute-start(bf16[328,128]{1,0:T(8,128)(2,1)S(1)} %get-tuple-element.91), channel_id=1, source_target_pairs={{0,2},{2,0},{4,6},{6,4},{8,10},{10,8},{12,14},{14,12},{16,18},{18,... | collective-permute-start | bytes 251912 | tf_op jit(solution)/shard_map/ppermute | solution.py:532
  167.7 6.4 %collective-permute-start.16 = (bf16[328,128]{1,0:T(8,128)(2,1)S(1)}, bf16[328,128]{1,0:T(8,128)(2,1)S(1)}, u32[]{:S(2)}, u32[]{:S(2)}) collective-permute-start(bf16[328,128]{1,0:T(8,128)(2,1)S(1)} %get-tuple-element.92), channel_id=1, source_target_pairs={{0,4},{2,6},{4,0},{6,2},{8,12},{10,14},{12,8},{14,10},{16,20},{18,... | collective-permute-start | bytes 251912 | tf_op jit(solution)/shard_map/ppermute | solution.py:532
  171.0 9.2 %collective-permute-start.18 = (bf16[328,128]{1,0:T(8,128)(2,1)S(1)}, bf16[328,128]{1,0:T(8,128)(2,1)S(1)}, u32[]{:S(2)}, u32[]{:S(2)}) collective-permute-start(bf16[328,128]{1,0:T(8,128)(2,1)S(1)} %get-tuple-element.93), channel_id=1, source_target_pairs={{0,6},{2,4},{4,2},{6,0},{8,14},{10,12},{12,10},{14,8},{16,22},{18,... | collective-permute-start | bytes 251912 | tf_op jit(solution)/shard_map/ppermute | solution.py:532
  172.0 8.8 %collective-permute-start.20 = (f32[128,1280]{1,0:T(8,128)S(1)}, f32[128,1280]{1,0:T(8,128)S(1)}, u32[]{:S(2)}, u32[]{:S(2)}) collective-permute-start(f32[128,1280]{1,0:T(8,128)S(1)} %get-tuple-element.94), channel_id=1, source_target_pairs={{0,1},{1,0},{2,3},{3,2},{4,5},{5,4},{6,7},{7,6},{8,9},{9,8},{10,11... | collective-permute-start | bytes 1966088 | tf_op jit(solution)/shard_map/ppermute | solution.py:528
  173.2 7.7 %collective-permute-start.13 = (bf16[328,128]{1,0:T(8,128)(2,1)S(1)}, bf16[328,128]{1,0:T(8,128)(2,1)S(1)}, u32[]{:S(2)}, u32[]{:S(2)}) collective-permute-start(bf16[328,128]{1,0:T(8,128)(2,1)S(1)} %get-tuple-element.90.g0), channel_id=1, source_target_pairs={{0,1},{1,0},{2,3},{3,2},{4,5},{5,4},{6,7},{7,6},{8,9},{9,8},{10,11... | collective-permute-start | bytes 251912 | tf_op jit(solution)/shard_map/ppermute | solution.py:528
  173.2 7.7 %collective-permute-start.15 = (bf16[328,128]{1,0:T(8,128)(2,1)S(1)}, bf16[328,128]{1,0:T(8,128)(2,1)S(1)}, u32[]{:S(2)}, u32[]{:S(2)}) collective-permute-start(bf16[328,128]{1,0:T(8,128)(2,1)S(1)} %collective-permute-done.14.g1), channel_id=1, source_target_pairs={{0,1},{1,0},{2,3},{3,2},{4,5},{5,4},{6,7},{7,6},{8,9},{9,8},{10,11... | collective-permute-start | bytes 251912 | tf_op jit(solution)/shard_map/ppermute | solution.py:528
  174.0 7.1 %collective-permute-start.17 = (bf16[328,128]{1,0:T(8,128)(2,1)S(1)}, bf16[328,128]{1,0:T(8,128)(2,1)S(1)}, u32[]{:S(2)}, u32[]{:S(2)}) collective-permute-start(bf16[328,128]{1,0:T(8,128)(2,1)S(1)} %collective-permute-done.16.g2), channel_id=1, source_target_pairs={{0,1},{1,0},{2,3},{3,2},{4,5},{5,4},{6,7},{7,6},{8,9},{9,8},{10,11... | collective-permute-start | bytes 251912 | tf_op jit(solution)/shard_map/ppermute | solution.py:528
  180.2 1.3 collective-permute-start.19
  (10 other events, 13.4 us)

commit v6 on v5

--- a/solution.py
+++ b/solution.py
@@ -293,7 +293,7 @@
         pay[b, m:, :] = block
 
 
-def rank_kernel(got, ksum, mean, a1, a2, a3, rank):
+def rank_kernel(got, ksum, mean, a1, a2, a3, kt, keep, recv, rank, recip):
     _, p, mine = place()
     n = ROWS // NEAR
     m = n // got.shape[0]
@@ -308,6 +308,7 @@
         means.append(mid)
     for i in range(HC):
         rank[HD * i : HD * (i + 1), :] = products(sums, means, i)
+        recip[:, col(i)] = reciprocal_of(both(keep, recv, 0, i), kt, i)
 
 
 def reciprocal_of(q, kt, i):
@@ -385,7 +386,7 @@
 
 
 def attend_kernel(
-    e1, e2, e3, s_own, rank, kt, keep, recv, local, taps_own, back, mine, other, pay, gks, state, rows
+    e1, e2, e3, s_own, rank, recips, kt, keep, recv, local, taps_own, back, mine, other, pay, gks, state, rows
 ):
     p = place()[1]
     nb = pay.shape[0]
@@ -402,7 +403,7 @@
     for i in range(HC):
         q, g = both(keep, recv, 0, i), both(keep, recv, 1, i)
         hi, lo = halves(pad_rows(mats[i] + rank[HD * i : HD * (i + 1), :]))
-        recip = reciprocal_of(q, key_total, i)
+        recip = recips[:, col(i)]
         out = mm(jnp.concatenate([q, q], axis=1), jnp.concatenate([hi, lo], axis=0), NN) * recip
         x = (out + local[:, col(i)]).astype(BF)
         mine[0, :, col(i)] = x[:half]
@@ -583,7 +584,11 @@
         [((nb, 2 * m + 8, LN), BF)],
         own_d, *got_c, down, taps_own, scratch=[((8, LN), F32)],
     )
-    (rank,) = call(rank_kernel, [((HC * HD, LN), F32)], got, ksum, mean, *got_a, us=2)
+    rank, recip = call(
+        rank_kernel,
+        [((HC * HD, LN), F32), ((2 * t, WC), F32)],
+        got, ksum, mean, *got_a, kt, keep_qg, recv_qg, us=2,
+    )
     got = far(pay)
     s_own, e1, e2, e3, taps_own, back = call(
         prefix_kernel,
@@ -594,7 +599,7 @@
     mine, other, pay, gks = call(
         attend_kernel,
         [pair, pair, ((nb, m + 16, LN), BF), row],
-        *got_e, s_own, rank, kt, keep_qg, recv_qg, local, taps_own, back,
+        *got_e, s_own, rank, recip, kt, keep_qg, recv_qg, local, taps_own, back,
         scratch=[state, ((16, LN), F32)], us=4,
     )
     got = far(pay)

time: 184 us -> 184 us (level)
  no operation moved by 1% of the time
where the time goes in v6:
time: 184 us; the launch traced here: 183 us
  starting transfers between devices  74.7 us (41%)
  waiting for transfers between devices  51.2 us (28%)
  blocking collectives  32.1 us (17%)
  Pallas kernels  18.1 us (10%)
  local copies, waits for them, and re-layouts  6.44 us (4%)
    all_to_all x2, waiting for transfers between devices, far(): return lax.all_to_all(x, 'tm', 0, 0, axis_index_groups=across, tiled=True)  42 us
    ppermute x9, starting transfers between devices, over(): return lax.ppermute(x, 'space', [(0, 1), (1, 0)])  34.2 us
    all_to_all x1, blocking collectives, far(): return lax.all_to_all(x, 'tm', 0, 0, axis_index_groups=across, tiled=True)  32.1 us
    ppermute x12, starting transfers between devices, near(): lax.ppermute(a, 'tm', [(i, i ^ k) for i in range(frames)])  23.6 us
    pallas_call x15, Pallas kernels, call(): pl.pallas_call(kernel, out_shape=[jax.ShapeDtypeStruct(s, d) for s, d in...  18.1 us
    all_to_all x2, starting transfers between devices, far(): return lax.all_to_all(x, 'tm', 0, 0, axis_index_groups=across, tiled=True)  16.9 us
    ppermute x12, waiting for transfers between devices, near(): lax.ppermute(a, 'tm', [(i, i ^ k) for i in range(frames)])  8.06 us
    unnamed x38, local copies, waits for them, and re-layouts  6.44 us
  transfers between devices with their start and end apart: 23, of which 9 were waited for; matrix products, arithmetic and copies ran while one was open for 0% of the time, Pallas kernels for 5%

profile of v6, /device:TPU:37, one launch (start us, length us, event | category | flops | bytes accessed | tf_op | source)
XLA Modules:
  0.0 183.4 jit_solution(13134690238736364400)
XLA Ops:
  0.6 1.1 copy-done
  2.2 20.5 %collective-permute-start = (bf16[1,128,1280]{2,1,0:T(8,128)(2,1)S(1)}, bf16[1,128,1280]{2,1,0:T(8,128)(2,1)S(1)}, u32[]{:S(2)}, u32[]{:S(2)}) collective-permute-start(bf16[1,128,1280]{2,1,0:T(8,128)(2,1)S(1)} %get-tuple-element.56.send_k), channel_id=1, source_target_pairs={{0,1},{1,0},{2,3},{3,2},{4,5},{5,4},{6,7},{7,6},{8,9},{9,8},{10,11... | collective-permute-start | bytes 983048 | tf_op jit(solution)/shard_map/ppermute | solution.py:529
  26.0 3.4 %collective-permute-start.4 = (bf16[288,128]{1,0:T(8,128)(2,1)S(1)}, bf16[288,128]{1,0:T(8,128)(2,1)S(1)}, u32[]{:S(2)}, u32[]{:S(2)}) collective-permute-start(bf16[288,128]{1,0:T(8,128)(2,1)S(1)} %get-tuple-element.64), channel_id=1, source_target_pairs={{0,6},{2,4},{4,2},{6,0},{8,14},{10,12},{12,10},{14,8},{16,22},{18,... | collective-permute-start | bytes 221192 | tf_op jit(solution)/shard_map/ppermute | solution.py:533
  30.3 1.3 collective-permute-start.5
  32.5 1.5 shard_map.95
  34.0 13.3 %all-to-all-start = ((bf16[8,64,128]{2,1,0:T(8,128)(2,1)}), bf16[8,64,128]{2,1,0:T(8,128)(2,1)S(1)}, u32[]{:S(2)}, u32[]{:S(2)}) async-start(bf16[8,64,128]{2,1,0:T(8,128)(2,1)} %get-tuple-element.65), calls=%async_computation | async-start | bytes 262144 | tf_op jit(solution)/shard_map/all_to_all | solution.py:538
  47.4 3.0 %shard_map.97 = (f32[256,1280]{1,0:T(8,128)S(1)}, f32[128,1280]{1,0:T(8,128)S(1)}, f32[128,1280]{1,0:T(8,128)S(1)}, f32[4,24,128]{2,1,0:T(8,128)S(1)}) custom-call(bf16[1,128,1280]{2,1,0:T(8,128)(2,1)S(1)} %get-tuple-element.57.keep_v, bf16[1,128,1280]{2,1,0:T(8,128)(2,1)S(1)} %collective-permute-done.1.recv_v, ...), custom_call_target="tpu_custom_call" | custom-call | flops 20000000000 | bytes 1000000 | tf_op jit(solution)/shard_map/pallas_call | solution.py:24
  51.1 1.1 copy-done.13
  53.1 18.5 %all-to-all-done.got = bf16[8,64,128]{2,1,0:T(8,128)(2,1)S(1)} async-done(((bf16[8,64,128]{2,1,0:T(8,128)(2,1)}), bf16[8,64,128]{2,1,0:T(8,128)(2,1)S(1)}, u32[]{:S(2)}, u32[]{:S(2)}) %all-to-all-start) | async-done | bytes 131104 | tf_op jit(solution)/shard_map/all_to_all | solution.py:538
  71.5 2.5 %shard_map.98 = (bf16[8,32,128]{2,1,0:T(8,128)(2,1)S(1)}, f32[10,128]{1,0:T(8,128)S(1)}, f32[256,128]{1,0:T(8,128)S(1)}, f32[24,128]{1,0:T(8,128)S(1)}, bf16[304...) custom-call(bf16[8,64,128]{2,1,0:T(8,128)(2,1)S(1)} %all-to-all-done.got, ...), custom_call_target="tpu_custom_call" | custom-call | flops 40000000000 | bytes 1000000 | tf_op jit(solution)/shard_map/pallas_call | solution.py:24
  74.1 5.1 %collective-permute-start.6 = (bf16[304,128]{1,0:T(8,128)(2,1)S(1)}, bf16[304,128]{1,0:T(8,128)(2,1)S(1)}, u32[]{:S(2)}, u32[]{:S(2)}) collective-permute-start(bf16[304,128]{1,0:T(8,128)(2,1)S(1)} %get-tuple-element.72), channel_id=1, source_target_pairs={{0,2},{2,0},{4,6},{6,4},{8,10},{10,8},{12,14},{14,12},{16,18},{18,... | collective-permute-start | bytes 233480 | tf_op jit(solution)/shard_map/ppermute | solution.py:533
  79.2 1.9 %collective-permute-start.7 = (bf16[304,128]{1,0:T(8,128)(2,1)S(1)}, bf16[304,128]{1,0:T(8,128)(2,1)S(1)}, u32[]{:S(2)}, u32[]{:S(2)}) collective-permute-start(bf16[304,128]{1,0:T(8,128)(2,1)S(1)} %get-tuple-element.73), channel_id=1, source_target_pairs={{0,4},{2,6},{4,0},{6,2},{8,12},{10,14},{12,8},{14,10},{16,20},{18,... | collective-permute-start | bytes 233480 | tf_op jit(solution)/shard_map/ppermute | solution.py:533
  81.0 1.0 collective-permute-start.8
  82.1 1.2 collective-permute-done.7.c2
  83.3 2.9 %collective-permute-done.8.c3 = bf16[304,128]{1,0:T(8,128)(2,1)S(1)} collective-permute-done((bf16[304,128]{1,0:T(8,128)(2,1)S(1)}, bf16[304,128]{1,0:T(8,128)(2,1)S(1)}, u32[]{:S(2)}, u32[]{:S(2)}) %collective-permute-start.8) | collective-permute-done | bytes 77856 | tf_op jit(solution)/shard_map/ppermute | solution.py:533
  86.3 32.1 %all_to_all.15.got = bf16[8,72,128]{2,1,0:T(8,128)(2,1)S(1)} all-to-all(bf16[8,72,128]{2,1,0:T(8,128)(2,1)S(1)} %shard_map.99), channel_id=1, replica_groups={{0,8,16,24,32,40,48,56},{2,10,18,26,34,42,50,58},{4,12,20,28,36,44,52,6..., dimensions={0} | all-to-all | bytes 294912 | tf_op jit(solution)/shard_map/all_to_all | solution.py:538
  118.8 5.4 %collective-permute-start.10 = (bf16[256,128]{1,0:T(8,128)(2,1)S(1)}, bf16[256,128]{1,0:T(8,128)(2,1)S(1)}, u32[]{:S(2)}, u32[]{:S(2)}) collective-permute-start(bf16[256,128]{1,0:T(8,128)(2,1)S(1)} %get-tuple-element.78), channel_id=1, source_target_pairs={{0,4},{2,6},{4,0},{6,2},{8,12},{10,14},{12,8},{14,10},{16,20},{18,... | collective-permute-start | bytes 196616 | tf_op jit(solution)/shard_map/ppermute | solution.py:533
  124.1 1.0 collective-permute-start.11
  125.2 1.2 shard_map.101
  126.4 3.0 %collective-permute-done.11.e3 = bf16[256,128]{1,0:T(8,128)(2,1)S(1)} collective-permute-done((bf16[256,128]{1,0:T(8,128)(2,1)S(1)}, bf16[256,128]{1,0:T(8,128)(2,1)S(1)}, u32[]{:S(2)}, u32[]{:S(2)}) %collective-permute-start.11) | collective-permute-done | bytes 65568 | tf_op jit(solution)/shard_map/ppermute | solution.py:533
  129.4 2.8 %shard_map.102 = (bf16[2,128,1280]{2,1,0:T(8,128)(2,1)S(1)}, bf16[2,128,1280]{2,1,0:T(8,128)(2,1)S(1)}, bf16[8,48,128]{2,1,0:T(8,128)(2,1)}, f32[10,128]{1,0:T(8,128)S(1)}) custom-call(bf16[256,128]{1,0:T(8,128)(2,1)S(1)} %collective-permute-done.9.e1, bf16[256,128]{1,0:T(8,128)(2,1)S(1)} %collective-permute-done.10.e2, ...), custom_call_target="tpu_custom_call" | custom-call | flops 40000000000 | bytes 1000000 | tf_op jit(solution)/shard_map/pallas_call | solution.py:24
  133.1 3.6 %collective-permute-start.12 = (bf16[2,128,1280]{2,1,0:T(8,128)(2,1)S(1)}, bf16[2,128,1280]{2,1,0:T(8,128)(2,1)S(1)}, u32[]{:S(2)}, u32[]{:S(2)}) collective-permute-start(bf16[2,128,1280]{2,1,0:T(8,128)(2,1)S(1)} %get-tuple-element.88), channel_id=1, source_target_pairs={{0,1},{1,0},{2,3},{3,2},{4,5},{5,4},{6,7},{7,6},{8,9},{9,8},{10,11... | collective-permute-start | bytes 1966088 | tf_op jit(solution)/shard_map/ppermute | solution.py:529
  136.7 3.6 %all-to-all-start.2 = ((bf16[8,48,128]{2,1,0:T(8,128)(2,1)}), bf16[8,48,128]{2,1,0:T(8,128)(2,1)S(1)}, u32[]{:S(2)}, u32[]{:S(2)}) async-start(bf16[8,48,128]{2,1,0:T(8,128)(2,1)} %get-tuple-element.91), calls=%async_computation.2 | async-start | bytes 196608 | tf_op jit(solution)/shard_map/all_to_all | solution.py:538
  140.3 1.1 copy-done.18
  141.4 1.5 shard_map.103
  142.9 23.5 %all-to-all-done.2.got = bf16[8,48,128]{2,1,0:T(8,128)(2,1)S(1)} async-done(((bf16[8,48,128]{2,1,0:T(8,128)(2,1)}), bf16[8,48,128]{2,1,0:T(8,128)(2,1)S(1)}, u32[]{:S(2)}, u32[]{:S(2)}) %all-to-all-start.2) | async-done | bytes 98336 | tf_op jit(solution)/shard_map/all_to_all | solution.py:538
  166.6 0.9 collective-permute-start.14
  167.6 3.3 %collective-permute-start.16 = (bf16[328,128]{1,0:T(8,128)(2,1)S(1)}, bf16[328,128]{1,0:T(8,128)(2,1)S(1)}, u32[]{:S(2)}, u32[]{:S(2)}) collective-permute-start(bf16[328,128]{1,0:T(8,128)(2,1)S(1)} %get-tuple-element.96), channel_id=1, source_target_pairs={{0,4},{2,6},{4,0},{6,2},{8,12},{10,14},{12,8},{14,10},{16,20},{18,... | collective-permute-start | bytes 251912 | tf_op jit(solution)/shard_map/ppermute | solution.py:533
  170.9 1.0 collective-permute-start.18
  171.9 1.2 collective-permute-start.20
  173.9 6.1 %collective-permute-start.17 = (bf16[328,128]{1,0:T(8,128)(2,1)S(1)}, bf16[328,128]{1,0:T(8,128)(2,1)S(1)}, u32[]{:S(2)}, u32[]{:S(2)}) collective-permute-start(bf16[328,128]{1,0:T(8,128)(2,1)S(1)} %collective-permute-done.16.g2), channel_id=1, source_target_pairs={{0,1},{1,0},{2,3},{3,2},{4,5},{5,4},{6,7},{7,6},{8,9},{9,8},{10,11... | collective-permute-start | bytes 251912 | tf_op jit(solution)/shard_map/ppermute | solution.py:529
  181.4 2.0 %shard_map.106 = (bf16[128,2240]{1,0:T(8,128)(2,1)}, bf16[128,2240]{1,0:T(8,128)(2,1)}, f32[3,3,2240]{2,1,0:T(4,128)}) custom-call(bf16[328,128]{1,0:T(8,128)(2,1)S(1)} %collective-permute-done.13.o0, bf16[328,128]{1,0:T(8,128)(2,1)S(1)} %collective-permute-done.15.o1, bf16[328,128]{1,0:T(8,128)(2,1)S(1)} %collective-permute-done.17.o2, ...), custom_call_target="tpu_custom_call" | custom-call | flops 20000000000 | bytes 1000000 | tf_op jit(solution)/shard_map/pallas_call | solution.py:24
  (68 shorter events, 10.8 us)
Async XLA Ops:
  1.7 21.0 %copy-start.1 = (bf16[1,4,32,2240]{3,2,1,0:T(8,128)(2,1)S(1)}, bf16[1,4,32,2240]{3,2,1,0:T(8,128)(2,1)}, u32[]{:S(2)}) copy-start(bf16[1,4,32,2240]{3,2,1,0:T(8,128)(2,1)} %param.7) | copy-start | bytes 1720324
  2.1 20.9 %copy-start.4 = (bf16[1,128,1280]{2,1,0:T(8,128)(2,1)}, bf16[1,128,1280]{2,1,0:T(8,128)(2,1)S(1)}, u32[]{:S(2)}) copy-start(bf16[1,128,1280]{2,1,0:T(8,128)(2,1)S(1)} %get-tuple-element.56.send_k) | copy-start | bytes 983044
  2.1 22.8 %copy-start.9 = (bf16[1,128,1280]{2,1,0:T(8,128)(2,1)}, bf16[1,128,1280]{2,1,0:T(8,128)(2,1)S(1)}, u32[]{:S(2)}) copy-start(bf16[1,128,1280]{2,1,0:T(8,128)(2,1)S(1)} %get-tuple-element.55.keep_k) | copy-start | bytes 983044
  2.2 22.2 %collective-permute-start = (bf16[1,128,1280]{2,1,0:T(8,128)(2,1)S(1)}, bf16[1,128,1280]{2,1,0:T(8,128)(2,1)S(1)}, u32[]{:S(2)}, u32[]{:S(2)}) collective-permute-start(bf16[1,128,1280]{2,1,0:T(8,128)(2,1)S(1)} %get-tuple-element.56.send_k), channel_id=1, source_target_pairs={{0,1},{1,0},{2,3},{3,2},{4,5},{5,4},{6,7},{7,6},{8,9},{9,8},{10,11... | collective-permute-start | bytes 983048 | tf_op jit(solution)/shard_map/ppermute | solution.py:529
  23.1 1.9 %collective-permute-start.1 = (bf16[1,128,1280]{2,1,0:T(8,128)(2,1)S(1)}, bf16[1,128,1280]{2,1,0:T(8,128)(2,1)S(1)}, u32[]{:S(2)}, u32[]{:S(2)}) collective-permute-start(bf16[1,128,1280]{2,1,0:T(8,128)(2,1)S(1)} %get-tuple-element.58.send_v), channel_id=1, source_target_pairs={{0,1},{1,0},{2,3},{3,2},{4,5},{5,4},{6,7},{7,6},{8,9},{9,8},{10,11... | collective-permute-start | bytes 983048 | tf_op jit(solution)/shard_map/ppermute | solution.py:529
  24.9 4.5 %copy-start.2 = (bf16[1,4,32,2240]{3,2,1,0:T(8,128)(2,1)S(1)}, bf16[1,4,32,2240]{3,2,1,0:T(8,128)(2,1)}, u32[]{:S(2)}) copy-start(bf16[1,4,32,2240]{3,2,1,0:T(8,128)(2,1)} %param.5) | copy-start | bytes 1720324
  24.9 4.5 %copy-start.3 = (bf16[1,4,32,2240]{3,2,1,0:T(8,128)(2,1)S(1)}, bf16[1,4,32,2240]{3,2,1,0:T(8,128)(2,1)}, u32[]{:S(2)}) copy-start(bf16[1,4,32,2240]{3,2,1,0:T(8,128)(2,1)} %param.8) | copy-start | bytes 1720324
  24.9 4.5 %copy-start.8 = (f32[3,3,2240]{2,1,0:T(4,128)S(1)}, f32[3,3,2240]{2,1,0:T(4,128)}, u32[]{:S(2)}) copy-start(f32[3,3,2240]{2,1,0:T(4,128)} %taps.1) | copy-start | bytes 241924
  25.7 5.9 %collective-permute-start.2 = (bf16[288,128]{1,0:T(8,128)(2,1)S(1)}, bf16[288,128]{1,0:T(8,128)(2,1)S(1)}, u32[]{:S(2)}, u32[]{:S(2)}) collective-permute-start(bf16[288,128]{1,0:T(8,128)(2,1)S(1)} %get-tuple-element.62), channel_id=1, source_target_pairs={{0,2},{2,0},{4,6},{6,4},{8,10},{10,8},{12,14},{14,12},{16,18},{18,... | collective-permute-start | bytes 221192 | tf_op jit(solution)/shard_map/ppermute | solution.py:533
  25.9 5.7 %collective-permute-start.3 = (bf16[288,128]{1,0:T(8,128)(2,1)S(1)}, bf16[288,128]{1,0:T(8,128)(2,1)S(1)}, u32[]{:S(2)}, u32[]{:S(2)}) collective-permute-start(bf16[288,128]{1,0:T(8,128)(2,1)S(1)} %get-tuple-element.63), channel_id=1, source_target_pairs={{0,4},{2,6},{4,0},{6,2},{8,12},{10,14},{12,8},{14,10},{16,20},{18,... | collective-permute-start | bytes 221192 | tf_op jit(solution)/shard_map/ppermute | solution.py:533
  26.0 6.5 %collective-permute-start.4 = (bf16[288,128]{1,0:T(8,128)(2,1)S(1)}, bf16[288,128]{1,0:T(8,128)(2,1)S(1)}, u32[]{:S(2)}, u32[]{:S(2)}) collective-permute-start(bf16[288,128]{1,0:T(8,128)(2,1)S(1)} %get-tuple-element.64), channel_id=1, source_target_pairs={{0,6},{2,4},{4,2},{6,0},{8,14},{10,12},{12,10},{14,8},{16,22},{18,... | collective-permute-start | bytes 221192 | tf_op jit(solution)/shard_map/ppermute | solution.py:533
  30.3 17.1 %collective-permute-start.5 = (bf16[2,128,1280]{2,1,0:T(8,128)(2,1)S(1)}, bf16[2,128,1280]{2,1,0:T(8,128)(2,1)S(1)}, u32[]{:S(2)}, u32[]{:S(2)}) collective-permute-start(bf16[2,128,1280]{2,1,0:T(8,128)(2,1)S(1)} %get-tuple-element.68), channel_id=1, source_target_pairs={{0,1},{1,0},{2,3},{3,2},{4,5},{5,4},{6,7},{7,6},{8,9},{9,8},{10,11... | collective-permute-start | bytes 1966088 | tf_op jit(solution)/shard_map/ppermute | solution.py:529
  34.0 37.5 %all-to-all-start = ((bf16[8,64,128]{2,1,0:T(8,128)(2,1)}), bf16[8,64,128]{2,1,0:T(8,128)(2,1)S(1)}, u32[]{:S(2)}, u32[]{:S(2)}) async-start(bf16[8,64,128]{2,1,0:T(8,128)(2,1)} %get-tuple-element.65), calls=%async_computation | async-start | bytes 262144 | tf_op jit(solution)/shard_map/all_to_all | solution.py:538
  74.1 8.0 %collective-permute-start.6 = (bf16[304,128]{1,0:T(8,128)(2,1)S(1)}, bf16[304,128]{1,0:T(8,128)(2,1)S(1)}, u32[]{:S(2)}, u32[]{:S(2)}) collective-permute-start(bf16[304,128]{1,0:T(8,128)(2,1)S(1)} %get-tuple-element.72), channel_id=1, source_target_pairs={{0,2},{2,0},{4,6},{6,4},{8,10},{10,8},{12,14},{14,12},{16,18},{18,... | collective-permute-start | bytes 233480 | tf_op jit(solution)/shard_map/ppermute | solution.py:533
  79.2 4.1 %collective-permute-start.7 = (bf16[304,128]{1,0:T(8,128)(2,1)S(1)}, bf16[304,128]{1,0:T(8,128)(2,1)S(1)}, u32[]{:S(2)}, u32[]{:S(2)}) collective-permute-start(bf16[304,128]{1,0:T(8,128)(2,1)S(1)} %get-tuple-element.73), channel_id=1, source_target_pairs={{0,4},{2,6},{4,0},{6,2},{8,12},{10,14},{12,8},{14,10},{16,20},{18,... | collective-permute-start | bytes 233480 | tf_op jit(solution)/shard_map/ppermute | solution.py:533
  81.0 5.1 %collective-permute-start.8 = (bf16[304,128]{1,0:T(8,128)(2,1)S(1)}, bf16[304,128]{1,0:T(8,128)(2,1)S(1)}, u32[]{:S(2)}, u32[]{:S(2)}) collective-permute-start(bf16[304,128]{1,0:T(8,128)(2,1)S(1)} %get-tuple-element.74), channel_id=1, source_target_pairs={{0,6},{2,4},{4,2},{6,0},{8,14},{10,12},{12,10},{14,8},{16,22},{18,... | collective-permute-start | bytes 233480 | tf_op jit(solution)/shard_map/ppermute | solution.py:533
  118.5 7.9 %collective-permute-start.9 = (bf16[256,128]{1,0:T(8,128)(2,1)S(1)}, bf16[256,128]{1,0:T(8,128)(2,1)S(1)}, u32[]{:S(2)}, u32[]{:S(2)}) collective-permute-start(bf16[256,128]{1,0:T(8,128)(2,1)S(1)} %get-tuple-element.77), channel_id=1, source_target_pairs={{0,2},{2,0},{4,6},{6,4},{8,10},{10,8},{12,14},{14,12},{16,18},{18,... | collective-permute-start | bytes 196616 | tf_op jit(solution)/shard_map/ppermute | solution.py:533
  118.8 7.7 %collective-permute-start.10 = (bf16[256,128]{1,0:T(8,128)(2,1)S(1)}, bf16[256,128]{1,0:T(8,128)(2,1)S(1)}, u32[]{:S(2)}, u32[]{:S(2)}) collective-permute-start(bf16[256,128]{1,0:T(8,128)(2,1)S(1)} %get-tuple-element.78), channel_id=1, source_target_pairs={{0,4},{2,6},{4,0},{6,2},{8,12},{10,14},{12,8},{14,10},{16,20},{18,... | collective-permute-start | bytes 196616 | tf_op jit(solution)/shard_map/ppermute | solution.py:533
  124.1 5.3 %collective-permute-start.11 = (bf16[256,128]{1,0:T(8,128)(2,1)S(1)}, bf16[256,128]{1,0:T(8,128)(2,1)S(1)}, u32[]{:S(2)}, u32[]{:S(2)}) collective-permute-start(bf16[256,128]{1,0:T(8,128)(2,1)S(1)} %get-tuple-element.79), channel_id=1, source_target_pairs={{0,6},{2,4},{4,2},{6,0},{8,14},{10,12},{12,10},{14,8},{16,22},{18,... | collective-permute-start | bytes 196616 | tf_op jit(solution)/shard_map/ppermute | solution.py:533
  133.1 7.2 %collective-permute-start.12 = (bf16[2,128,1280]{2,1,0:T(8,128)(2,1)S(1)}, bf16[2,128,1280]{2,1,0:T(8,128)(2,1)S(1)}, u32[]{:S(2)}, u32[]{:S(2)}) collective-permute-start(bf16[2,128,1280]{2,1,0:T(8,128)(2,1)S(1)} %get-tuple-element.88), channel_id=1, source_target_pairs={{0,1},{1,0},{2,3},{3,2},{4,5},{5,4},{6,7},{7,6},{8,9},{9,8},{10,11... | collective-permute-start | bytes 1966088 | tf_op jit(solution)/shard_map/ppermute | solution.py:529
  136.7 29.7 %all-to-all-start.2 = ((bf16[8,48,128]{2,1,0:T(8,128)(2,1)}), bf16[8,48,128]{2,1,0:T(8,128)(2,1)S(1)}, u32[]{:S(2)}, u32[]{:S(2)}) async-start(bf16[8,48,128]{2,1,0:T(8,128)(2,1)} %get-tuple-element.91), calls=%async_computation.2 | async-start | bytes 196608 | tf_op jit(solution)/shard_map/all_to_all | solution.py:538
  166.4 13.7 %copy-start.10 = (bf16[1,128,1280]{2,1,0:T(8,128)(2,1)S(1)}, bf16[1,128,1280]{2,1,0:T(8,128)(2,1)}, u32[]{:S(2)}) copy-start(bf16[1,128,1280]{2,1,0:T(8,128)(2,1)} %copy-done.9) | copy-start | bytes 983044
  166.4 13.7 %copy-start.12 = (bf16[1,128,1280]{2,1,0:T(8,128)(2,1)S(1)}, bf16[1,128,1280]{2,1,0:T(8,128)(2,1)}, u32[]{:S(2)}) copy-start(bf16[1,128,1280]{2,1,0:T(8,128)(2,1)} %copy-done.11) | copy-start | bytes 983044
  166.4 13.7 %copy-start.16 = (f32[128,1280]{1,0:T(8,128)S(1)}, f32[128,1280]{1,0:T(8,128)}, u32[]{:S(2)}) copy-start(f32[128,1280]{1,0:T(8,128)} %copy-done.15) | copy-start | bytes 1966084
  166.6 6.5 %collective-permute-start.14 = (bf16[328,128]{1,0:T(8,128)(2,1)S(1)}, bf16[328,128]{1,0:T(8,128)(2,1)S(1)}, u32[]{:S(2)}, u32[]{:S(2)}) collective-permute-start(bf16[328,128]{1,0:T(8,128)(2,1)S(1)} %get-tuple-element.95), channel_id=1, source_target_pairs={{0,2},{2,0},{4,6},{6,4},{8,10},{10,8},{12,14},{14,12},{16,18},{18,... | collective-permute-start | bytes 251912 | tf_op jit(solution)/shard_map/ppermute | solution.py:533
  167.6 6.4 %collective-permute-start.16 = (bf16[328,128]{1,0:T(8,128)(2,1)S(1)}, bf16[328,128]{1,0:T(8,128)(2,1)S(1)}, u32[]{:S(2)}, u32[]{:S(2)}) collective-permute-start(bf16[328,128]{1,0:T(8,128)(2,1)S(1)} %get-tuple-element.96), channel_id=1, source_target_pairs={{0,4},{2,6},{4,0},{6,2},{8,12},{10,14},{12,8},{14,10},{16,20},{18,... | collective-permute-start | bytes 251912 | tf_op jit(solution)/shard_map/ppermute | solution.py:533
  170.9 9.2 %collective-permute-start.18 = (bf16[328,128]{1,0:T(8,128)(2,1)S(1)}, bf16[328,128]{1,0:T(8,128)(2,1)S(1)}, u32[]{:S(2)}, u32[]{:S(2)}) collective-permute-start(bf16[328,128]{1,0:T(8,128)(2,1)S(1)} %get-tuple-element.97), channel_id=1, source_target_pairs={{0,6},{2,4},{4,2},{6,0},{8,14},{10,12},{12,10},{14,8},{16,22},{18,... | collective-permute-start | bytes 251912 | tf_op jit(solution)/shard_map/ppermute | solution.py:533
  171.9 8.8 %collective-permute-start.20 = (f32[128,1280]{1,0:T(8,128)S(1)}, f32[128,1280]{1,0:T(8,128)S(1)}, u32[]{:S(2)}, u32[]{:S(2)}) collective-permute-start(f32[128,1280]{1,0:T(8,128)S(1)} %get-tuple-element.98), channel_id=1, source_target_pairs={{0,1},{1,0},{2,3},{3,2},{4,5},{5,4},{6,7},{7,6},{8,9},{9,8},{10,11... | collective-permute-start | bytes 1966088 | tf_op jit(solution)/shard_map/ppermute | solution.py:529
  173.1 7.6 %collective-permute-start.13 = (bf16[328,128]{1,0:T(8,128)(2,1)S(1)}, bf16[328,128]{1,0:T(8,128)(2,1)S(1)}, u32[]{:S(2)}, u32[]{:S(2)}) collective-permute-start(bf16[328,128]{1,0:T(8,128)(2,1)S(1)} %get-tuple-element.94.g0), channel_id=1, source_target_pairs={{0,1},{1,0},{2,3},{3,2},{4,5},{5,4},{6,7},{7,6},{8,9},{9,8},{10,11... | collective-permute-start | bytes 251912 | tf_op jit(solution)/shard_map/ppermute | solution.py:529
  173.1 7.6 %collective-permute-start.15 = (bf16[328,128]{1,0:T(8,128)(2,1)S(1)}, bf16[328,128]{1,0:T(8,128)(2,1)S(1)}, u32[]{:S(2)}, u32[]{:S(2)}) collective-permute-start(bf16[328,128]{1,0:T(8,128)(2,1)S(1)} %collective-permute-done.14.g1), channel_id=1, source_target_pairs={{0,1},{1,0},{2,3},{3,2},{4,5},{5,4},{6,7},{7,6},{8,9},{9,8},{10,11... | collective-permute-start | bytes 251912 | tf_op jit(solution)/shard_map/ppermute | solution.py:529
  173.9 7.1 %collective-permute-start.17 = (bf16[328,128]{1,0:T(8,128)(2,1)S(1)}, bf16[328,128]{1,0:T(8,128)(2,1)S(1)}, u32[]{:S(2)}, u32[]{:S(2)}) collective-permute-start(bf16[328,128]{1,0:T(8,128)(2,1)S(1)} %collective-permute-done.16.g2), channel_id=1, source_target_pairs={{0,1},{1,0},{2,3},{3,2},{4,5},{5,4},{6,7},{7,6},{8,9},{9,8},{10,11... | collective-permute-start | bytes 251912 | tf_op jit(solution)/shard_map/ppermute | solution.py:529
  180.1 1.3 collective-permute-start.19
  (10 other events, 13.2 us)
